TPU v7x, 512 devices: a whole 4x4x16 slice. The times are simulated.
512 devices in a mesh: child: 16 (over x, z_lo), shard: 32 (over y, z_hi, core).
Axes of the slice: x: 4, y: 4, z: 16 (z_hi: 4, z_lo: 4; z = z_hi * 4 + z_lo), core: 2. Of those that a mesh axis runs over, the one named last changes fastest.
Arguments:
- child_tensors: bfloat16 [16, 256, 256, 256], P('child', 'shard'), may hold values from -6 to 6
- leg_ops: bfloat16 [8, 256, 256], replicated, may hold values from -0.375 to 0.375
- term_ops: int32 [16, 4, 2], P('child'), may hold values from 0 to 7
- term_coef: float32 [16, 4], P('child'), may hold values from 0.5 to 1.5
- parent: bfloat16 [16, 256, 256], P('child', 'shard'), may hold values from -0.375 to 0.375
- top_env: float32 [256, 256], replicated, may hold values from -6 to 6
Outputs:
- applied: bfloat16 [16, 256, 256, 256], P('child', None, 'shard')
Inputs may be any that keep to these rules, and one draw needn't show every extreme that they name: `term_ops`: each entry names one of the 8 leg operators.
All inputs are finite; a program needn't handle non-finite values.
Results may differ from a plain program's by a relative error of at most 0.0091.
Values may be sent and summed in bfloat16 or wider, within the bound.
No kernel may reach another device: no remote copies, remote signals or barrier semaphores. Data moves between devices by JAX's collectives and lax.ppermute only.
A program may use at most 64 MiB of HBM per device.

v0:
```python
import math

import jax
import jax.numpy as jnp
from jax import lax
from jax.sharding import PartitionSpec as P


def from_everyone(shard, axis):
    length = lax.axis_size(axis)
    return lax.all_to_all(
        jnp.broadcast_to(shard[None], (length, *shard.shape)), axis, 0, 0, tiled=True
    )


def joined_along(parts, dim):
    lengths = list(parts.shape[1:])
    lengths[dim] *= parts.shape[0]
    return jnp.moveaxis(parts, 0, dim).reshape(lengths)


def gather_directly(shard, axis, dim):
    parts = from_everyone(shard, axis)
    return joined_along(parts, dim)


def filled_up(lines, length):
    spare = -lines.shape[0] % length
    if not spare:
        return lines
    return jnp.concatenate([lines, jnp.zeros((spare, *lines.shape[1:]), lines.dtype)])


def in_blocks(shard, dim, length):
    lengths = shard.shape
    parts = shard.reshape(*lengths[:dim], length, lengths[dim] // length, *lengths[dim + 1 :])
    return jnp.moveaxis(parts, dim, 0)


def sum_at_owner(shard, axis, dim):
    parts = in_blocks(shard, dim, lax.axis_size(axis))
    arrived = lax.all_to_all(parts, axis, split_axis=0, concat_axis=0, tiled=True)
    return arrived.astype(jnp.float32).sum(axis=0)


def total_of(shard, axes):
    lines = shard.reshape(-1, shard.shape[-1])
    padded = filled_up(lines, lax.axis_size(axes))
    whole = gather_directly(sum_at_owner(padded, axes, 0).astype(jnp.bfloat16), axes, 0)
    return lax.slice_in_dim(whole, 0, len(lines)).reshape(shard.shape).astype(jnp.float32)


def sent_and_summed(shard, axis, dim):
    length = lax.axis_size(axis)
    parts = lax.all_to_all(in_blocks(shard, dim, length), axis, 0, 0, tiled=True)
    return jnp.sum(parts, axis=0)


def sum_by_parts(shard, axes):
    lines = shard.reshape(-1, shard.shape[-1])
    own = sent_and_summed(filled_up(lines, lax.axis_size(axes)), axes, 0)
    whole = gather_directly(own, axes, 0)
    return whole[: len(lines)].reshape(shard.shape)


def shards(child_tensors, leg_ops, term_ops, term_coef, parent, top_env):
    high = lax.Precision.HIGHEST
    tensor = child_tensors[0]
    bond = tensor.shape[1]
    picks = term_ops[0]
    weights = term_coef[0]
    number = weights.shape[0]
    onehot = (picks[:, :, None] == jnp.arange(leg_ops.shape[0])[None, None, :]).astype(jnp.bfloat16)
    chosen = jnp.einsum(
        "tjn,nab->tjab", onehot, leg_ops, preferred_element_type=jnp.float32
    ).astype(jnp.bfloat16)
    left_ops = chosen[:, 0]
    right_ops = chosen[:, 1]
    parent_block = parent[0]
    parent_full = gather_directly(parent_block, "shard", 0).astype(jnp.float32)
    regrouped = lax.all_to_all(tensor, "shard", split_axis=1, concat_axis=0, tiled=True)
    upward = lax.all_to_all(tensor, "shard", split_axis=2, concat_axis=0, tiled=True)
    summed = jnp.zeros((bond, bond, upward.shape[2]), jnp.float32)
    for term in range(number):
        image = jnp.einsum(
            "lru,rs->lsu", upward, right_ops[term], preferred_element_type=jnp.float32
        ).astype(jnp.bfloat16)
        summed = summed + weights[term] * jnp.einsum(
            "lk,lsu->ksu", left_ops[term], image, preferred_element_type=jnp.float32
        )
    local = lax.all_to_all(
        summed.astype(jnp.bfloat16), "shard", split_axis=1, concat_axis=2, tiled=True
    ).astype(summed.dtype)
    rounded = local.astype(jnp.bfloat16)
    env_part = (
        jnp.einsum("lsu,lsv->uv", regrouped, rounded, preferred_element_type=jnp.float32) / bond
    )
    env = total_of(env_part.astype(jnp.bfloat16), "shard")
    lifted = jnp.dot(parent_full.T, jnp.dot(env, parent_full, precision=high), precision=high)
    total = sum_by_parts(lifted, "child")
    coupling = total - lifted + top_env
    factor = 1.0 / math.sqrt(bond * lax.axis_size("child"))
    hole = (
        jnp.dot(jnp.dot(parent_full, coupling, precision=high), parent_full.T, precision=high)
        * factor
    ).astype(jnp.bfloat16)
    result = local + jnp.einsum("lsu,uv->lsv", regrouped, hole, preferred_element_type=jnp.float32)
    return result.astype(jnp.bfloat16)[None]


def solution(mesh):
    in_specs = (
        P("child", "shard", None, None),
        P(),
        P("child", None, None),
        P("child", None),
        P("child", "shard", None),
        P(),
    )
    out_specs = P("child", None, "shard", None)
    return jax.shard_map(shards, mesh=mesh, in_specs=in_specs, out_specs=out_specs, check_vma=False)
```

profile of v0, /device:TPU:1, one launch (start us, length us, event | category | flops | bytes accessed | tf_op | source)
XLA Modules:
  0.0 294.6 jit_solution(2771705331370317324)
XLA Ops:
  0.0 2.7 copy.60
  2.7 19.4 %all-to-all-start = ((bf16[8,256,256]{1,0,2:T(8,128)(2,1)}), bf16[8,256,256]{1,0,2:T(8,128)(2,1)S(1)}, u32[]{:S(2)}, u32[]{:S(2)}) async-start(bf16[8,256,256]{1,0,2:T(8,128)(2,1)} %bitcast.9), calls=%async_computation | async-start | bytes 2097152 | tf_op jit(solution)/shard_map/all_to_all | solution.py:82
  22.1 0.0 copy-done
  22.1 0.0 copy-start.1
  22.1 0.0 copy-start.6
  22.1 1.6 copy.81
  23.7 49.5 %all-to-all-done = bf16[8,256,256]{1,0,2:T(8,128)(2,1)S(1)} async-done(((bf16[8,256,256]{1,0,2:T(8,128)(2,1)}), bf16[8,256,256]{1,0,2:T(8,128)(2,1)S(1)}, u32[]{:S(2)}, u32[]{:S(2)}) %all-to-all-start) | async-done | bytes 1048608 | tf_op jit(solution)/shard_map/all_to_all | solution.py:82
  73.1 9.1 %all-to-all-start.2 = ((bf16[8,256,256]{2,0,1:T(8,128)(2,1)}), bf16[8,256,256]{2,0,1:T(8,128)(2,1)}, u32[]{:S(2)}, u32[]{:S(2)}) async-start(bf16[8,256,256]{2,0,1:T(8,128)(2,1)} %copy.81), calls=%async_computation.2 | async-start | bytes 2097152 | tf_op jit(solution)/shard_map/all_to_all | solution.py:81
  82.2 0.9 convolution_convert_fusion
  83.1 1.5 fusion.52
  84.7 0.0 copy-start.4
  84.7 0.1 copy.104
  84.8 0.8 copy.105
  85.6 0.8 copy.107
  86.4 0.8 copy.108
  87.2 0.8 copy.109
  88.0 0.8 copy.110
  88.8 0.1 copy.111
  88.9 0.1 copy.112
  89.1 0.7 fusion.53
  89.8 0.3 copy.62
  90.1 1.7 fusion.2
  91.7 3.1 %fusion.4 = f32[256,256,8]{1,0,2:T(8,128)} fusion(bf16[256,256,8]{1,2,0:T(8,128)(2,1)S(1)} %bitcast.138, bf16[1,1,256,256]{2,3,1,0:T(8,128)(2,1)} %copy.108, bf16[1,1,256,256]{2,3,1,0:T(8,128)(2,1)} %copy.107), kind=kOutput, calls=%fused_computation.11 | convolution fusion | flops 537395200 | bytes 3407872 | tf_op jit(solution)/shard_map/lk,lsu->ksu/dot_general | solution.py:88
  94.8 3.0 %fusion.6 = f32[256,256,8]{1,0,2:T(8,128)} fusion(bf16[256,256,8]{1,2,0:T(8,128)(2,1)S(1)} %bitcast.139, bf16[1,1,256,256]{2,3,1,0:T(8,128)(2,1)} %copy.110, bf16[1,1,256,256]{2,3,1,0:T(8,128)(2,1)S(1)} %copy-done.2), kind=kOutput, calls=%fused_computation.13 | convolution fusion | flops 537395200 | bytes 3407872 | tf_op jit(solution)/shard_map/lk,lsu->ksu/dot_general | solution.py:88
  97.8 6.7 %add_convert_fusion = bf16[256,256,8]{1,0,2:T(8,128)(2,1)} fusion(f32[256,256,8]{1,0,2:T(8,128)} %fusion.6, f32[256,256,8]{1,0,2:T(8,128)} %fusion.4, f32[256,256,8]{1,0,2:T(8,128)S(1)} %fusion.2, f32[]{:T(128)} %bitcast.27, f32[]{:T(128)} %bitcast.21, f32[]{:T(128)} %bitcast.15, f32[]{:T(128)} %bitcast, bf16[256,256,8]{1,2,0:T(8,128)(2,1)S(1)} %bitcast.140, ...), kind=kOutput, calls=%fused_computation.2 | convolution fusion | flops 541589504 | bytes 8650768 | tf_op jit(solution)/shard_map/lk,lsu->ksu/dot_general | solution.py:88
  104.6 2.6 copy.79
  107.2 8.0 %all-to-all-done.2 = bf16[8,256,256]{2,0,1:T(8,128)(2,1)} async-done(((bf16[8,256,256]{2,0,1:T(8,128)(2,1)}), bf16[8,256,256]{2,0,1:T(8,128)(2,1)}, u32[]{:S(2)}, u32[]{:S(2)}) %all-to-all-start.2) | async-done | bytes 1048608 | tf_op jit(solution)/shard_map/all_to_all | solution.py:81
  115.1 24.5 %all-to-all-start.1 = ((bf16[256,256,8]{0,2,1:T(8,128)(2,1)}), bf16[256,256,8]{0,2,1:T(8,128)(2,1)S(1)}, u32[]{:S(2)}, u32[]{:S(2)}) async-start(bf16[256,256,8]{0,2,1:T(8,128)(2,1)} %copy.79), calls=%async_computation.1 | async-start | bytes 2097152 | tf_op jit(solution)/shard_map/all_to_all | solution.py:91
  139.6 1.5 copy.83
  141.1 0.0 copy-start.5
  141.2 28.6 %all-to-all-done.1 = bf16[256,256,8]{0,2,1:T(8,128)(2,1)S(1)} async-done(((bf16[256,256,8]{0,2,1:T(8,128)(2,1)}), bf16[256,256,8]{0,2,1:T(8,128)(2,1)S(1)}, u32[]{:S(2)}, u32[]{:S(2)}) %all-to-all-start.1) | async-done | bytes 1048608 | tf_op jit(solution)/shard_map/all_to_all | solution.py:91
  169.8 0.6 fusion.13
  170.4 0.0 copy-start.3
  170.4 45.9 %all_to_all.79 = bf16[32,8,256]{2,1,0:T(8,128)(2,1)S(1)} all-to-all(bf16[32,8,256]{2,1,0:T(8,128)(2,1)S(1)} %fusion.13), channel_id=1, replica_groups=mesh['child'=16,'shard'=32] {'shard'}, dimensions={0} | all-to-all | bytes 262144 | tf_op jit(solution)/shard_map/all_to_all | solution.py:42
  216.3 0.0 copy-done.5
  216.3 0.7 broadcast_in_dim.12
  217.0 3.7 %all-to-all-start.5 = ((bf16[32,8,256]{2,1,0:T(8,128)(2,1)}), bf16[32,8,256]{2,1,0:T(8,128)(2,1)S(1)}, u32[]{:S(2)}, u32[]{:S(2)}) async-start(bf16[32,8,256]{2,1,0:T(8,128)(2,1)} %broadcast_in_dim.12), calls=%async_computation.5 | async-start | bytes 262144 | tf_op jit(solution)/shard_map/all_to_all | solution.py:11
  220.8 17.4 %all-to-all-done.5 = bf16[32,8,256]{2,1,0:T(8,128)(2,1)S(1)} async-done(((bf16[32,8,256]{2,1,0:T(8,128)(2,1)}), bf16[32,8,256]{2,1,0:T(8,128)(2,1)S(1)}, u32[]{:S(2)}, u32[]{:S(2)}) %all-to-all-start.5) | async-done | bytes 131104 | tf_op jit(solution)/shard_map/all_to_all | solution.py:11
  238.2 20.8 %all_to_all.80 = bf16[32,8,256]{2,1,0:T(8,128)(2,1)S(1)} all-to-all(bf16[32,8,256]{2,1,0:T(8,128)(2,1)S(1)} %broadcast_in_dim.10), channel_id=1, replica_groups=mesh['child'=16,'shard'=32] {'shard'}, dimensions={0} | all-to-all | bytes 262144 | tf_op jit(solution)/shard_map/all_to_all | solution.py:11
  259.1 0.2 fusion.46
  259.3 0.3 fusion.44
  259.6 18.6 %all_to_all.81 = f32[16,16,256]{2,1,0:T(8,128)S(1)} all-to-all(f32[16,16,256]{2,1,0:T(8,128)S(1)} %bitcast.147), channel_id=1, replica_groups=mesh['child'=16,'shard'=32] {'child'}, dimensions={0} | all-to-all | bytes 524288 | tf_op jit(solution)/shard_map/all_to_all | solution.py:55
  278.2 13.2 %all_to_all.82 = f32[16,16,256]{2,1,0:T(8,128)S(1)} all-to-all(f32[16,16,256]{2,1,0:T(8,128)S(1)} %broadcast_in_dim.26), channel_id=1, replica_groups=mesh['child'=16,'shard'=32] {'child'}, dimensions={0} | all-to-all | bytes 524288 | tf_op jit(solution)/shard_map/all_to_all | solution.py:11
  291.4 0.1 fusion.28
  291.5 0.4 fusion.42
  291.9 0.4 fusion.12
  292.3 0.5 fusion.8
  292.8 1.8 copy.88
  (11 shorter events, 0.1 us)
Async XLA Ops:
  0.0 22.1 %copy-start = (bf16[1,8,256,256]{3,2,1,0:T(8,128)(2,1)S(1)}, bf16[1,8,256,256]{3,2,1,0:T(8,128)(2,1)}, u32[]{:S(2)}) copy-start(bf16[1,8,256,256]{3,2,1,0:T(8,128)(2,1)} %param.6) | copy-start | bytes 3145732
  2.7 70.4 %all-to-all-start = ((bf16[8,256,256]{1,0,2:T(8,128)(2,1)}), bf16[8,256,256]{1,0,2:T(8,128)(2,1)S(1)}, u32[]{:S(2)}, u32[]{:S(2)}) async-start(bf16[8,256,256]{1,0,2:T(8,128)(2,1)} %bitcast.9), calls=%async_computation | async-start | bytes 2097152 | tf_op jit(solution)/shard_map/all_to_all | solution.py:82
  22.1 60.1 %copy-start.1 = (bf16[8,256,256]{2,1,0:T(8,128)(2,1)S(1)}, bf16[8,256,256]{2,1,0:T(8,128)(2,1)}, u32[]{:S(2)}) copy-start(bf16[8,256,256]{2,1,0:T(8,128)(2,1)} %param.7) | copy-start | bytes 3145732
  22.1 60.1 %copy-start.6 = (s32[1,4,2]{1,2,0:T(2,128)S(1)}, s32[1,4,2]{1,2,0:T(2,128)}, u32[]{:S(2)}) copy-start(s32[1,4,2]{1,2,0:T(2,128)} %param.8) | copy-start | bytes 100
  73.1 42.0 %all-to-all-start.2 = ((bf16[8,256,256]{2,0,1:T(8,128)(2,1)}), bf16[8,256,256]{2,0,1:T(8,128)(2,1)}, u32[]{:S(2)}, u32[]{:S(2)}) async-start(bf16[8,256,256]{2,0,1:T(8,128)(2,1)} %copy.81), calls=%async_computation.2 | async-start | bytes 2097152 | tf_op jit(solution)/shard_map/all_to_all | solution.py:81
  84.7 4.4 %copy-start.4 = (f32[1,4]{1,0:T(1,128)S(1)}, f32[1,4]{1,0:T(1,128)}, u32[]{:S(2)}) copy-start(f32[1,4]{1,0:T(1,128)} %param.9) | copy-start | bytes 52
  91.7 3.1 %copy-start.2 = (bf16[1,1,256,256]{2,3,1,0:T(8,128)(2,1)S(1)}, bf16[1,1,256,256]{2,3,1,0:T(8,128)(2,1)}, u32[]{:S(2)}) copy-start(bf16[1,1,256,256]{2,3,1,0:T(8,128)(2,1)} %copy.109) | copy-start | bytes 393220
  115.1 54.6 %all-to-all-start.1 = ((bf16[256,256,8]{0,2,1:T(8,128)(2,1)}), bf16[256,256,8]{0,2,1:T(8,128)(2,1)S(1)}, u32[]{:S(2)}, u32[]{:S(2)}) async-start(bf16[256,256,8]{0,2,1:T(8,128)(2,1)} %copy.79), calls=%async_computation.1 | async-start | bytes 2097152 | tf_op jit(solution)/shard_map/all_to_all | solution.py:91
  141.1 75.2 %copy-start.5 = (bf16[1,8,256]{2,1,0:T(8,128)(2,1)S(1)}, bf16[1,8,256]{2,1,0:T(8,128)(2,1)}, u32[]{:S(2)}) copy-start(bf16[1,8,256]{2,1,0:T(8,128)(2,1)} %param.10) | copy-start | bytes 12292
  170.4 121.0 %copy-start.3 = (f32[256,256]{1,0:T(8,128)S(1)}, f32[256,256]{1,0:T(8,128)}, u32[]{:S(2)}) copy-start(f32[256,256]{1,0:T(8,128)} %param.11) | copy-start | bytes 786436
  217.0 21.2 %all-to-all-start.5 = ((bf16[32,8,256]{2,1,0:T(8,128)(2,1)}), bf16[32,8,256]{2,1,0:T(8,128)(2,1)S(1)}, u32[]{:S(2)}, u32[]{:S(2)}) async-start(bf16[32,8,256]{2,1,0:T(8,128)(2,1)} %broadcast_in_dim.12), calls=%async_computation.5 | async-start | bytes 262144 | tf_op jit(solution)/shard_map/all_to_all | solution.py:11
where the time goes:
time: 296 us; the launch traced here: 295 us
  waiting for transfers between devices  103 us (35%)
  blocking collectives  98.5 us (33%)
  starting transfers between devices  56.6 us (19%)
  local copies, waits for them, and re-layouts  17.8 us (6%)
  matrix products  17.8 us (6%)
    all_to_all x1, waiting for transfers between devices, shards(): lax.all_to_all(tensor, 'shard', split_axis=2, concat_axis=0, tiled=True)  49.5 us
    all_to_all x1, blocking collectives, sum_at_owner(): lax.all_to_all(parts, axis, split_axis=0, concat_axis=0, tiled=True)  45.9 us
    all_to_all x2, blocking collectives, from_everyone(): lax.all_to_all(jnp.broadcast_to(shard[None], (length, *shard.shape)), axi...  34 us
    all_to_all x1, waiting for transfers between devices, shards(): lax.all_to_all(summed.astype(jnp.bfloat16), 'shard', split_axis=1, concat...  28.6 us
    all_to_all x1, starting transfers between devices, shards(): lax.all_to_all(summed.astype(jnp.bfloat16), 'shard', split_axis=1, concat...  24.5 us
    all_to_all x1, starting transfers between devices, shards(): lax.all_to_all(tensor, 'shard', split_axis=2, concat_axis=0, tiled=True)  19.4 us
    all_to_all x1, blocking collectives, sent_and_summed(): lax.all_to_all(in_blocks(shard, dim, length), axis, 0, 0, tiled=True)  18.6 us
    all_to_all x1, waiting for transfers between devices, from_everyone(): lax.all_to_all(jnp.broadcast_to(shard[None], (length, *shard.shape)), axi...  17.4 us
  transfers between devices with their start and end apart: 4, of which 4 were waited for; matrix products, arithmetic and copies ran while one was open for 10% of the time, Pallas kernels for 0%

commit v1 on v0

v1 whole, which is shorter than its diff:
```python
import math

import jax
import jax.numpy as jnp
from jax import lax
from jax.experimental import pallas as pl
from jax.experimental.pallas import tpu as pltpu
from jax.sharding import Mesh, PartitionSpec as P


X, ZL, Y, ZH, C = 4, 4, 4, 4, 2
PLANE = ("x", "y", "c")
LINE = ("zl", "zh")
HIGH = lax.Precision.HIGHEST
F32 = jnp.float32
BF16 = jnp.bfloat16


def exchange(parts, axes):
    return lax.all_to_all(parts, axes, 0, 0, tiled=True)


def shifted(piece, shift):
    return lax.ppermute(piece, "zh", [(i, (i + shift) % ZH) for i in range(ZH)])


def tied(*values):
    return lax.optimization_barrier(values)


def local_kernel(picks, coefs, tensor, bank, bank_t, out):
    def column(u, carry):
        block = tensor[u]
        total = None
        for term in range(picks.shape[0]):
            right = bank[picks[term, 1]]
            left = bank_t[picks[term, 0]]
            image = jnp.dot(block, right, preferred_element_type=F32).astype(BF16)
            part = coefs[term] * jnp.dot(left, image, preferred_element_type=F32)
            total = part if total is None else total + part
        out[u] = total.astype(out.dtype)
        return carry

    lax.fori_loop(0, tensor.shape[0], column, 0)


def local_columns(tensor, bank, bank_t, picks, coefs):
    blk, bond, _ = tensor.shape
    flops = 4 * blk * bond**3 * picks.shape[0]
    return pl.pallas_call(
        local_kernel,
        out_shape=jax.ShapeDtypeStruct((blk, bond, bond), BF16),
        in_specs=[pl.BlockSpec(memory_space=pltpu.SMEM)] * 2
        + [pl.BlockSpec(memory_space=pltpu.VMEM)] * 3,
        out_specs=pl.BlockSpec(memory_space=pltpu.VMEM),
        cost_estimate=pl.CostEstimate(
            flops=flops, bytes_accessed=8 * blk * bond * bond, transcendentals=0
        ),
        name="local_columns",
    )(picks, coefs, tensor, bank, bank_t)


def result_kernel(right, hole, arrived, out):
    lines = 256

    def chunk(i, carry):
        at = pl.ds(pl.multiple_of(i * lines, lines), lines)
        moved = jnp.dot(right[at, :], hole[...], preferred_element_type=F32)
        out[at, :] = (arrived[at, :].astype(F32) + moved).astype(out.dtype)
        return carry

    lax.fori_loop(0, right.shape[0] // lines, chunk, 0)


def result_rows(right, hole, arrived):
    rows, bond = right.shape
    return pl.pallas_call(
        result_kernel,
        out_shape=jax.ShapeDtypeStruct((rows, bond), BF16),
        in_specs=[pl.BlockSpec(memory_space=pltpu.VMEM)] * 3,
        out_specs=pl.BlockSpec(memory_space=pltpu.VMEM),
        cost_estimate=pl.CostEstimate(
            flops=2 * rows * bond * bond, bytes_accessed=6 * rows * bond, transcendentals=0
        ),
        name="result_rows",
    )(right, hole, arrived)


def body(child_tensors, leg_ops, term_ops, term_coef, parent, top_env):
    x, zl, zh = lax.axis_index("x"), lax.axis_index("zl"), lax.axis_index("zh")
    plane = (x * Y + lax.axis_index("y")) * C + lax.axis_index("c")
    tensor = child_tensors[0]
    blk, bond, _ = tensor.shape
    rows = parent[0]
    terms = term_coef.shape[1]

    turned = tensor.transpose(2, 0, 1).reshape(X * Y * C, blk, blk, bond)
    own_rows = jnp.broadcast_to(rows[None, None], (X * Y * C, 1, blk, bond))
    met = exchange(jnp.concatenate([turned, own_rows], axis=1), PLANE)

    by_leg = tensor.reshape(blk, Y, ZH, C, blk, bond)

    def for_right(shift):
        piece = lax.dynamic_index_in_dim(by_leg, (zh + shift) % ZH, 2, keepdims=False)
        return piece.transpose(1, 2, 0, 3, 4).reshape(Y * C, blk, blk, bond)

    near_1, near_3 = shifted(for_right(1), 1), shifted(for_right(3), 3)
    met, near_1, near_3 = tied(met, near_1, near_3)
    met = met.reshape(X, Y * C, blk + 1, blk, bond)

    def for_plane(shift):
        return lax.dynamic_index_in_dim(met, (zh + shift) % ZH, 0, keepdims=False)

    home = jnp.zeros((Y, ZH, C, blk + 1, blk, bond), BF16)
    moved = [for_plane(0)] + [shifted(for_plane(s), s) for s in (1, 3, 2)]
    for s, piece in zip((0, 1, 3, 2), moved):
        piece = piece.reshape(Y, 1, C, blk + 1, blk, bond)
        home = lax.dynamic_update_slice_in_dim(home, piece, (zh - s) % ZH, 1)
    home = home.reshape(Y * ZH * C, blk + 1, blk, bond)
    home_t = home[:, :blk]
    home_p = home[:, blk].reshape(bond, bond).astype(F32)

    said = jnp.concatenate([term_ops[0].astype(F32), term_coef[0][:, None]], axis=1)
    said = jnp.pad(said, ((0, 8 - terms), (0, 125)))
    said, _ = tied(said, met)
    heard = exchange(jnp.broadcast_to(said[None], (X, 8, 128)), ("x",))
    mine = lax.dynamic_index_in_dim(heard, zh, 0, keepdims=False)
    picks = mine[:terms, :2].astype(jnp.int32)
    coefs = mine[:terms, 2]

    near, _ = tied(jnp.stack([for_right(0), near_1, near_3], axis=1), met)
    near = exchange(near, ("y", "c"))
    far, _ = tied(for_right(2), near)
    far = exchange(far, ("y", "c"))

    own_p = lax.dynamic_index_in_dim(met[:, :, blk], x, 0, keepdims=False)
    own_p, _ = tied(own_p, near)
    block_p = jnp.zeros((Y, ZH, C, blk, bond), BF16)
    for s in (0, 1, 3, 2):
        piece = (shifted(own_p, s) if s else own_p).reshape(Y, 1, C, blk, bond)
        block_p = lax.dynamic_update_slice_in_dim(block_p, piece, (zh - s) % ZH, 1)
    block_p = block_p.reshape(bond, bond).astype(F32)

    columns = home_t.transpose(1, 0, 2, 3).reshape(blk, bond, bond)
    columns, near, far = tied(columns, near, far)
    far = shifted(far, 2)
    local = local_columns(columns, leg_ops, leg_ops.transpose(0, 2, 1), picks, coefs)

    leaving = local.reshape(blk, bond, Y, ZH, C, blk).transpose(3, 2, 4, 0, 5, 1)

    def for_away(shift):
        return lax.dynamic_index_in_dim(leaving, (zh + shift) % ZH, 0, keepdims=False)

    away = jnp.zeros((X, Y, C, blk, blk, bond), BF16)
    for s in (0, 1, 3, 2):
        piece = shifted(for_away(s), s) if s else for_away(s)
        away = lax.dynamic_update_slice_in_dim(away, piece[None], (zh - s) % ZH, 0)

    local_rows = local.reshape(blk, bond // blk, blk, bond).transpose(1, 0, 2, 3)
    both = exchange(jnp.concatenate([home_t, local_rows], axis=1), PLANE)
    bra = both[:, :blk].reshape(bond, blk, bond)
    ket = both[:, blk:].reshape(bond, blk, bond)
    env = jnp.einsum("ulr,vlr->uv", bra, ket, preferred_element_type=F32) / bond
    lifted = jnp.dot(home_p.T, jnp.dot(env, home_p, precision=HIGH), precision=HIGH)
    lifted = exchange(lifted.astype(BF16).reshape(X * Y * C, blk, bond), PLANE)
    lifted = lifted.astype(F32).sum(axis=0)
    everyone = exchange(jnp.broadcast_to(lifted[None], (ZL * ZH, blk, bond)), LINE)
    total = everyone.sum(axis=0)
    mates = lax.dynamic_index_in_dim(
        everyone.reshape(ZL, ZH, blk, bond), zl, 0, keepdims=False
    )
    top_rows = lax.dynamic_slice_in_dim(top_env, plane * blk, blk, 0)
    coupling = ((total + top_rows)[None] - mates).astype(BF16)
    coupling = jnp.broadcast_to(coupling[:, None], (X, Y * C, blk, bond))
    coupling = exchange(coupling.reshape(X * Y * C, blk, bond), PLANE)
    coupling = coupling.reshape(bond, bond).astype(F32)
    factor = 1.0 / math.sqrt(bond * X * ZL)
    hole = jnp.dot(jnp.dot(block_p, coupling, precision=HIGH), block_p.T, precision=HIGH)
    hole = (hole * factor).astype(BF16)

    right = jnp.zeros((Y, ZH, C, blk, blk, bond), BF16)
    for s, piece in ((0, near[:, 0]), (1, near[:, 1]), (3, near[:, 2]), (2, far)):
        piece = piece.reshape(Y, 1, C, blk, blk, bond)
        right = lax.dynamic_update_slice_in_dim(right, piece, (zh - s) % ZH, 1)
    right = right.reshape(bond * blk, bond)
    away, _ = tied(away.reshape(X * Y * C, blk, blk, bond), coupling)
    arrived = exchange(away, PLANE).reshape(bond, blk, bond)
    arrived = arrived.transpose(2, 1, 0).reshape(bond * blk, bond)
    return result_rows(right, hole, arrived).reshape(1, bond, blk, bond)


def solution(mesh):
    fine = Mesh(mesh.devices.reshape(X, ZL, Y, ZH, C), ("x", "zl", "y", "zh", "c"))
    child, shard = ("x", "zl"), ("y", "zh", "c")
    in_specs = (
        P(child, shard, None, None),
        P(),
        P(child, None, None),
        P(child, None),
        P(child, shard, None),
        P(),
    )
    out_specs = P(child, None, shard, None)
    return jax.shard_map(
        body, mesh=fine, in_specs=in_specs, out_specs=out_specs, check_vma=False
    )
```

time: 296 us -> 276 us (0.932)
  the two profiles are of different devices: /device:TPU:1 before, /device:TPU:99 now
where the time goes in v1:
time: 276 us; the launch traced here: 274 us
  starting transfers between devices  153 us (55%)
  waiting for transfers between devices  73 us (26%)
  local copies, waits for them, and re-layouts  26.3 us (10%)
  Pallas kernels  11.9 us (4%)
  other arithmetic  5.97 us (2%)
  matrix products  3.11 us (1%)
    ppermute x12, starting transfers between devices, shifted(): return lax.ppermute(piece, 'zh', [(i, (i + shift) % ZH) for i in range(ZH)])  87.1 us
    all_to_all x9, starting transfers between devices, exchange(): return lax.all_to_all(parts, axes, 0, 0, tiled=True)  66.4 us
    ppermute x12, waiting for transfers between devices, shifted(): return lax.ppermute(piece, 'zh', [(i, (i + shift) % ZH) for i in range(ZH)])  45.6 us
    all_to_all x9, waiting for transfers between devices, exchange(): return lax.all_to_all(parts, axes, 0, 0, tiled=True)  27.4 us
    pallas_call x1, Pallas kernels, local_columns(): pl.pallas_call(local_kernel, out_shape=jax.ShapeDtypeStruct((blk, bond, b...  7.77 us
    dynamic_update_slice x4, local copies, waits for them, and re-layouts, body(): away = lax.dynamic_update_slice_in_dim(away, piece[None], (zh - s) % ZH, 0)  5.73 us
  transfers between devices with their start and end apart: 21, of which 10 were waited for; matrix products, arithmetic and copies ran while one was open for 10% of the time, Pallas kernels for 0%

profile of v1, /device:TPU:99, one launch (start us, length us, event | category | flops | bytes accessed | tf_op | source)
XLA Modules:
  0.0 274.4 jit_solution(15835691969327865991)
XLA Ops:
  0.0 1.9 copy.89
  1.9 1.2 pad_maximum_fusion.1
  3.1 8.0 %all-to-all-start = ((bf16[32,9,8,256]{3,2,1,0:T(8,128)(2,1)}), bf16[32,9,8,256]{3,2,1,0:T(8,128)(2,1)S(1)}, u32[]{:S(2)}, u32[]{:S(2)}) async-start(bf16[32,9,8,256]{3,2,1,0:T(8,128)(2,1)} %pad_maximum_fusion.1), calls=%async_computation | async-start | bytes 2359296 | tf_op jit(solution)/shard_map/all_to_all | solution.py:20
  12.0 8.8 %collective-permute-start = (bf16[8,8,8,256]{3,2,1,0:T(8,128)(2,1)S(1)}, bf16[8,8,8,256]{3,2,1,0:T(8,128)(2,1)S(1)}, u32[]{:S(2)}, u32[]{:S(2)}) collective-permute-start(bf16[8,8,8,256]{3,2,1,0:T(8,128)(2,1)S(1)} %copy.90), channel_id=1, source_target_pairs={{0,2},{2,4},{4,6},{6,0},{1,3},{3,5},{5,7},{7,1},{8,10},{10,12},{12... | collective-permute-start | bytes 786440 | tf_op jit(solution)/shard_map/ppermute | solution.py:24
  20.9 2.9 %collective-permute-start.1 = (bf16[8,8,8,256]{3,2,1,0:T(8,128)(2,1)S(1)}, bf16[8,8,8,256]{3,2,1,0:T(8,128)(2,1)}, u32[]{:S(2)}, u32[]{:S(2)}) collective-permute-start(bf16[8,8,8,256]{3,2,1,0:T(8,128)(2,1)S(1)} %copy.91), channel_id=1, source_target_pairs={{0,6},{2,0},{4,2},{6,4},{1,7},{3,1},{5,3},{7,5},{8,14},{10,8},{12,... | collective-permute-start | bytes 786440 | tf_op jit(solution)/shard_map/ppermute | solution.py:24
  23.9 1.3 copy.107
  25.2 19.8 %collective-permute-done = bf16[8,8,8,256]{3,2,1,0:T(8,128)(2,1)S(1)} collective-permute-done((bf16[8,8,8,256]{3,2,1,0:T(8,128)(2,1)S(1)}, bf16[8,8,8,256]{3,2,1,0:T(8,128)(2,1)S(1)}, u32[]{:S(2)}, u32[]{:S(2)}) %collective-permute-start) | collective-permute-done | bytes 262176 | tf_op jit(solution)/shard_map/ppermute | solution.py:24
  46.3 5.5 %collective-permute-start.2 = (bf16[8,9,8,256]{3,2,1,0:T(8,128)(2,1)}, bf16[8,9,8,256]{3,2,1,0:T(8,128)(2,1)S(1)}, u32[]{:S(2)}, u32[]{:S(2)}) collective-permute-start(bf16[8,9,8,256]{3,2,1,0:T(8,128)(2,1)} %get-tuple-element.31), channel_id=1, source_target_pairs={{0,2},{2,4},{4,6},{6,0},{1,3},{3,5},{5,7},{7,1},{8,10},{10,12},{12... | collective-permute-start | bytes 884744 | tf_op jit(solution)/shard_map/ppermute | solution.py:24
  51.8 3.7 %collective-permute-start.3 = (bf16[8,9,8,256]{3,2,1,0:T(8,128)(2,1)}, bf16[8,9,8,256]{3,2,1,0:T(8,128)(2,1)S(1)}, u32[]{:S(2)}, u32[]{:S(2)}) collective-permute-start(bf16[8,9,8,256]{3,2,1,0:T(8,128)(2,1)} %get-tuple-element.30), channel_id=1, source_target_pairs={{0,6},{2,0},{4,2},{6,4},{1,7},{3,1},{5,3},{7,5},{8,14},{10,8},{12,... | collective-permute-start | bytes 884744 | tf_op jit(solution)/shard_map/ppermute | solution.py:24
  55.5 8.8 %collective-permute-start.4 = (bf16[8,9,8,256]{3,2,1,0:T(8,128)(2,1)}, bf16[8,9,8,256]{3,2,1,0:T(8,128)(2,1)S(1)}, u32[]{:S(2)}, u32[]{:S(2)}) collective-permute-start(bf16[8,9,8,256]{3,2,1,0:T(8,128)(2,1)} %get-tuple-element.29), channel_id=1, source_target_pairs={{0,4},{2,6},{4,0},{6,2},{1,5},{3,7},{5,1},{7,3},{8,12},{10,14},{12... | collective-permute-start | bytes 884744 | tf_op jit(solution)/shard_map/ppermute | solution.py:24
  65.0 4.2 %all-to-all-start.3 = ((f32[4,8,128]{2,1,0:T(8,128)}), f32[4,8,128]{2,1,0:T(8,128)S(1)}, u32[]{:S(2)}, u32[]{:S(2)}) async-start(f32[4,8,128]{2,1,0:T(8,128)} %broadcast_in_dim.46), calls=%async_computation.3 | async-start | bytes 32768 | tf_op jit(solution)/shard_map/all_to_all | solution.py:20
  69.2 1.9 pad_maximum_fusion.2
  71.2 1.3 all-to-all-done.3
  72.6 11.5 %all-to-all-start.1 = ((bf16[8,3,8,8,256]{4,3,2,1,0:T(8,128)(2,1)}), bf16[8,3,8,8,256]{4,3,2,1,0:T(8,128)(2,1)S(1)}, u32[]{:S(2)}, u32[]{:S(2)}) async-start(bf16[8,3,8,8,256]{4,3,2,1,0:T(8,128)(2,1)} %pad_maximum_fusion.2), calls=%async_computation.1 | async-start | bytes 1572864 | tf_op jit(solution)/shard_map/all_to_all | solution.py:20
  85.4 3.0 %collective-permute-done.4 = bf16[8,9,8,256]{3,2,1,0:T(8,128)(2,1)S(1)} collective-permute-done((bf16[8,9,8,256]{3,2,1,0:T(8,128)(2,1)}, bf16[8,9,8,256]{3,2,1,0:T(8,128)(2,1)S(1)}, u32[]{:S(2)}, u32[]{:S(2)}) %collective-permute-start.4) | collective-permute-done | bytes 294944 | tf_op jit(solution)/shard_map/ppermute | solution.py:24
  88.4 7.8 %all-to-all-done.1 = bf16[8,3,8,8,256]{4,3,2,1,0:T(8,128)(2,1)S(1)} async-done(((bf16[8,3,8,8,256]{4,3,2,1,0:T(8,128)(2,1)}), bf16[8,3,8,8,256]{4,3,2,1,0:T(8,128)(2,1)S(1)}, u32[]{:S(2)}, u32[]{:S(2)}) %all-to-all-start.1) | async-done | bytes 786464 | tf_op jit(solution)/shard_map/all_to_all | solution.py:20
  96.9 4.9 %all-to-all-start.2 = ((bf16[8,8,8,256]{3,2,1,0:T(8,128)(2,1)}), bf16[8,8,8,256]{3,2,1,0:T(8,128)(2,1)}, u32[]{:S(2)}, u32[]{:S(2)}) async-start(bf16[8,8,8,256]{3,2,1,0:T(8,128)(2,1)} %copy.97), calls=%async_computation.2 | async-start | bytes 524288 | tf_op jit(solution)/shard_map/all_to_all | solution.py:20
  102.0 1.0 copy.129
  103.0 5.4 %all-to-all-done.2 = bf16[8,8,8,256]{3,2,1,0:T(8,128)(2,1)} async-done(((bf16[8,8,8,256]{3,2,1,0:T(8,128)(2,1)}), bf16[8,8,8,256]{3,2,1,0:T(8,128)(2,1)}, u32[]{:S(2)}, u32[]{:S(2)}) %all-to-all-start.2) | async-done | bytes 262176 | tf_op jit(solution)/shard_map/all_to_all | solution.py:20
  108.4 7.8 %local_columns.1 = bf16[8,256,256]{2,1,0:T(8,128)(2,1)} custom-call(s32[4,2]{1,0:T(4,128)} %slice_convert_fusion.picks, f32[4]{0:T(128)} %slice_reduce_fusion.coefs, bf16[8,256,256]{2,1,0:T(8,128)(2,1)} %bitcast.165, bf16[8,256,256]{2,1,0:T(8,128)(2,1)} %bank.1, bf16[8,256,256]{2,1,0:T(8,128)(2,1)} %bitcast.164), custom_call_target="tpu_custom_call" | custom-call | flops 2147483648 | bytes 4194304 | tf_op jit(solution)/shard_map/local_columns/pallas_call | solution.py:50
  116.2 1.3 copy_bitcast_fusion
  117.6 1.5 pad_maximum_fusion
  119.1 5.8 %all-to-all-start.4 = ((bf16[32,16,8,256]{3,2,1,0:T(8,128)(2,1)}), bf16[32,16,8,256]{3,2,1,0:T(8,128)(2,1)S(1)}, u32[]{:S(2)}, u32[]{:S(2)}) async-start(bf16[32,16,8,256]{3,2,1,0:T(8,128)(2,1)} %pad_maximum_fusion), calls=%async_computation.4 | async-start | bytes 4194304 | tf_op jit(solution)/shard_map/all_to_all | solution.py:20
  125.9 23.7 %collective-permute-start.6 = (bf16[8,8,256]{2,1,0:T(8,128)(2,1)S(1)}, bf16[8,8,256]{2,1,0:T(8,128)(2,1)S(1)}, u32[]{:S(2)}, u32[]{:S(2)}) collective-permute-start(bf16[8,8,256]{2,1,0:T(8,128)(2,1)S(1)} %dynamic-slice_bitcast_fusion.7), channel_id=1, source_target_pairs={{0,2},{2,4},{4,6},{6,0},{1,3},{3,5},{5,7},{7,1},{8,10},{10,12},{12... | collective-permute-start | bytes 98312 | tf_op jit(solution)/shard_map/ppermute | solution.py:24
  149.6 1.9 collective-permute-start.7
  151.5 7.0 %collective-permute-start.8 = (bf16[8,8,256]{2,1,0:T(8,128)(2,1)S(1)}, bf16[8,8,256]{2,1,0:T(8,128)(2,1)S(1)}, u32[]{:S(2)}, u32[]{:S(2)}) collective-permute-start(bf16[8,8,256]{2,1,0:T(8,128)(2,1)S(1)} %dynamic-slice_bitcast_fusion.7), channel_id=1, source_target_pairs={{0,4},{2,6},{4,0},{6,2},{1,5},{3,7},{5,1},{7,3},{8,12},{10,14},{12... | collective-permute-start | bytes 98312 | tf_op jit(solution)/shard_map/ppermute | solution.py:24
  158.6 2.3 copy.111
  160.9 2.2 dynamic-slice_bitcast_fusion.3
  163.1 2.2 collective-permute-start.9
  165.3 7.0 %collective-permute-start.10 = (bf16[4,2,8,8,256]{4,3,1,0,2:T(8,128)(2,1)}, bf16[4,2,8,8,256]{4,3,1,0,2:T(8,128)(2,1)}, u32[]{:S(2)}, u32[]{:S(2)}) collective-permute-start(bf16[4,2,8,8,256]{4,3,1,0,2:T(8,128)(2,1)} %get-tuple-element.34), channel_id=1, source_target_pairs={{0,6},{2,0},{4,2},{6,4},{1,7},{3,1},{5,3},{7,5},{8,14},{10,8},{12,... | collective-permute-start | bytes 786440 | tf_op jit(solution)/shard_map/ppermute | solution.py:24
  172.3 7.0 %collective-permute-start.11 = (bf16[4,2,8,8,256]{4,3,1,0,2:T(8,128)(2,1)}, bf16[4,2,8,8,256]{4,3,1,0,2:T(8,128)(2,1)}, u32[]{:S(2)}, u32[]{:S(2)}) collective-permute-start(bf16[4,2,8,8,256]{4,3,1,0,2:T(8,128)(2,1)} %get-tuple-element.33), channel_id=1, source_target_pairs={{0,4},{2,6},{4,0},{6,2},{1,5},{3,7},{5,1},{7,3},{8,12},{10,14},{12... | collective-permute-start | bytes 786440 | tf_op jit(solution)/shard_map/ppermute | solution.py:24
  181.4 8.8 %all-to-all-start.5 = ((bf16[32,8,256]{2,1,0:T(8,128)(2,1)}), bf16[32,8,256]{2,1,0:T(8,128)(2,1)S(1)}, u32[]{:S(2)}, u32[]{:S(2)}) async-start(bf16[32,8,256]{2,1,0:T(8,128)(2,1)} %fusion.2), calls=%async_computation.5 | async-start | bytes 262144 | tf_op jit(solution)/shard_map/all_to_all | solution.py:20
  190.2 1.1 broadcast.21.clone.1
  192.0 5.2 %all-to-all-done.5 = bf16[32,8,256]{2,1,0:T(8,128)(2,1)S(1)} async-done(((bf16[32,8,256]{2,1,0:T(8,128)(2,1)}), bf16[32,8,256]{2,1,0:T(8,128)(2,1)S(1)}, u32[]{:S(2)}, u32[]{:S(2)}) %all-to-all-start.5) | async-done | bytes 131104 | tf_op jit(solution)/shard_map/all_to_all | solution.py:20
  197.9 9.9 %all-to-all-start.6 = ((f32[16,8,256]{2,1,0:T(8,128)}), f32[16,8,256]{2,1,0:T(8,128)S(1)}, u32[]{:S(2)}, u32[]{:S(2)}) async-start(f32[16,8,256]{2,1,0:T(8,128)} %broadcast_in_dim.47), calls=%async_computation.6 | async-start | bytes 262144 | tf_op jit(solution)/shard_map/all_to_all | solution.py:20
  207.8 1.7 copy_dynamic-update-slice_fusion.2
  209.5 1.7 copy_dynamic-update-slice_fusion.1
  211.2 8.6 %collective-permute-done.11 = bf16[4,2,8,8,256]{4,3,1,0,2:T(8,128)(2,1)} collective-permute-done((bf16[4,2,8,8,256]{4,3,1,0,2:T(8,128)(2,1)}, bf16[4,2,8,8,256]{4,3,1,0,2:T(8,128)(2,1)}, u32[]{:S(2)}, u32[]{:S(2)}) %collective-permute-start.11) | collective-permute-done | bytes 262176 | tf_op jit(solution)/shard_map/ppermute | solution.py:24
  219.7 1.7 copy_dynamic-update-slice_fusion
  221.4 1.9 all-to-all-done.6
  223.3 7.9 %all-to-all-start.8 = ((bf16[32,8,8,256]{3,2,1,0:T(8,128)(2,1)}), bf16[32,8,8,256]{3,2,1,0:T(8,128)(2,1)S(1)}, u32[]{:S(2)}, u32[]{:S(2)}) async-start(bf16[32,8,8,256]{3,2,1,0:T(8,128)(2,1)} %bitcast.78), calls=%async_computation.8 | async-start | bytes 2097152 | tf_op jit(solution)/shard_map/all_to_all | solution.py:20
  231.2 8.6 %collective-permute-start.5 = (bf16[8,8,8,256]{3,2,1,0:T(8,128)(2,1)}, bf16[8,8,8,256]{3,2,1,0:T(8,128)(2,1)S(1)}, u32[]{:S(2)}, u32[]{:S(2)}) collective-permute-start(bf16[8,8,8,256]{3,2,1,0:T(8,128)(2,1)} %all-to-all-done.2), channel_id=1, source_target_pairs={{0,4},{2,6},{4,0},{6,2},{1,5},{3,7},{5,1},{7,3},{8,12},{10,14},{12... | collective-permute-start | bytes 786440 | tf_op jit(solution)/shard_map/ppermute | solution.py:24
  240.8 5.8 %all-to-all-done.8 = bf16[32,8,8,256]{3,2,1,0:T(8,128)(2,1)S(1)} async-done(((bf16[32,8,8,256]{3,2,1,0:T(8,128)(2,1)}), bf16[32,8,8,256]{3,2,1,0:T(8,128)(2,1)S(1)}, u32[]{:S(2)}, u32[]{:S(2)}) %all-to-all-start.8) | async-done | bytes 1048608 | tf_op jit(solution)/shard_map/all_to_all | solution.py:20
  247.3 5.4 %all-to-all-start.7 = ((bf16[32,8,256]{2,1,0:T(8,128)(2,1)}), bf16[32,8,256]{2,1,0:T(8,128)(2,1)S(1)}, u32[]{:S(2)}, u32[]{:S(2)}) async-start(bf16[32,8,256]{2,1,0:T(8,128)(2,1)} %bitcast.65), calls=%async_computation.7 | async-start | bytes 262144 | tf_op jit(solution)/shard_map/all_to_all | solution.py:20
  252.7 14.3 %collective-permute-done.5 = bf16[8,8,8,256]{3,2,1,0:T(8,128)(2,1)S(1)} collective-permute-done((bf16[8,8,8,256]{3,2,1,0:T(8,128)(2,1)}, bf16[8,8,8,256]{3,2,1,0:T(8,128)(2,1)S(1)}, u32[]{:S(2)}, u32[]{:S(2)}) %collective-permute-start.5) | collective-permute-done | bytes 262176 | tf_op jit(solution)/shard_map/ppermute | solution.py:24
  267.0 2.1 copy.116
  269.3 1.0 fusion.1.hole
  270.3 4.1 %result_rows.1 = bf16[2048,256]{1,0:T(8,128)(2,1)} custom-call(bf16[2048,256]{1,0:T(8,128)(2,1)} %bitcast.153, bf16[256,256]{1,0:T(8,128)(2,1)} %fusion.1.hole, bf16[2048,256]{1,0:T(8,128)(2,1)} %bitcast.152), custom_call_target="tpu_custom_call" | custom-call | flops 268435456 | bytes 3145728 | tf_op jit(solution)/shard_map/result_rows/pallas_call | solution.py:77
  (77 shorter events, 11.6 us)
Async XLA Ops:
  0.0 1.9 copy-start.8
  3.1 8.1 %copy-start.2 = (bf16[1,8,256,256]{3,2,1,0:T(8,128)(2,1)S(1)}, bf16[1,8,256,256]{3,2,1,0:T(8,128)(2,1)}, u32[]{:S(2)}) copy-start(bf16[1,8,256,256]{3,2,1,0:T(8,128)(2,1)} %param.6) | copy-start | bytes 3145732
  3.1 41.9 %all-to-all-start = ((bf16[32,9,8,256]{3,2,1,0:T(8,128)(2,1)}), bf16[32,9,8,256]{3,2,1,0:T(8,128)(2,1)S(1)}, u32[]{:S(2)}, u32[]{:S(2)}) async-start(bf16[32,9,8,256]{3,2,1,0:T(8,128)(2,1)} %pad_maximum_fusion.1), calls=%async_computation | async-start | bytes 2359296 | tf_op jit(solution)/shard_map/all_to_all | solution.py:20
  11.2 12.7 %copy-start.6 = (bf16[8,256,256]{2,1,0:T(8,128)(2,1)S(1)}, bf16[8,256,256]{2,1,0:T(8,128)(2,1)}, u32[]{:S(2)}) copy-start(bf16[8,256,256]{2,1,0:T(8,128)(2,1)} %bank.1) | copy-start | bytes 3145732
  12.0 32.9 %collective-permute-start = (bf16[8,8,8,256]{3,2,1,0:T(8,128)(2,1)S(1)}, bf16[8,8,8,256]{3,2,1,0:T(8,128)(2,1)S(1)}, u32[]{:S(2)}, u32[]{:S(2)}) collective-permute-start(bf16[8,8,8,256]{3,2,1,0:T(8,128)(2,1)S(1)} %copy.90), channel_id=1, source_target_pairs={{0,2},{2,4},{4,6},{6,0},{1,3},{3,5},{5,7},{7,1},{8,10},{10,12},{12... | collective-permute-start | bytes 786440 | tf_op jit(solution)/shard_map/ppermute | solution.py:24
  20.9 4.3 %copy-start.9 = (s32[1,4,2]{1,2,0:T(2,128)S(1)}, s32[1,4,2]{1,2,0:T(2,128)}, u32[]{:S(2)}) copy-start(s32[1,4,2]{1,2,0:T(2,128)} %param.8) | copy-start | bytes 100
  20.9 4.3 %copy-start.10 = (f32[1,4]{1,0:T(1,128)S(1)}, f32[1,4]{1,0:T(1,128)}, u32[]{:S(2)}) copy-start(f32[1,4]{1,0:T(1,128)} %param.9) | copy-start | bytes 52
  20.9 24.1 %collective-permute-start.1 = (bf16[8,8,8,256]{3,2,1,0:T(8,128)(2,1)S(1)}, bf16[8,8,8,256]{3,2,1,0:T(8,128)(2,1)}, u32[]{:S(2)}, u32[]{:S(2)}) collective-permute-start(bf16[8,8,8,256]{3,2,1,0:T(8,128)(2,1)S(1)} %copy.91), channel_id=1, source_target_pairs={{0,6},{2,0},{4,2},{6,4},{1,7},{3,1},{5,3},{7,5},{8,14},{10,8},{12,... | collective-permute-start | bytes 786440 | tf_op jit(solution)/shard_map/ppermute | solution.py:24
  45.0 1.3 copy-start
  45.0 24.2 %copy-start.7 = (bf16[8,4,1,2,8,256]{5,4,3,2,1,0:T(8,128)(2,1)S(1)}, bf16[8,4,1,2,8,256]{5,4,3,2,1,0:T(8,128)(2,1)}, u32[]{:S(2)}) copy-start(bf16[8,4,1,2,8,256]{5,4,3,2,1,0:T(8,128)(2,1)} %get-tuple-element.38) | copy-start | bytes 786436
  46.3 39.0 %collective-permute-start.2 = (bf16[8,9,8,256]{3,2,1,0:T(8,128)(2,1)}, bf16[8,9,8,256]{3,2,1,0:T(8,128)(2,1)S(1)}, u32[]{:S(2)}, u32[]{:S(2)}) collective-permute-start(bf16[8,9,8,256]{3,2,1,0:T(8,128)(2,1)} %get-tuple-element.31), channel_id=1, source_target_pairs={{0,2},{2,4},{4,6},{6,0},{1,3},{3,5},{5,7},{7,1},{8,10},{10,12},{12... | collective-permute-start | bytes 884744 | tf_op jit(solution)/shard_map/ppermute | solution.py:24
  51.8 33.6 %collective-permute-start.3 = (bf16[8,9,8,256]{3,2,1,0:T(8,128)(2,1)}, bf16[8,9,8,256]{3,2,1,0:T(8,128)(2,1)S(1)}, u32[]{:S(2)}, u32[]{:S(2)}) collective-permute-start(bf16[8,9,8,256]{3,2,1,0:T(8,128)(2,1)} %get-tuple-element.30), channel_id=1, source_target_pairs={{0,6},{2,0},{4,2},{6,4},{1,7},{3,1},{5,3},{7,5},{8,14},{10,8},{12,... | collective-permute-start | bytes 884744 | tf_op jit(solution)/shard_map/ppermute | solution.py:24
  55.5 32.9 %collective-permute-start.4 = (bf16[8,9,8,256]{3,2,1,0:T(8,128)(2,1)}, bf16[8,9,8,256]{3,2,1,0:T(8,128)(2,1)S(1)}, u32[]{:S(2)}, u32[]{:S(2)}) collective-permute-start(bf16[8,9,8,256]{3,2,1,0:T(8,128)(2,1)} %get-tuple-element.29), channel_id=1, source_target_pairs={{0,4},{2,6},{4,0},{6,2},{1,5},{3,7},{5,1},{7,3},{8,12},{10,14},{12... | collective-permute-start | bytes 884744 | tf_op jit(solution)/shard_map/ppermute | solution.py:24
  65.0 7.6 %all-to-all-start.3 = ((f32[4,8,128]{2,1,0:T(8,128)}), f32[4,8,128]{2,1,0:T(8,128)S(1)}, u32[]{:S(2)}, u32[]{:S(2)}) async-start(f32[4,8,128]{2,1,0:T(8,128)} %broadcast_in_dim.46), calls=%async_computation.3 | async-start | bytes 32768 | tf_op jit(solution)/shard_map/all_to_all | solution.py:20
  72.6 23.6 %all-to-all-start.1 = ((bf16[8,3,8,8,256]{4,3,2,1,0:T(8,128)(2,1)}), bf16[8,3,8,8,256]{4,3,2,1,0:T(8,128)(2,1)S(1)}, u32[]{:S(2)}, u32[]{:S(2)}) async-start(bf16[8,3,8,8,256]{4,3,2,1,0:T(8,128)(2,1)} %pad_maximum_fusion.2), calls=%async_computation.1 | async-start | bytes 1572864 | tf_op jit(solution)/shard_map/all_to_all | solution.py:20
  96.2 5.7 %copy-start.3 = (bf16[8,3,8,8,256]{4,3,2,1,0:T(8,128)(2,1)}, bf16[8,3,8,8,256]{4,3,2,1,0:T(8,128)(2,1)S(1)}, u32[]{:S(2)}) copy-start(bf16[8,3,8,8,256]{4,3,2,1,0:T(8,128)(2,1)S(1)} %all-to-all-done.1) | copy-start | bytes 2359300
  96.9 11.5 %all-to-all-start.2 = ((bf16[8,8,8,256]{3,2,1,0:T(8,128)(2,1)}), bf16[8,8,8,256]{3,2,1,0:T(8,128)(2,1)}, u32[]{:S(2)}, u32[]{:S(2)}) async-start(bf16[8,8,8,256]{3,2,1,0:T(8,128)(2,1)} %copy.97), calls=%async_computation.2 | async-start | bytes 524288 | tf_op jit(solution)/shard_map/all_to_all | solution.py:20
  119.1 60.2 %all-to-all-start.4 = ((bf16[32,16,8,256]{3,2,1,0:T(8,128)(2,1)}), bf16[32,16,8,256]{3,2,1,0:T(8,128)(2,1)S(1)}, u32[]{:S(2)}, u32[]{:S(2)}) async-start(bf16[32,16,8,256]{3,2,1,0:T(8,128)(2,1)} %pad_maximum_fusion), calls=%async_computation.4 | async-start | bytes 4194304 | tf_op jit(solution)/shard_map/all_to_all | solution.py:20
  125.9 32.7 %collective-permute-start.6 = (bf16[8,8,256]{2,1,0:T(8,128)(2,1)S(1)}, bf16[8,8,256]{2,1,0:T(8,128)(2,1)S(1)}, u32[]{:S(2)}, u32[]{:S(2)}) collective-permute-start(bf16[8,8,256]{2,1,0:T(8,128)(2,1)S(1)} %dynamic-slice_bitcast_fusion.7), channel_id=1, source_target_pairs={{0,2},{2,4},{4,6},{6,0},{1,3},{3,5},{5,7},{7,1},{8,10},{10,12},{12... | collective-permute-start | bytes 98312 | tf_op jit(solution)/shard_map/ppermute | solution.py:24
  149.6 9.0 %collective-permute-start.7 = (bf16[8,8,256]{2,1,0:T(8,128)(2,1)S(1)}, bf16[8,8,256]{2,1,0:T(8,128)(2,1)S(1)}, u32[]{:S(2)}, u32[]{:S(2)}) collective-permute-start(bf16[8,8,256]{2,1,0:T(8,128)(2,1)S(1)} %dynamic-slice_bitcast_fusion.7), channel_id=1, source_target_pairs={{0,6},{2,0},{4,2},{6,4},{1,7},{3,1},{5,3},{7,5},{8,14},{10,8},{12,... | collective-permute-start | bytes 98312 | tf_op jit(solution)/shard_map/ppermute | solution.py:24
  151.5 79.7 %collective-permute-start.8 = (bf16[8,8,256]{2,1,0:T(8,128)(2,1)S(1)}, bf16[8,8,256]{2,1,0:T(8,128)(2,1)S(1)}, u32[]{:S(2)}, u32[]{:S(2)}) collective-permute-start(bf16[8,8,256]{2,1,0:T(8,128)(2,1)S(1)} %dynamic-slice_bitcast_fusion.7), channel_id=1, source_target_pairs={{0,4},{2,6},{4,0},{6,2},{1,5},{3,7},{5,1},{7,3},{8,12},{10,14},{12... | collective-permute-start | bytes 98312 | tf_op jit(solution)/shard_map/ppermute | solution.py:24
  163.1 44.7 %collective-permute-start.9 = (bf16[4,2,8,8,256]{4,3,1,0,2:T(8,128)(2,1)}, bf16[4,2,8,8,256]{4,3,1,0,2:T(8,128)(2,1)}, u32[]{:S(2)}, u32[]{:S(2)}) collective-permute-start(bf16[4,2,8,8,256]{4,3,1,0,2:T(8,128)(2,1)} %get-tuple-element.35), channel_id=1, source_target_pairs={{0,2},{2,4},{4,6},{6,0},{1,3},{3,5},{5,7},{7,1},{8,10},{10,12},{12... | collective-permute-start | bytes 786440 | tf_op jit(solution)/shard_map/ppermute | solution.py:24
  165.3 44.2 %collective-permute-start.10 = (bf16[4,2,8,8,256]{4,3,1,0,2:T(8,128)(2,1)}, bf16[4,2,8,8,256]{4,3,1,0,2:T(8,128)(2,1)}, u32[]{:S(2)}, u32[]{:S(2)}) collective-permute-start(bf16[4,2,8,8,256]{4,3,1,0,2:T(8,128)(2,1)} %get-tuple-element.34), channel_id=1, source_target_pairs={{0,6},{2,0},{4,2},{6,4},{1,7},{3,1},{5,3},{7,5},{8,14},{10,8},{12,... | collective-permute-start | bytes 786440 | tf_op jit(solution)/shard_map/ppermute | solution.py:24
  172.3 47.5 %collective-permute-start.11 = (bf16[4,2,8,8,256]{4,3,1,0,2:T(8,128)(2,1)}, bf16[4,2,8,8,256]{4,3,1,0,2:T(8,128)(2,1)}, u32[]{:S(2)}, u32[]{:S(2)}) collective-permute-start(bf16[4,2,8,8,256]{4,3,1,0,2:T(8,128)(2,1)} %get-tuple-element.33), channel_id=1, source_target_pairs={{0,4},{2,6},{4,0},{6,2},{1,5},{3,7},{5,1},{7,3},{8,12},{10,14},{12... | collective-permute-start | bytes 786440 | tf_op jit(solution)/shard_map/ppermute | solution.py:24
  180.1 11.2 %copy-start.5 = (bf16[1,4,2,8,8,256]{5,4,2,0,1,3:T(8,128)(2,1)S(1)}, bf16[1,4,2,8,8,256]{5,4,2,0,1,3:T(8,128)(2,1)}, u32[]{:S(2)}) copy-start(bf16[1,4,2,8,8,256]{5,4,2,0,1,3:T(8,128)(2,1)} %get-tuple-element.36) | copy-start | bytes 786436
  181.4 15.8 %all-to-all-start.5 = ((bf16[32,8,256]{2,1,0:T(8,128)(2,1)}), bf16[32,8,256]{2,1,0:T(8,128)(2,1)S(1)}, u32[]{:S(2)}, u32[]{:S(2)}) async-start(bf16[32,8,256]{2,1,0:T(8,128)(2,1)} %fusion.2), calls=%async_computation.5 | async-start | bytes 262144 | tf_op jit(solution)/shard_map/all_to_all | solution.py:20
  197.9 25.4 %all-to-all-start.6 = ((f32[16,8,256]{2,1,0:T(8,128)}), f32[16,8,256]{2,1,0:T(8,128)S(1)}, u32[]{:S(2)}, u32[]{:S(2)}) async-start(f32[16,8,256]{2,1,0:T(8,128)} %broadcast_in_dim.47), calls=%async_computation.6 | async-start | bytes 262144 | tf_op jit(solution)/shard_map/all_to_all | solution.py:20
  221.4 18.4 %copy-start.4 = (bf16[8,3,8,8,256]{4,3,2,1,0:T(8,128)(2,1)S(1)}, bf16[8,3,8,8,256]{4,3,2,1,0:T(8,128)(2,1)}, u32[]{:S(2)}) copy-start(bf16[8,3,8,8,256]{4,3,2,1,0:T(8,128)(2,1)} %copy-done.3) | copy-start | bytes 2359300
  223.3 23.3 %all-to-all-start.8 = ((bf16[32,8,8,256]{3,2,1,0:T(8,128)(2,1)}), bf16[32,8,8,256]{3,2,1,0:T(8,128)(2,1)S(1)}, u32[]{:S(2)}, u32[]{:S(2)}) async-start(bf16[32,8,8,256]{3,2,1,0:T(8,128)(2,1)} %bitcast.78), calls=%async_computation.8 | async-start | bytes 2097152 | tf_op jit(solution)/shard_map/all_to_all | solution.py:20
  231.2 35.8 %collective-permute-start.5 = (bf16[8,8,8,256]{3,2,1,0:T(8,128)(2,1)}, bf16[8,8,8,256]{3,2,1,0:T(8,128)(2,1)S(1)}, u32[]{:S(2)}, u32[]{:S(2)}) collective-permute-start(bf16[8,8,8,256]{3,2,1,0:T(8,128)(2,1)} %all-to-all-done.2), channel_id=1, source_target_pairs={{0,4},{2,6},{4,0},{6,2},{1,5},{3,7},{5,1},{7,3},{8,12},{10,14},{12... | collective-permute-start | bytes 786440 | tf_op jit(solution)/shard_map/ppermute | solution.py:24
  247.3 21.7 %all-to-all-start.7 = ((bf16[32,8,256]{2,1,0:T(8,128)(2,1)}), bf16[32,8,256]{2,1,0:T(8,128)(2,1)S(1)}, u32[]{:S(2)}, u32[]{:S(2)}) async-start(bf16[32,8,256]{2,1,0:T(8,128)(2,1)} %bitcast.65), calls=%async_computation.7 | async-start | bytes 262144 | tf_op jit(solution)/shard_map/all_to_all | solution.py:20
  267.0 2.3 copy-start.1

commit v2 on v1

v2 whole, which is shorter than its diff:
```python
import math

import jax
import jax.numpy as jnp
from jax import lax
from jax.experimental import pallas as pl
from jax.experimental.pallas import tpu as pltpu
from jax.sharding import Mesh, PartitionSpec as P

X, ZL, Y, ZH, C = 4, 4, 4, 4, 2
SHARD = ("y", "zh", "c")
PLANE = ("x", "y", "c")
LINE = ("zl", "zh")
HIGH = lax.Precision.HIGHEST
F32 = jnp.float32
BF16 = jnp.bfloat16


def exchange(parts, axes):
    return lax.all_to_all(parts, axes, 0, 0, tiled=True)


def local_kernel(picks, coefs, tensor, bank, bank_t, out):
    def column(u, carry):
        block = tensor[u]
        total = None
        for term in range(picks.shape[0]):
            left = bank[picks[term, 0]]
            right = bank_t[picks[term, 1]]
            image = jax.lax.dot_general(
                right, block, (((1,), (1,)), ((), ())), preferred_element_type=F32
            ).astype(BF16)
            part = coefs[term] * jnp.dot(image, left, preferred_element_type=F32)
            total = part if total is None else total + part
        out[u] = total.astype(out.dtype)
        return carry

    lax.fori_loop(0, tensor.shape[0], column, 0)


def local_columns(tensor, bank, bank_t, picks, coefs):
    blk, bond, _ = tensor.shape
    flops = 4 * blk * bond**3 * picks.shape[0]
    return pl.pallas_call(
        local_kernel,
        out_shape=jax.ShapeDtypeStruct((blk, bond, bond), BF16),
        in_specs=[pl.BlockSpec(memory_space=pltpu.SMEM)] * 2
        + [pl.BlockSpec(memory_space=pltpu.VMEM)] * 3,
        out_specs=pl.BlockSpec(memory_space=pltpu.VMEM),
        cost_estimate=pl.CostEstimate(
            flops=flops, bytes_accessed=8 * blk * bond * bond, transcendentals=0
        ),
        compiler_params=pltpu.CompilerParams(vmem_limit_bytes=16 * 2**20),
        name="local_columns",
    )(picks, coefs, tensor, bank, bank_t)


def result_kernel(right, hole, arrived, out):
    lines = 256

    def chunk(i, carry):
        at = pl.ds(pl.multiple_of(i * lines, lines), lines)
        moved = jnp.dot(right[at, :], hole[...], preferred_element_type=F32)
        out[at, :] = (arrived[at, :].astype(F32) + moved).astype(out.dtype)
        return carry

    lax.fori_loop(0, right.shape[0] // lines, chunk, 0)


def result_rows(right, hole, arrived):
    rows, bond = right.shape
    return pl.pallas_call(
        result_kernel,
        out_shape=jax.ShapeDtypeStruct((rows, bond), BF16),
        in_specs=[pl.BlockSpec(memory_space=pltpu.VMEM)] * 3,
        out_specs=pl.BlockSpec(memory_space=pltpu.VMEM),
        cost_estimate=pl.CostEstimate(
            flops=2 * rows * bond * bond, bytes_accessed=6 * rows * bond, transcendentals=0
        ),
        compiler_params=pltpu.CompilerParams(vmem_limit_bytes=16 * 2**20),
        name="result_rows",
    )(right, hole, arrived)


def shards(child_tensors, leg_ops, term_ops, term_coef, parent, top_env):
    zl = lax.axis_index("zl")
    plane = (lax.axis_index("x") * Y + lax.axis_index("y")) * C + lax.axis_index("c")
    tensor = child_tensors[0]
    blk, bond, _ = tensor.shape
    devices = Y * ZH * C

    turned = tensor.transpose(2, 0, 1).reshape(devices, blk, blk, bond)
    columns = exchange(turned, SHARD).transpose(1, 0, 2, 3).reshape(blk, bond, bond)

    rows = jnp.broadcast_to(parent[0][None, None], (devices, 1, blk, bond))
    blocks = tensor.reshape(blk, devices, blk, bond).transpose(1, 0, 2, 3)
    blocks = exchange(jnp.concatenate([blocks, rows], axis=1), SHARD)
    right = blocks[:, :blk].reshape(bond * blk, bond)
    lift = blocks[:, blk].reshape(bond, bond).astype(F32)

    local = local_columns(columns, leg_ops, leg_ops.transpose(0, 2, 1), term_ops[0], term_coef[0])
    local = local.reshape(blk, devices, blk, bond).transpose(1, 0, 2, 3)
    local = exchange(local, SHARD).reshape(bond, blk, bond)
    local = local.transpose(2, 1, 0).reshape(bond * blk, bond)

    env = jnp.einsum("pu,pv->uv", right, local, preferred_element_type=F32) / bond
    lifted = jnp.dot(lift.T, jnp.dot(env, lift, precision=HIGH), precision=HIGH)

    lifted = exchange(lifted.astype(BF16).reshape(X * Y * C, blk, bond), PLANE)
    lifted = lifted.reshape(X, Y * C, blk, bond).astype(F32).sum(axis=1).astype(BF16)
    lifted = exchange(jnp.broadcast_to(lifted[None], (ZL * ZH, X, blk, bond)), LINE)
    lifted = lifted.reshape(ZL, ZH, X, blk, bond).astype(F32).sum(axis=1)
    total = lifted.sum(axis=(0, 1))
    mates = lax.dynamic_index_in_dim(lifted, zl, 0, keepdims=False)
    top_rows = lax.dynamic_slice_in_dim(top_env, plane * blk, blk, 0)
    coupling = ((total + top_rows)[None] - mates).astype(BF16)
    coupling = jnp.broadcast_to(coupling[:, None], (X, Y * C, blk, bond))
    coupling = exchange(coupling.reshape(X * Y * C, blk, bond), PLANE)
    coupling = coupling.reshape(bond, bond).astype(F32)
    factor = 1.0 / math.sqrt(bond * X * ZL)
    hole = jnp.dot(jnp.dot(lift, coupling, precision=HIGH), lift.T, precision=HIGH)
    hole = (hole * factor).astype(BF16)

    return result_rows(right, hole, local).reshape(1, bond, blk, bond)


def solution(mesh):
    fine = Mesh(mesh.devices.reshape(X, ZL, Y, ZH, C), ("x", "zl", "y", "zh", "c"))
    child, shard = ("x", "zl"), ("y", "zh", "c")
    in_specs = (
        P(child, shard, None, None),
        P(),
        P(child, None, None),
        P(child, None),
        P(child, shard, None),
        P(),
    )
    out_specs = P(child, None, shard, None)
    return jax.shard_map(shards, mesh=fine, in_specs=in_specs, out_specs=out_specs, check_vma=False)
```

time: 276 us -> 261 us (0.946)
  the two profiles are of different devices: /device:TPU:99 before, /device:TPU:1 now
where the time goes in v2:
time: 261 us; the launch traced here: 258 us
  waiting for transfers between devices  120 us (46%)
  starting transfers between devices  87.5 us (34%)
  blocking collectives  28 us (11%)
  local copies, waits for them, and re-layouts  10.4 us (4%)
  Pallas kernels  8.63 us (3%)
    all_to_all x4, waiting for transfers between devices, exchange(): return lax.all_to_all(parts, axes, 0, 0, tiled=True)  120 us
    all_to_all x4, starting transfers between devices, exchange(): return lax.all_to_all(parts, axes, 0, 0, tiled=True)  87.5 us
    all_to_all x2, blocking collectives, exchange(): return lax.all_to_all(parts, axes, 0, 0, tiled=True)  28 us
    pallas_call x1, Pallas kernels, local_columns(): pl.pallas_call(local_kernel, out_shape=jax.ShapeDtypeStruct((blk, bond, b...  6.13 us
  transfers between devices with their start and end apart: 4, of which 4 were waited for; matrix products, arithmetic and copies ran while one was open for 2% of the time, Pallas kernels for 2%

profile of v2, /device:TPU:1, one launch (start us, length us, event | category | flops | bytes accessed | tf_op | source)
XLA Modules:
  0.0 258.5 jit_solution(6999432085689769714)
XLA Ops:
  0.0 2.6 %copy.20 = bf16[1,8,256,256]{2,1,3,0:T(8,128)(2,1)} copy(bf16[1,8,256,256]{3,2,1,0:T(8,128)(2,1)} %param.6) | data formatting | bytes 2097152 | tf_op args[0]
  2.6 0.0 copy-start.2
  2.6 19.5 %all-to-all-start.1 = ((bf16[32,8,8,256]{3,2,1,0:T(8,128)(2,1)}), bf16[32,8,8,256]{3,2,1,0:T(8,128)(2,1)S(1)}, u32[]{:S(2)}, u32[]{:S(2)}) async-start(bf16[32,8,8,256]{3,2,1,0:T(8,128)(2,1)} %bitcast.9), calls=%async_computation.1 | async-start | bytes 2097152 | tf_op jit(solution)/shard_map/all_to_all | solution.py:20
  22.1 0.0 copy-done.2
  22.2 0.0 copy-start.5
  22.2 0.1 copy_bitcast_fusion.2
  22.3 0.6 copy-done.5
  22.9 1.1 pad_maximum_fusion
  24.0 0.0 copy-start.6
  24.0 0.0 copy-start
  24.0 49.2 %all-to-all-done.1 = bf16[32,8,8,256]{3,2,1,0:T(8,128)(2,1)S(1)} async-done(((bf16[32,8,8,256]{3,2,1,0:T(8,128)(2,1)}), bf16[32,8,8,256]{3,2,1,0:T(8,128)(2,1)S(1)}, u32[]{:S(2)}, u32[]{:S(2)}) %all-to-all-start.1) | async-done | bytes 1048608 | tf_op jit(solution)/shard_map/all_to_all | solution.py:20
  73.2 0.0 copy-start.3
  73.2 9.0 %all-to-all-start = ((bf16[32,9,8,256]{3,2,1,0:T(8,128)(2,1)}), bf16[32,9,8,256]{3,2,1,0:T(8,128)(2,1)S(1)}, u32[]{:S(2)}, u32[]{:S(2)}) async-start(bf16[32,9,8,256]{3,2,1,0:T(8,128)(2,1)} %pad_maximum_fusion), calls=%async_computation | async-start | bytes 2359296 | tf_op jit(solution)/shard_map/all_to_all | solution.py:20
  82.2 0.0 copy-done.3
  82.2 0.0 copy-done.6
  82.2 0.1 copy.23.picks
  82.3 0.0 copy-done
  82.3 0.5 copy.22
  82.9 0.0 copy-start.1
  82.9 1.3 copy_bitcast_fusion.1.tensor
  84.2 0.0 copy-done.1
  84.2 6.1 %local_columns.1 = bf16[8,256,256]{2,1,0:T(8,128)(2,1)S(1)} custom-call(s32[4,2]{1,0:T(4,128)S(1)} %copy.23.picks, f32[4]{0:T(128)S(1)} %bitcast.60, bf16[8,256,256]{2,1,0:T(8,128)(2,1)S(1)} %copy_bitcast_fusion.1.tensor, bf16[8,256,256]{2,1,0:T(8,128)(2,1)S(1)} %copy-done, bf16[8,256,256]{2,1,0:T(8,128)(2,1)S(1)} %bitcast.59), custom_call_target="tpu_custom_call" | custom-call | flops 2147483648 | bytes 4194304 | tf_op jit(solution)/shard_map/local_columns/pallas_call | solution.py:44
  90.3 1.1 copy_bitcast_fusion
  91.4 25.1 %all-to-all-done = bf16[32,9,8,256]{3,2,1,0:T(8,128)(2,1)S(1)} async-done(((bf16[32,9,8,256]{3,2,1,0:T(8,128)(2,1)}), bf16[32,9,8,256]{3,2,1,0:T(8,128)(2,1)S(1)}, u32[]{:S(2)}, u32[]{:S(2)}) %all-to-all-start) | async-done | bytes 1179680 | tf_op jit(solution)/shard_map/all_to_all | solution.py:20
  116.5 30.5 %all-to-all-start.2 = ((bf16[32,8,8,256]{3,2,1,0:T(8,128)(2,1)}), bf16[32,8,8,256]{3,2,1,0:T(8,128)(2,1)S(1)}, u32[]{:S(2)}, u32[]{:S(2)}) async-start(bf16[32,8,8,256]{3,2,1,0:T(8,128)(2,1)} %copy_bitcast_fusion), calls=%async_computation.2 | async-start | bytes 2097152 | tf_op jit(solution)/shard_map/all_to_all | solution.py:20
  147.1 0.1 slice.8
  147.2 30.1 %all-to-all-done.2 = bf16[32,8,8,256]{3,2,1,0:T(8,128)(2,1)S(1)} async-done(((bf16[32,8,8,256]{3,2,1,0:T(8,128)(2,1)}), bf16[32,8,8,256]{3,2,1,0:T(8,128)(2,1)S(1)}, u32[]{:S(2)}, u32[]{:S(2)}) %all-to-all-start.2) | async-done | bytes 1048608 | tf_op jit(solution)/shard_map/all_to_all | solution.py:20
  177.3 0.0 copy-start.4
  177.3 1.0 copy-done.4
  178.2 2.2 copy.25
  180.4 0.5 convolution_multiply_fusion.1
  180.9 0.3 fusion.4
  181.2 0.3 fusion.1
  181.5 14.8 %all_to_all.30 = bf16[32,8,256]{2,1,0:T(8,128)(2,1)S(1)} all-to-all(bf16[32,8,256]{2,1,0:T(8,128)(2,1)S(1)} %fusion.1), channel_id=1, replica_groups=mesh['x'=4,'zl'=4,'y'=4,'zh'=4,'c'=2] {'x','y','c'}, dimensions={0} | all-to-all | bytes 262144 | tf_op jit(solution)/shard_map/all_to_all | solution.py:20
  196.3 0.7 broadcast_in_dim.10
  197.1 28.5 %all-to-all-start.4 = ((bf16[16,4,8,256]{3,2,1,0:T(8,128)(2,1)}), bf16[16,4,8,256]{3,2,1,0:T(8,128)(2,1)S(1)}, u32[]{:S(2)}, u32[]{:S(2)}) async-start(bf16[16,4,8,256]{3,2,1,0:T(8,128)(2,1)} %broadcast_in_dim.10), calls=%async_computation.4 | async-start | bytes 524288 | tf_op jit(solution)/shard_map/all_to_all | solution.py:20
  225.5 15.8 %all-to-all-done.4 = bf16[16,4,8,256]{3,2,1,0:T(8,128)(2,1)S(1)} async-done(((bf16[16,4,8,256]{3,2,1,0:T(8,128)(2,1)}), bf16[16,4,8,256]{3,2,1,0:T(8,128)(2,1)S(1)}, u32[]{:S(2)}, u32[]{:S(2)}) %all-to-all-start.4) | async-done | bytes 262176 | tf_op jit(solution)/shard_map/all_to_all | solution.py:20
  241.4 0.1 convert_reduce_fusion
  241.4 0.7 dynamic-slice_add_fusion
  242.2 13.2 %all_to_all.31 = bf16[32,8,256]{2,1,0:T(8,128)(2,1)S(1)} all-to-all(bf16[32,8,256]{2,1,0:T(8,128)(2,1)S(1)} %bitcast.62), channel_id=1, replica_groups=mesh['x'=4,'zl'=4,'y'=4,'zh'=4,'c'=2] {'x','y','c'}, dimensions={0} | all-to-all | bytes 262144 | tf_op jit(solution)/shard_map/all_to_all | solution.py:20
  255.4 0.2 fusion.2
  255.6 0.3 fusion.hole
  256.0 2.5 result_rows.1
  (5 shorter events, 0.1 us)
Async XLA Ops:
  2.6 19.5 %copy-start.2 = (bf16[1,8,256,256]{3,2,1,0:T(8,128)(2,1)S(1)}, bf16[1,8,256,256]{3,2,1,0:T(8,128)(2,1)}, u32[]{:S(2)}) copy-start(bf16[1,8,256,256]{3,2,1,0:T(8,128)(2,1)} %param.6) | copy-start | bytes 3145732
  2.6 70.6 %all-to-all-start.1 = ((bf16[32,8,8,256]{3,2,1,0:T(8,128)(2,1)}), bf16[32,8,8,256]{3,2,1,0:T(8,128)(2,1)S(1)}, u32[]{:S(2)}, u32[]{:S(2)}) async-start(bf16[32,8,8,256]{3,2,1,0:T(8,128)(2,1)} %bitcast.9), calls=%async_computation.1 | async-start | bytes 2097152 | tf_op jit(solution)/shard_map/all_to_all | solution.py:20
  22.2 0.7 copy-start.5
  24.0 58.2 %copy-start.6 = (s32[1,4,2]{1,2,0:T(2,128)S(1)}, s32[1,4,2]{1,2,0:T(2,128)}, u32[]{:S(2)}) copy-start(s32[1,4,2]{1,2,0:T(2,128)} %param.8) | copy-start | bytes 100
  24.0 58.4 %copy-start = (bf16[8,256,256]{2,1,0:T(8,128)(2,1)S(1)}, bf16[8,256,256]{2,1,0:T(8,128)(2,1)}, u32[]{:S(2)}) copy-start(bf16[8,256,256]{2,1,0:T(8,128)(2,1)} %bank.1) | copy-start | bytes 3145732
  73.2 9.0 %copy-start.3 = (bf16[32,8,8,256]{3,2,1,0:T(8,128)(2,1)}, bf16[32,8,8,256]{3,2,1,0:T(8,128)(2,1)S(1)}, u32[]{:S(2)}) copy-start(bf16[32,8,8,256]{3,2,1,0:T(8,128)(2,1)S(1)} %all-to-all-done.1) | copy-start | bytes 3145732
  73.2 43.3 %all-to-all-start = ((bf16[32,9,8,256]{3,2,1,0:T(8,128)(2,1)}), bf16[32,9,8,256]{3,2,1,0:T(8,128)(2,1)S(1)}, u32[]{:S(2)}, u32[]{:S(2)}) async-start(bf16[32,9,8,256]{3,2,1,0:T(8,128)(2,1)} %pad_maximum_fusion), calls=%async_computation | async-start | bytes 2359296 | tf_op jit(solution)/shard_map/all_to_all | solution.py:20
  82.9 1.3 copy-start.1
  116.5 60.7 %all-to-all-start.2 = ((bf16[32,8,8,256]{3,2,1,0:T(8,128)(2,1)}), bf16[32,8,8,256]{3,2,1,0:T(8,128)(2,1)S(1)}, u32[]{:S(2)}, u32[]{:S(2)}) async-start(bf16[32,8,8,256]{3,2,1,0:T(8,128)(2,1)} %copy_bitcast_fusion), calls=%async_computation.2 | async-start | bytes 2097152 | tf_op jit(solution)/shard_map/all_to_all | solution.py:20
  177.3 1.0 copy-start.4
  197.1 44.3 %all-to-all-start.4 = ((bf16[16,4,8,256]{3,2,1,0:T(8,128)(2,1)}), bf16[16,4,8,256]{3,2,1,0:T(8,128)(2,1)S(1)}, u32[]{:S(2)}, u32[]{:S(2)}) async-start(bf16[16,4,8,256]{3,2,1,0:T(8,128)(2,1)} %broadcast_in_dim.10), calls=%async_computation.4 | async-start | bytes 524288 | tf_op jit(solution)/shard_map/all_to_all | solution.py:20

commit v3 on v1

v3 whole, which is shorter than its diff:
```python
import math

import jax
import jax.numpy as jnp
from jax import lax
from jax.experimental import pallas as pl
from jax.experimental.pallas import tpu as pltpu
from jax.sharding import Mesh, PartitionSpec as P


X, ZL, Y, ZH, C = 4, 4, 4, 4, 2
SHARD = ("y", "zh", "c")
PLANE = ("x", "y", "c")
LINE = ("zl", "zh")
HIGH = lax.Precision.HIGHEST
F32 = jnp.float32
BF16 = jnp.bfloat16


def exchange(parts, axes):
    return lax.all_to_all(parts, axes, 0, 0, tiled=True)


def shifted(piece, shift):
    return lax.ppermute(piece, "zh", [(i, (i + shift) % ZH) for i in range(ZH)])


def tied(*values):
    return lax.optimization_barrier(values)


def local_kernel(picks, coefs, tensor, bank, bank_t, out):
    def column(u, carry):
        block = tensor[u]
        total = None
        for term in range(picks.shape[0]):
            right = bank[picks[term, 1]]
            left = bank_t[picks[term, 0]]
            image = jnp.dot(block, right, preferred_element_type=F32).astype(BF16)
            part = coefs[term] * jnp.dot(left, image, preferred_element_type=F32)
            total = part if total is None else total + part
        out[u] = total.astype(out.dtype)
        return carry

    lax.fori_loop(0, tensor.shape[0], column, 0)


def local_columns(tensor, bank, bank_t, picks, coefs):
    blk, bond, _ = tensor.shape
    flops = 4 * blk * bond**3 * picks.shape[0]
    return pl.pallas_call(
        local_kernel,
        out_shape=jax.ShapeDtypeStruct((blk, bond, bond), BF16),
        in_specs=[pl.BlockSpec(memory_space=pltpu.SMEM)] * 2
        + [pl.BlockSpec(memory_space=pltpu.VMEM)] * 3,
        out_specs=pl.BlockSpec(memory_space=pltpu.VMEM),
        cost_estimate=pl.CostEstimate(
            flops=flops, bytes_accessed=8 * blk * bond * bond, transcendentals=0
        ),
        compiler_params=pltpu.CompilerParams(vmem_limit_bytes=16 * 2**20),
        name="local_columns",
    )(picks, coefs, tensor, bank, bank_t)


def result_kernel(right, hole, arrived, out):
    lines = 256

    def chunk(i, carry):
        at = pl.ds(pl.multiple_of(i * lines, lines), lines)
        moved = jnp.dot(right[at, :], hole[...], preferred_element_type=F32)
        out[at, :] = (arrived[at, :].astype(F32) + moved).astype(out.dtype)
        return carry

    lax.fori_loop(0, right.shape[0] // lines, chunk, 0)


def result_rows(right, hole, arrived):
    rows, bond = right.shape
    return pl.pallas_call(
        result_kernel,
        out_shape=jax.ShapeDtypeStruct((rows, bond), BF16),
        in_specs=[pl.BlockSpec(memory_space=pltpu.VMEM)] * 3,
        out_specs=pl.BlockSpec(memory_space=pltpu.VMEM),
        cost_estimate=pl.CostEstimate(
            flops=2 * rows * bond * bond, bytes_accessed=6 * rows * bond, transcendentals=0
        ),
        compiler_params=pltpu.CompilerParams(vmem_limit_bytes=16 * 2**20),
        name="result_rows",
    )(right, hole, arrived)


def body(child_tensors, leg_ops, term_ops, term_coef, parent, top_env):
    x, zl, zh = lax.axis_index("x"), lax.axis_index("zl"), lax.axis_index("zh")
    plane = (x * Y + lax.axis_index("y")) * C + lax.axis_index("c")
    tensor = child_tensors[0]
    blk, bond, _ = tensor.shape
    rows = parent[0]
    terms = term_coef.shape[1]
    mates_n = Y * C

    high = lax.reduce_precision(term_coef[0], 8, 7)
    mid = lax.reduce_precision(term_coef[0] - high, 8, 7)
    low = term_coef[0] - high - mid
    told = jnp.concatenate([term_ops[0].reshape(-1).astype(F32), high, mid, low]).astype(BF16)
    told = jnp.pad(told[None], ((0, blk - 1), (0, bond - 5 * terms)))
    turned = tensor.transpose(2, 0, 1).reshape(X, bond // X, blk, bond)
    extra = jnp.broadcast_to(jnp.stack([rows, told])[None], (X, 2, blk, bond))
    met = exchange(jnp.concatenate([turned, extra], axis=1), ("x",))
    met_rows = met[:, bond // X]
    heard = lax.dynamic_index_in_dim(met[:, bond // X + 1], zh, 0, keepdims=False)[0].astype(F32)
    picks = heard[: 2 * terms].reshape(terms, 2).astype(jnp.int32)
    coefs = heard[2 * terms : 5 * terms].reshape(3, terms).sum(axis=0)

    met = met[:, : bond // X].reshape(X, Y, C, blk, blk, bond).transpose(1, 0, 2, 3, 4, 5)
    home = exchange(met.reshape(Y * ZH * C, blk, blk, bond), SHARD)

    by_leg = tensor.reshape(blk, Y, ZH, C, blk, bond)

    def for_right(shift):
        piece = lax.dynamic_index_in_dim(by_leg, (zh + shift) % ZH, 2, keepdims=False)
        piece = piece.transpose(1, 2, 0, 3, 4).reshape(mates_n * blk, blk, bond)
        return jnp.concatenate([piece, rows[None]], axis=0)

    def for_home(shift):
        return lax.dynamic_index_in_dim(met_rows, (zh + shift) % X, 0)

    legs = {s: for_right(s) for s in range(ZH)}
    parts = {s: for_home(s) for s in range(ZH)}
    for s in (1, 3, 2):
        parts[s] = shifted(parts[s], s)
    for s in (1, 3):
        legs[s] = shifted(legs[s], s)
    home_rows = jnp.zeros((ZH, blk, bond), BF16)
    for s in range(ZH):
        home_rows = lax.dynamic_update_slice_in_dim(home_rows, parts[s], (zh - s) % ZH, 0)

    columns = home.transpose(1, 0, 2, 3).reshape(blk, bond, bond)
    local = local_columns(columns, leg_ops, leg_ops.transpose(0, 2, 1), picks, coefs)

    leaving = local.reshape(blk, bond, Y, ZH, C, blk).transpose(3, 2, 4, 0, 5, 1)

    def for_away(shift):
        return lax.dynamic_index_in_dim(leaving, (zh + shift) % ZH, 0, keepdims=False)

    away = jnp.zeros((X, Y, C, blk, blk, bond), BF16)
    for s in (0, 1, 3, 2):
        piece = shifted(for_away(s), s) if s else for_away(s)
        away = lax.dynamic_update_slice_in_dim(away, piece[None], (zh - s) % ZH, 0)

    local_rows = local.reshape(blk, bond // blk, blk, bond).transpose(1, 0, 2, 3)
    said = lax.dynamic_index_in_dim(home_rows, x, 0)[None]
    said = jnp.broadcast_to(said, (X * Y * C, 1, blk, bond))
    both = exchange(jnp.concatenate([home, local_rows, said], axis=1), PLANE)
    bra = both[:, :blk].reshape(bond, blk, bond)
    ket = both[:, blk : 2 * blk].reshape(bond, blk, bond)
    home_p = both[:, 2 * blk].reshape(X, Y, C, blk, bond).transpose(1, 0, 2, 3, 4)
    home_p = home_p.reshape(bond, bond).astype(F32)
    env = jnp.einsum("ulr,vlr->uv", bra, ket, preferred_element_type=F32) / bond
    lifted = jnp.dot(home_p.T, jnp.dot(env, home_p, precision=HIGH), precision=HIGH)
    lifted = exchange(lifted.astype(BF16).reshape(X * Y * C, blk, bond), PLANE)
    lifted = lifted.astype(F32).sum(axis=0).astype(BF16)
    everyone = exchange(jnp.broadcast_to(lifted[None], (ZL * ZH, blk, bond)), LINE)

    far, everyone = tied(legs[2], everyone)
    legs[2] = shifted(far, 2)

    everyone = everyone.astype(F32)
    total = everyone.sum(axis=0)
    mates = lax.dynamic_index_in_dim(
        everyone.reshape(ZL, ZH, blk, bond), zl, 0, keepdims=False
    )
    top_rows = lax.dynamic_slice_in_dim(top_env, plane * blk, blk, 0)
    coupling = ((total + top_rows)[None] - mates).astype(BF16)
    coupling = jnp.broadcast_to(coupling[:, None], (X, Y * C, blk, bond))
    coupling = exchange(coupling.reshape(X * Y * C, blk, bond), PLANE)
    coupling = coupling.reshape(bond, bond).astype(F32)

    split = mates_n * blk
    right = jnp.zeros((Y, C, ZH, blk + 1, blk, bond), BF16)
    for s in (0, 1, 3, 2):
        piece = legs[s][:split].reshape(Y, C, 1, blk, blk, bond)
        row = jnp.broadcast_to(legs[s][split:], (Y, C, 1, 1, blk, bond))
        piece = jnp.concatenate([piece, row], axis=3)
        right = lax.dynamic_update_slice_in_dim(right, piece, (zh - s) % ZH, 2)
    right = exchange(right.reshape(mates_n, ZH, blk + 1, blk, bond), ("y", "c"))
    right = right.reshape(Y, C, ZH, blk + 1, blk, bond).transpose(0, 2, 1, 3, 4, 5)
    lift = right[:, :, :, blk].reshape(bond, bond).astype(F32)
    right = right[:, :, :, :blk].reshape(bond * blk, bond)

    factor = 1.0 / math.sqrt(bond * X * ZL)
    hole = jnp.dot(jnp.dot(lift, coupling, precision=HIGH), lift.T, precision=HIGH)
    hole = (hole * factor).astype(BF16)

    arrived = exchange(away.reshape(X * Y * C, blk, blk, bond), PLANE).reshape(bond, blk, bond)
    arrived = arrived.transpose(2, 1, 0).reshape(bond * blk, bond)
    return result_rows(right, hole, arrived).reshape(1, bond, blk, bond)


def solution(mesh):
    fine = Mesh(mesh.devices.reshape(X, ZL, Y, ZH, C), ("x", "zl", "y", "zh", "c"))
    child, shard = ("x", "zl"), ("y", "zh", "c")
    in_specs = (
        P(child, shard, None, None),
        P(),
        P(child, None, None),
        P(child, None),
        P(child, shard, None),
        P(),
    )
    out_specs = P(child, None, shard, None)
    return jax.shard_map(body, mesh=fine, in_specs=in_specs, out_specs=out_specs, check_vma=False)
```

time: 276 us -> 303 us (1.098)
  the two profiles are of different devices: /device:TPU:99 before, /device:TPU:33 now
where the time goes in v3:
time: 303 us; the launch traced here: 302 us
  waiting for transfers between devices  132 us (44%)
  starting transfers between devices  108 us (36%)
  local copies, waits for them, and re-layouts  25.8 us (9%)
  blocking collectives  18.1 us (6%)
  Pallas kernels  7.97 us (3%)
  other arithmetic  7.32 us (2%)
    ppermute x9, waiting for transfers between devices, shifted(): return lax.ppermute(piece, 'zh', [(i, (i + shift) % ZH) for i in range(ZH)])  99.4 us
    all_to_all x7, starting transfers between devices, exchange(): return lax.all_to_all(parts, axes, 0, 0, tiled=True)  60.8 us
    ppermute x9, starting transfers between devices, shifted(): return lax.ppermute(piece, 'zh', [(i, (i + shift) % ZH) for i in range(ZH)])  47 us
    all_to_all x7, waiting for transfers between devices, exchange(): return lax.all_to_all(parts, axes, 0, 0, tiled=True)  32.3 us
    all_to_all x1, blocking collectives, exchange(): return lax.all_to_all(parts, axes, 0, 0, tiled=True)  18.1 us
  transfers between devices with their start and end apart: 16, of which 8 were waited for; matrix products, arithmetic and copies ran while one was open for 8% of the time, Pallas kernels for 0%

profile of v3, /device:TPU:33, one launch (start us, length us, event | category | flops | bytes accessed | tf_op | source)
XLA Modules:
  0.0 301.8 jit_solution(6730880549504695430)
XLA Ops:
  1.6 1.9 copy.90
  3.6 18.1 %all_to_all.40 = bf16[4,66,8,256]{3,2,1,0:T(8,128)(2,1)S(1)} all-to-all(bf16[4,66,8,256]{3,2,1,0:T(8,128)(2,1)S(1)} %pad_maximum_fusion.1), channel_id=1, replica_groups=mesh['x'=4,'zl'=4,'y'=4,'zh'=4,'c'=2] {'x'}, dimensions={0} | all-to-all | bytes 2162688 | tf_op jit(solution)/shard_map/all_to_all | solution.py:21
  21.8 0.9 copy-done.3
  22.7 1.0 copy.92
  23.8 19.2 %all-to-all-start.1 = ((bf16[32,8,8,256]{3,2,1,0:T(8,128)(2,1)}), bf16[32,8,8,256]{3,2,1,0:T(8,128)(2,1)S(1)}, u32[]{:S(2)}, u32[]{:S(2)}) async-start(bf16[32,8,8,256]{3,2,1,0:T(8,128)(2,1)} %bitcast.26), calls=%async_computation.1 | async-start | bytes 2097152 | tf_op jit(solution)/shard_map/all_to_all | solution.py:21
  44.6 7.2 %collective-permute-start.4 = (bf16[1,8,256]{2,1,0:T(8,128)(2,1)S(1)}, bf16[1,8,256]{2,1,0:T(8,128)(2,1)S(1)}, u32[]{:S(2)}, u32[]{:S(2)}) collective-permute-start(bf16[1,8,256]{2,1,0:T(8,128)(2,1)S(1)} %get-tuple-element.20), channel_id=1, source_target_pairs={{0,6},{2,0},{4,2},{6,4},{1,7},{3,1},{5,3},{7,5},{8,14},{10,8},{12,... | collective-permute-start | bytes 12296 | tf_op jit(solution)/shard_map/ppermute | solution.py:25
  51.7 7.0 %collective-permute-start.3 = (bf16[1,8,256]{2,1,0:T(8,128)(2,1)S(1)}, bf16[1,8,256]{2,1,0:T(8,128)(2,1)S(1)}, u32[]{:S(2)}, u32[]{:S(2)}) collective-permute-start(bf16[1,8,256]{2,1,0:T(8,128)(2,1)S(1)} %get-tuple-element.21), channel_id=1, source_target_pairs={{0,4},{2,6},{4,0},{6,2},{1,5},{3,7},{5,1},{7,3},{8,12},{10,14},{12... | collective-permute-start | bytes 12296 | tf_op jit(solution)/shard_map/ppermute | solution.py:25
  58.7 7.0 %collective-permute-start.2 = (bf16[1,8,256]{2,1,0:T(8,128)(2,1)S(1)}, bf16[1,8,256]{2,1,0:T(8,128)(2,1)S(1)}, u32[]{:S(2)}, u32[]{:S(2)}) collective-permute-start(bf16[1,8,256]{2,1,0:T(8,128)(2,1)S(1)} %get-tuple-element.22), channel_id=1, source_target_pairs={{0,2},{2,4},{4,6},{6,0},{1,3},{3,5},{5,7},{7,1},{8,10},{10,12},{12... | collective-permute-start | bytes 12296 | tf_op jit(solution)/shard_map/ppermute | solution.py:25
  66.0 11.2 %collective-permute-done.2 = bf16[1,8,256]{2,1,0:T(8,128)(2,1)S(1)} collective-permute-done((bf16[1,8,256]{2,1,0:T(8,128)(2,1)S(1)}, bf16[1,8,256]{2,1,0:T(8,128)(2,1)S(1)}, u32[]{:S(2)}, u32[]{:S(2)}) %collective-permute-start.2) | collective-permute-done | bytes 4128 | tf_op jit(solution)/shard_map/ppermute | solution.py:25
  77.2 19.0 %collective-permute-done.3 = bf16[1,8,256]{2,1,0:T(8,128)(2,1)S(1)} collective-permute-done((bf16[1,8,256]{2,1,0:T(8,128)(2,1)S(1)}, bf16[1,8,256]{2,1,0:T(8,128)(2,1)S(1)}, u32[]{:S(2)}, u32[]{:S(2)}) %collective-permute-start.3) | collective-permute-done | bytes 4128 | tf_op jit(solution)/shard_map/ppermute | solution.py:25
  96.2 2.9 all-to-all-done.1
  99.1 0.9 copy-done.1
  100.0 5.5 %local_columns.1 = bf16[8,256,256]{2,1,0:T(8,128)(2,1)S(1)} custom-call(s32[4,2]{1,0:T(4,128)S(1)} %convert_element_type.53.picks, f32[4]{0:T(128)S(1)} %reduce_sum.30.coefs, bf16[8,256,256]{2,1,0:T(8,128)(2,1)S(1)} %copy_bitcast_fusion.1.tensor, bf16[8,256,256]{2,1,0:T(8,128)(2,1)S(1)} %copy-done, bf16[8,256,256]{2,1,0:T(8,128)(2,1)S(1)} %bitcast.148), custom_call_target="tpu_custom_call" | custom-call | flops 2147483648 | bytes 4194304 | tf_op jit(solution)/shard_map/local_columns/pallas_call | solution.py:51
  105.7 1.1 copy-done.2
  106.7 1.7 pad_maximum_fusion
  108.4 4.1 %all-to-all-start.2 = ((bf16[32,17,8,256]{3,2,1,0:T(8,128)(2,1)}), bf16[32,17,8,256]{3,2,1,0:T(8,128)(2,1)S(1)}, u32[]{:S(2)}, u32[]{:S(2)}) async-start(bf16[32,17,8,256]{3,2,1,0:T(8,128)(2,1)} %pad_maximum_fusion), calls=%async_computation.2 | async-start | bytes 4456448 | tf_op jit(solution)/shard_map/all_to_all | solution.py:21
  112.5 1.3 constant_dynamic-slice_fusion.7
  113.9 0.9 pad_maximum_fusion.2
  114.8 2.4 collective-permute-start.1
  117.2 6.8 %collective-permute-start = (bf16[65,8,256]{2,1,0:T(8,128)(2,1)}, bf16[65,8,256]{2,1,0:T(8,128)(2,1)}, u32[]{:S(2)}, u32[]{:S(2)}) collective-permute-start(bf16[65,8,256]{2,1,0:T(8,128)(2,1)} %get-tuple-element.25), channel_id=1, source_target_pairs={{0,2},{2,4},{4,6},{6,0},{1,3},{3,5},{5,7},{7,1},{8,10},{10,12},{12... | collective-permute-start | bytes 798728 | tf_op jit(solution)/shard_map/ppermute | solution.py:25
  124.2 1.1 copy.85
  125.3 1.3 copy.103
  126.6 2.0 dynamic-slice_bitcast_fusion
  128.6 4.1 %collective-permute-start.8 = (bf16[4,2,8,8,256]{4,3,1,0,2:T(8,128)(2,1)}, bf16[4,2,8,8,256]{4,3,1,0,2:T(8,128)(2,1)}, u32[]{:S(2)}, u32[]{:S(2)}) collective-permute-start(bf16[4,2,8,8,256]{4,3,1,0,2:T(8,128)(2,1)} %get-tuple-element.13), channel_id=1, source_target_pairs={{0,4},{2,6},{4,0},{6,2},{1,5},{3,7},{5,1},{7,3},{8,12},{10,14},{12... | collective-permute-start | bytes 786440 | tf_op jit(solution)/shard_map/ppermute | solution.py:25
  132.7 7.3 %collective-permute-start.7 = (bf16[4,2,8,8,256]{4,3,1,0,2:T(8,128)(2,1)}, bf16[4,2,8,8,256]{4,3,1,0,2:T(8,128)(2,1)}, u32[]{:S(2)}, u32[]{:S(2)}) collective-permute-start(bf16[4,2,8,8,256]{4,3,1,0,2:T(8,128)(2,1)} %get-tuple-element.14), channel_id=1, source_target_pairs={{0,6},{2,0},{4,2},{6,4},{1,7},{3,1},{5,3},{7,5},{8,14},{10,8},{12,... | collective-permute-start | bytes 786440 | tf_op jit(solution)/shard_map/ppermute | solution.py:25
  140.0 1.9 collective-permute-start.6
  142.1 1.0 bitcast_dynamic-update-slice_fusion
  144.3 1.0 fusion.2
  145.3 8.7 %all-to-all-start.3 = ((bf16[32,8,256]{2,1,0:T(8,128)(2,1)}), bf16[32,8,256]{2,1,0:T(8,128)(2,1)S(1)}, u32[]{:S(2)}, u32[]{:S(2)}) async-start(bf16[32,8,256]{2,1,0:T(8,128)(2,1)} %fusion.2), calls=%async_computation.3 | async-start | bytes 262144 | tf_op jit(solution)/shard_map/all_to_all | solution.py:21
  154.0 40.8 %collective-permute-done.6 = bf16[4,2,8,8,256]{4,3,1,0,2:T(8,128)(2,1)} collective-permute-done((bf16[4,2,8,8,256]{4,3,1,0,2:T(8,128)(2,1)S(1)}, bf16[4,2,8,8,256]{4,3,1,0,2:T(8,128)(2,1)}, u32[]{:S(2)}, u32[]{:S(2)}) %collective-permute-start.6) | collective-permute-done | bytes 262176 | tf_op jit(solution)/shard_map/ppermute | solution.py:25
  194.8 1.0 bitcast_dynamic-update-slice_fusion.2
  196.5 8.8 %all-to-all-start.4 = ((bf16[16,8,256]{2,1,0:T(8,128)(2,1)}), bf16[16,8,256]{2,1,0:T(8,128)(2,1)S(1)}, u32[]{:S(2)}, u32[]{:S(2)}) async-start(bf16[16,8,256]{2,1,0:T(8,128)(2,1)} %broadcast_in_dim.67), calls=%async_computation.4 | async-start | bytes 131072 | tf_op jit(solution)/shard_map/all_to_all | solution.py:21
  205.3 1.0 bitcast_dynamic-update-slice_fusion.1
  206.3 1.1 copy.105
  207.4 1.7 copy_dynamic-update-slice_fusion
  209.1 7.6 %all-to-all-done.4 = bf16[16,8,256]{2,1,0:T(8,128)(2,1)S(1)} async-done(((bf16[16,8,256]{2,1,0:T(8,128)(2,1)}), bf16[16,8,256]{2,1,0:T(8,128)(2,1)S(1)}, u32[]{:S(2)}, u32[]{:S(2)}) %all-to-all-start.4) | async-done | bytes 65568 | tf_op jit(solution)/shard_map/all_to_all | solution.py:21
  216.7 9.0 %all-to-all-start.7 = ((bf16[32,8,8,256]{3,2,1,0:T(8,128)(2,1)}), bf16[32,8,8,256]{3,2,1,0:T(8,128)(2,1)S(1)}, u32[]{:S(2)}, u32[]{:S(2)}) async-start(bf16[32,8,8,256]{3,2,1,0:T(8,128)(2,1)} %bitcast.69), calls=%async_computation.7 | async-start | bytes 2097152 | tf_op jit(solution)/shard_map/all_to_all | solution.py:21
  226.4 3.3 %collective-permute-start.5 = (bf16[65,8,256]{2,1,0:T(8,128)(2,1)S(1)}, bf16[65,8,256]{2,1,0:T(8,128)(2,1)S(1)}, u32[]{:S(2)}, u32[]{:S(2)}) collective-permute-start(bf16[65,8,256]{2,1,0:T(8,128)(2,1)S(1)} %copy-done.4), channel_id=1, source_target_pairs={{0,4},{2,6},{4,0},{6,2},{1,5},{3,7},{5,1},{7,3},{8,12},{10,14},{12... | collective-permute-start | bytes 798728 | tf_op jit(solution)/shard_map/ppermute | solution.py:25
  230.4 1.0 slice.95
  231.4 1.0 slice.93
  232.4 0.8 fusion.5
  233.9 28.4 %collective-permute-done.5 = bf16[65,8,256]{2,1,0:T(8,128)(2,1)S(1)} collective-permute-done((bf16[65,8,256]{2,1,0:T(8,128)(2,1)S(1)}, bf16[65,8,256]{2,1,0:T(8,128)(2,1)S(1)}, u32[]{:S(2)}, u32[]{:S(2)}) %collective-permute-start.5) | collective-permute-done | bytes 266272 | tf_op jit(solution)/shard_map/ppermute | solution.py:25
  263.1 5.0 %all-to-all-start.5 = ((bf16[8,4,9,8,256]{4,3,2,1,0:T(8,128)(2,1)}), bf16[8,4,9,8,256]{4,3,2,1,0:T(8,128)(2,1)S(1)}, u32[]{:S(2)}, u32[]{:S(2)}) async-start(bf16[8,4,9,8,256]{4,3,2,1,0:T(8,128)(2,1)} %bitcast.47), calls=%async_computation.5 | async-start | bytes 2359296 | tf_op jit(solution)/shard_map/all_to_all | solution.py:21
  268.9 15.6 %all-to-all-done.5 = bf16[8,4,9,8,256]{4,3,2,1,0:T(8,128)(2,1)S(1)} async-done(((bf16[8,4,9,8,256]{4,3,2,1,0:T(8,128)(2,1)}), bf16[8,4,9,8,256]{4,3,2,1,0:T(8,128)(2,1)S(1)}, u32[]{:S(2)}, u32[]{:S(2)}) %all-to-all-start.5) | async-done | bytes 1179680 | tf_op jit(solution)/shard_map/all_to_all | solution.py:21
  285.1 6.0 %all-to-all-start.6 = ((bf16[32,8,256]{2,1,0:T(8,128)(2,1)}), bf16[32,8,256]{2,1,0:T(8,128)(2,1)S(1)}, u32[]{:S(2)}, u32[]{:S(2)}) async-start(bf16[32,8,256]{2,1,0:T(8,128)(2,1)} %bitcast.55), calls=%async_computation.6 | async-start | bytes 262144 | tf_op jit(solution)/shard_map/all_to_all | solution.py:21
  291.1 1.3 copy.107
  292.7 6.1 %all-to-all-done.6 = bf16[32,8,256]{2,1,0:T(8,128)(2,1)S(1)} async-done(((bf16[32,8,256]{2,1,0:T(8,128)(2,1)}), bf16[32,8,256]{2,1,0:T(8,128)(2,1)S(1)}, u32[]{:S(2)}, u32[]{:S(2)}) %all-to-all-start.6) | async-done | bytes 131104 | tf_op jit(solution)/shard_map/all_to_all | solution.py:21
  299.4 2.5 result_rows.1
  (78 shorter events, 10.9 us)
Async XLA Ops:
  0.0 3.5 %copy-start.5 = (bf16[1,8,256]{2,1,0:T(8,128)(2,1)S(1)}, bf16[1,8,256]{2,1,0:T(8,128)(2,1)}, u32[]{:S(2)}) copy-start(bf16[1,8,256]{2,1,0:T(8,128)(2,1)} %param.10) | copy-start | bytes 12292
  21.7 1.0 copy-start.3
  23.8 19.3 %copy-start = (bf16[8,256,256]{2,1,0:T(8,128)(2,1)S(1)}, bf16[8,256,256]{2,1,0:T(8,128)(2,1)}, u32[]{:S(2)}) copy-start(bf16[8,256,256]{2,1,0:T(8,128)(2,1)} %bank.1) | copy-start | bytes 3145732
  23.8 75.3 %all-to-all-start.1 = ((bf16[32,8,8,256]{3,2,1,0:T(8,128)(2,1)}), bf16[32,8,8,256]{3,2,1,0:T(8,128)(2,1)S(1)}, u32[]{:S(2)}, u32[]{:S(2)}) async-start(bf16[32,8,8,256]{3,2,1,0:T(8,128)(2,1)} %bitcast.26), calls=%async_computation.1 | async-start | bytes 2097152 | tf_op jit(solution)/shard_map/all_to_all | solution.py:21
  44.6 51.6 %collective-permute-start.4 = (bf16[1,8,256]{2,1,0:T(8,128)(2,1)S(1)}, bf16[1,8,256]{2,1,0:T(8,128)(2,1)S(1)}, u32[]{:S(2)}, u32[]{:S(2)}) collective-permute-start(bf16[1,8,256]{2,1,0:T(8,128)(2,1)S(1)} %get-tuple-element.20), channel_id=1, source_target_pairs={{0,6},{2,0},{4,2},{6,4},{1,7},{3,1},{5,3},{7,5},{8,14},{10,8},{12,... | collective-permute-start | bytes 12296 | tf_op jit(solution)/shard_map/ppermute | solution.py:25
  51.7 44.4 %collective-permute-start.3 = (bf16[1,8,256]{2,1,0:T(8,128)(2,1)S(1)}, bf16[1,8,256]{2,1,0:T(8,128)(2,1)S(1)}, u32[]{:S(2)}, u32[]{:S(2)}) collective-permute-start(bf16[1,8,256]{2,1,0:T(8,128)(2,1)S(1)} %get-tuple-element.21), channel_id=1, source_target_pairs={{0,4},{2,6},{4,0},{6,2},{1,5},{3,7},{5,1},{7,3},{8,12},{10,14},{12... | collective-permute-start | bytes 12296 | tf_op jit(solution)/shard_map/ppermute | solution.py:25
  58.7 18.4 %collective-permute-start.2 = (bf16[1,8,256]{2,1,0:T(8,128)(2,1)S(1)}, bf16[1,8,256]{2,1,0:T(8,128)(2,1)S(1)}, u32[]{:S(2)}, u32[]{:S(2)}) collective-permute-start(bf16[1,8,256]{2,1,0:T(8,128)(2,1)S(1)} %get-tuple-element.22), channel_id=1, source_target_pairs={{0,2},{2,4},{4,6},{6,0},{1,3},{3,5},{5,7},{7,1},{8,10},{10,12},{12... | collective-permute-start | bytes 12296 | tf_op jit(solution)/shard_map/ppermute | solution.py:25
  99.1 1.0 copy-start.1
  105.5 1.2 copy-start.2
  108.4 34.7 %all-to-all-start.2 = ((bf16[32,17,8,256]{3,2,1,0:T(8,128)(2,1)}), bf16[32,17,8,256]{3,2,1,0:T(8,128)(2,1)S(1)}, u32[]{:S(2)}, u32[]{:S(2)}) async-start(bf16[32,17,8,256]{3,2,1,0:T(8,128)(2,1)} %pad_maximum_fusion), calls=%async_computation.2 | async-start | bytes 4456448 | tf_op jit(solution)/shard_map/all_to_all | solution.py:21
  114.8 110.9 %collective-permute-start.1 = (bf16[65,8,256]{2,1,0:T(8,128)(2,1)}, bf16[65,8,256]{2,1,0:T(8,128)(2,1)}, u32[]{:S(2)}, u32[]{:S(2)}) collective-permute-start(bf16[65,8,256]{2,1,0:T(8,128)(2,1)} %get-tuple-element.24), channel_id=1, source_target_pairs={{0,6},{2,0},{4,2},{6,4},{1,7},{3,1},{5,3},{7,5},{8,14},{10,8},{12,... | collective-permute-start | bytes 798728 | tf_op jit(solution)/shard_map/ppermute | solution.py:25
  117.2 112.5 %collective-permute-start = (bf16[65,8,256]{2,1,0:T(8,128)(2,1)}, bf16[65,8,256]{2,1,0:T(8,128)(2,1)}, u32[]{:S(2)}, u32[]{:S(2)}) collective-permute-start(bf16[65,8,256]{2,1,0:T(8,128)(2,1)} %get-tuple-element.25), channel_id=1, source_target_pairs={{0,2},{2,4},{4,6},{6,0},{1,3},{3,5},{5,7},{7,1},{8,10},{10,12},{12... | collective-permute-start | bytes 798728 | tf_op jit(solution)/shard_map/ppermute | solution.py:25
  128.6 78.8 %collective-permute-start.8 = (bf16[4,2,8,8,256]{4,3,1,0,2:T(8,128)(2,1)}, bf16[4,2,8,8,256]{4,3,1,0,2:T(8,128)(2,1)}, u32[]{:S(2)}, u32[]{:S(2)}) collective-permute-start(bf16[4,2,8,8,256]{4,3,1,0,2:T(8,128)(2,1)} %get-tuple-element.13), channel_id=1, source_target_pairs={{0,4},{2,6},{4,0},{6,2},{1,5},{3,7},{5,1},{7,3},{8,12},{10,14},{12... | collective-permute-start | bytes 786440 | tf_op jit(solution)/shard_map/ppermute | solution.py:25
  132.7 72.6 %collective-permute-start.7 = (bf16[4,2,8,8,256]{4,3,1,0,2:T(8,128)(2,1)}, bf16[4,2,8,8,256]{4,3,1,0,2:T(8,128)(2,1)}, u32[]{:S(2)}, u32[]{:S(2)}) collective-permute-start(bf16[4,2,8,8,256]{4,3,1,0,2:T(8,128)(2,1)} %get-tuple-element.14), channel_id=1, source_target_pairs={{0,6},{2,0},{4,2},{6,4},{1,7},{3,1},{5,3},{7,5},{8,14},{10,8},{12,... | collective-permute-start | bytes 786440 | tf_op jit(solution)/shard_map/ppermute | solution.py:25
  140.0 54.8 %collective-permute-start.6 = (bf16[4,2,8,8,256]{4,3,1,0,2:T(8,128)(2,1)S(1)}, bf16[4,2,8,8,256]{4,3,1,0,2:T(8,128)(2,1)}, u32[]{:S(2)}, u32[]{:S(2)}) collective-permute-start(bf16[4,2,8,8,256]{4,3,1,0,2:T(8,128)(2,1)S(1)} %get-tuple-element.15), channel_id=1, source_target_pairs={{0,2},{2,4},{4,6},{6,0},{1,3},{3,5},{5,7},{7,1},{8,10},{10,12},{12... | collective-permute-start | bytes 786440 | tf_op jit(solution)/shard_map/ppermute | solution.py:25
  145.3 50.5 %all-to-all-start.3 = ((bf16[32,8,256]{2,1,0:T(8,128)(2,1)}), bf16[32,8,256]{2,1,0:T(8,128)(2,1)S(1)}, u32[]{:S(2)}, u32[]{:S(2)}) async-start(bf16[32,8,256]{2,1,0:T(8,128)(2,1)} %fusion.2), calls=%async_computation.3 | async-start | bytes 262144 | tf_op jit(solution)/shard_map/all_to_all | solution.py:21
  196.5 20.2 %all-to-all-start.4 = ((bf16[16,8,256]{2,1,0:T(8,128)(2,1)}), bf16[16,8,256]{2,1,0:T(8,128)(2,1)S(1)}, u32[]{:S(2)}, u32[]{:S(2)}) async-start(bf16[16,8,256]{2,1,0:T(8,128)(2,1)} %broadcast_in_dim.67), calls=%async_computation.4 | async-start | bytes 131072 | tf_op jit(solution)/shard_map/all_to_all | solution.py:21
  209.1 17.3 %copy-start.4 = (bf16[65,8,256]{2,1,0:T(8,128)(2,1)S(1)}, bf16[65,8,256]{2,1,0:T(8,128)(2,1)}, u32[]{:S(2)}) copy-start(bf16[65,8,256]{2,1,0:T(8,128)(2,1)} %get-tuple-element.7) | copy-start | bytes 798724
  216.7 46.4 %all-to-all-start.7 = ((bf16[32,8,8,256]{3,2,1,0:T(8,128)(2,1)}), bf16[32,8,8,256]{3,2,1,0:T(8,128)(2,1)S(1)}, u32[]{:S(2)}, u32[]{:S(2)}) async-start(bf16[32,8,8,256]{3,2,1,0:T(8,128)(2,1)} %bitcast.69), calls=%async_computation.7 | async-start | bytes 2097152 | tf_op jit(solution)/shard_map/all_to_all | solution.py:21
  226.4 35.9 %collective-permute-start.5 = (bf16[65,8,256]{2,1,0:T(8,128)(2,1)S(1)}, bf16[65,8,256]{2,1,0:T(8,128)(2,1)S(1)}, u32[]{:S(2)}, u32[]{:S(2)}) collective-permute-start(bf16[65,8,256]{2,1,0:T(8,128)(2,1)S(1)} %copy-done.4), channel_id=1, source_target_pairs={{0,4},{2,6},{4,0},{6,2},{1,5},{3,7},{5,1},{7,3},{8,12},{10,14},{12... | collective-permute-start | bytes 798728 | tf_op jit(solution)/shard_map/ppermute | solution.py:25
  263.1 21.4 %all-to-all-start.5 = ((bf16[8,4,9,8,256]{4,3,2,1,0:T(8,128)(2,1)}), bf16[8,4,9,8,256]{4,3,2,1,0:T(8,128)(2,1)S(1)}, u32[]{:S(2)}, u32[]{:S(2)}) async-start(bf16[8,4,9,8,256]{4,3,2,1,0:T(8,128)(2,1)} %bitcast.47), calls=%async_computation.5 | async-start | bytes 2359296 | tf_op jit(solution)/shard_map/all_to_all | solution.py:21
  285.1 13.7 %all-to-all-start.6 = ((bf16[32,8,256]{2,1,0:T(8,128)(2,1)}), bf16[32,8,256]{2,1,0:T(8,128)(2,1)S(1)}, u32[]{:S(2)}, u32[]{:S(2)}) async-start(bf16[32,8,256]{2,1,0:T(8,128)(2,1)} %bitcast.55), calls=%async_computation.6 | async-start | bytes 262144 | tf_op jit(solution)/shard_map/all_to_all | solution.py:21

commit v4 on v2

--- a/solution.py
+++ b/solution.py
@@ -10,7 +10,6 @@
 X, ZL, Y, ZH, C = 4, 4, 4, 4, 2
 SHARD = ("y", "zh", "c")
 PLANE = ("x", "y", "c")
-LINE = ("zl", "zh")
 HIGH = lax.Precision.HIGHEST
 F32 = jnp.float32
 BF16 = jnp.bfloat16
@@ -18,6 +17,21 @@
 
 def exchange(parts, axes):
     return lax.all_to_all(parts, axes, 0, 0, tiled=True)
+
+
+def gathered(piece, axis, length):
+    at = lax.axis_index(axis)
+    whole = jnp.zeros((length, *piece.shape), piece.dtype)
+    for shift in range(length):
+        moved = piece
+        if shift:
+            moved = permuted(piece, axis, [(i, (i + shift) % length) for i in range(length)])
+        whole = lax.dynamic_update_slice_in_dim(whole, moved[None], (at - shift) % length, 0)
+    return whole
+
+
+def permuted(piece, axis, pairs):
+    return lax.ppermute(piece, axis, pairs)
 
 
 def local_kernel(picks, coefs, tensor, bank, bank_t, out):
@@ -83,7 +97,6 @@
 
 
 def shards(child_tensors, leg_ops, term_ops, term_coef, parent, top_env):
-    zl = lax.axis_index("zl")
     plane = (lax.axis_index("x") * Y + lax.axis_index("y")) * C + lax.axis_index("c")
     tensor = child_tensors[0]
     blk, bond, _ = tensor.shape
@@ -92,14 +105,17 @@
     turned = tensor.transpose(2, 0, 1).reshape(devices, blk, blk, bond)
     columns = exchange(turned, SHARD).transpose(1, 0, 2, 3).reshape(blk, bond, bond)
 
-    rows = jnp.broadcast_to(parent[0][None, None], (devices, 1, blk, bond))
+    lift = gathered(parent[0], "zh", ZH)
+
     blocks = tensor.reshape(blk, devices, blk, bond).transpose(1, 0, 2, 3)
-    blocks = exchange(jnp.concatenate([blocks, rows], axis=1), SHARD)
-    right = blocks[:, :blk].reshape(bond * blk, bond)
-    lift = blocks[:, blk].reshape(bond, bond).astype(F32)
+    blocks, lift = lax.optimization_barrier((blocks, lift))
+    right = exchange(blocks, SHARD).reshape(bond * blk, bond)
 
     local = local_columns(columns, leg_ops, leg_ops.transpose(0, 2, 1), term_ops[0], term_coef[0])
     local = local.reshape(blk, devices, blk, bond).transpose(1, 0, 2, 3)
+    local, right, lift = lax.optimization_barrier((local, right, lift))
+    lift = gathered(gathered(lift, "c", C), "y", Y)
+    lift = lift.transpose(0, 2, 1, 3, 4).reshape(bond, bond).astype(F32)
     local = exchange(local, SHARD).reshape(bond, blk, bond)
     local = local.transpose(2, 1, 0).reshape(bond * blk, bond)
 
@@ -108,10 +124,10 @@
 
     lifted = exchange(lifted.astype(BF16).reshape(X * Y * C, blk, bond), PLANE)
     lifted = lifted.reshape(X, Y * C, blk, bond).astype(F32).sum(axis=1).astype(BF16)
-    lifted = exchange(jnp.broadcast_to(lifted[None], (ZL * ZH, X, blk, bond)), LINE)
-    lifted = lifted.reshape(ZL, ZH, X, blk, bond).astype(F32).sum(axis=1)
-    total = lifted.sum(axis=(0, 1))
-    mates = lax.dynamic_index_in_dim(lifted, zl, 0, keepdims=False)
+    lifted = exchange(jnp.broadcast_to(lifted[None], (ZH, X, blk, bond)), ("zh",))
+    mates = lifted.astype(F32).sum(axis=0)
+    total = exchange(jnp.broadcast_to(mates.sum(axis=0)[None], (ZL, blk, bond)), ("zl",))
+    total = total.sum(axis=0)
     top_rows = lax.dynamic_slice_in_dim(top_env, plane * blk, blk, 0)
     coupling = ((total + top_rows)[None] - mates).astype(BF16)
     coupling = jnp.broadcast_to(coupling[:, None], (X, Y * C, blk, bond))

time: 261 us -> 259 us (level)
  waiting for transfers between devices: 120 us -> 70.6 us
  blocking collectives: 28 us -> 67.3 us
  starting transfers between devices: 87.5 us -> 98.4 us
    all_to_all x4, waiting for transfers between devices: 120 us -> 40.1 us  [exchange(): return lax.all_to_all(parts, axes, 0, 0, tiled=True)]
    all_to_all x2 -> x3, blocking collectives: 28 us -> 67.3 us  [exchange(): return lax.all_to_all(parts, axes, 0, 0, tiled=True)]
    ppermute x0 -> x7, starting transfers between devices: none -> 34 us  [permuted(): return lax.ppermute(piece, axis, pairs)]
    ppermute x0 -> x7, waiting for transfers between devices: none -> 30.5 us  [permuted(): return lax.ppermute(piece, axis, pairs)]
    all_to_all x4, starting transfers between devices: 87.5 us -> 64.4 us  [exchange(): return lax.all_to_all(parts, axes, 0, 0, tiled=True)]
  transfers between devices with their start and end apart: 4 -> 11, of which waited for: 4 -> 9; matrix products, arithmetic and copies ran while one was open for 2% -> 2% of each run, Pallas kernels for 2% -> 2%
where the time goes in v4:
time: 259 us; the launch traced here: 258 us
  starting transfers between devices  98.4 us (38%)
  waiting for transfers between devices  70.6 us (27%)
  blocking collectives  67.3 us (26%)
  local copies, waits for them, and re-layouts  10 us (4%)
  Pallas kernels  8.64 us (3%)
    all_to_all x3, blocking collectives, exchange(): return lax.all_to_all(parts, axes, 0, 0, tiled=True)  67.3 us
    all_to_all x4, starting transfers between devices, exchange(): return lax.all_to_all(parts, axes, 0, 0, tiled=True)  64.4 us
    all_to_all x4, waiting for transfers between devices, exchange(): return lax.all_to_all(parts, axes, 0, 0, tiled=True)  40.1 us
    ppermute x7, starting transfers between devices, permuted(): return lax.ppermute(piece, axis, pairs)  34 us
    ppermute x7, waiting for transfers between devices, permuted(): return lax.ppermute(piece, axis, pairs)  30.5 us
    pallas_call x1, Pallas kernels, local_columns(): pl.pallas_call(local_kernel, out_shape=jax.ShapeDtypeStruct((blk, bond, b...  6.14 us
  transfers between devices with their start and end apart: 11, of which 9 were waited for; matrix products, arithmetic and copies ran while one was open for 2% of the time, Pallas kernels for 2%

profile of v4, /device:TPU:1, one launch (start us, length us, event | category | flops | bytes accessed | tf_op | source)
XLA Modules:
  0.0 257.7 jit_solution(15934893298524461778)
XLA Ops:
  0.0 2.6 %copy.20 = bf16[1,8,256,256]{2,1,3,0:T(8,128)(2,1)} copy(bf16[1,8,256,256]{3,2,1,0:T(8,128)(2,1)} %param.6) | data formatting | bytes 2097152 | tf_op args[0]
  2.6 19.5 %all-to-all-start = ((bf16[32,8,8,256]{3,2,1,0:T(8,128)(2,1)}), bf16[32,8,8,256]{3,2,1,0:T(8,128)(2,1)S(1)}, u32[]{:S(2)}, u32[]{:S(2)}) async-start(bf16[32,8,8,256]{3,2,1,0:T(8,128)(2,1)} %bitcast.4), calls=%async_computation | async-start | bytes 2097152 | tf_op jit(solution)/shard_map/all_to_all | solution.py:19
  22.1 0.0 copy-done.4
  22.1 7.2 %collective-permute-start = (bf16[8,256]{1,0:T(8,128)(2,1)S(1)}, bf16[8,256]{1,0:T(8,128)(2,1)S(1)}, u32[]{:S(2)}, u32[]{:S(2)}) collective-permute-start(bf16[8,256]{1,0:T(8,128)(2,1)S(1)} %bitcast.82), channel_id=1, source_target_pairs={{0,2},{2,4},{4,6},{6,0},{1,3},{3,5},{5,7},{7,1},{8,10},{10,12},{12... | collective-permute-start | bytes 12296 | tf_op jit(solution)/shard_map/ppermute | solution.py:34
  29.3 7.0 %collective-permute-start.1 = (bf16[8,256]{1,0:T(8,128)(2,1)S(1)}, bf16[8,256]{1,0:T(8,128)(2,1)S(1)}, u32[]{:S(2)}, u32[]{:S(2)}) collective-permute-start(bf16[8,256]{1,0:T(8,128)(2,1)S(1)} %bitcast.83), channel_id=1, source_target_pairs={{0,4},{2,6},{4,0},{6,2},{1,5},{3,7},{5,1},{7,3},{8,12},{10,14},{12... | collective-permute-start | bytes 12296 | tf_op jit(solution)/shard_map/ppermute | solution.py:34
  36.3 7.0 %collective-permute-start.2 = (bf16[8,256]{1,0:T(8,128)(2,1)S(1)}, bf16[8,256]{1,0:T(8,128)(2,1)S(1)}, u32[]{:S(2)}, u32[]{:S(2)}) collective-permute-start(bf16[8,256]{1,0:T(8,128)(2,1)S(1)} %bitcast.84), channel_id=1, source_target_pairs={{0,6},{2,0},{4,2},{6,4},{1,7},{3,1},{5,3},{7,5},{8,14},{10,8},{12,... | collective-permute-start | bytes 12296 | tf_op jit(solution)/shard_map/ppermute | solution.py:34
  43.4 0.0 copy-done.2
  43.4 1.1 copy_bitcast_fusion
  44.5 6.4 %collective-permute-done = bf16[8,256]{1,0:T(8,128)(2,1)S(1)} collective-permute-done((bf16[8,256]{1,0:T(8,128)(2,1)S(1)}, bf16[8,256]{1,0:T(8,128)(2,1)S(1)}, u32[]{:S(2)}, u32[]{:S(2)}) %collective-permute-start) | collective-permute-done | bytes 4128 | tf_op jit(solution)/shard_map/ppermute | solution.py:34
  50.8 9.0 %collective-permute-done.1 = bf16[8,256]{1,0:T(8,128)(2,1)S(1)} collective-permute-done((bf16[8,256]{1,0:T(8,128)(2,1)S(1)}, bf16[8,256]{1,0:T(8,128)(2,1)S(1)}, u32[]{:S(2)}, u32[]{:S(2)}) %collective-permute-start.1) | collective-permute-done | bytes 4128 | tf_op jit(solution)/shard_map/ppermute | solution.py:34
  59.8 12.5 %collective-permute-done.2 = bf16[8,256]{1,0:T(8,128)(2,1)S(1)} collective-permute-done((bf16[8,256]{1,0:T(8,128)(2,1)S(1)}, bf16[8,256]{1,0:T(8,128)(2,1)S(1)}, u32[]{:S(2)}, u32[]{:S(2)}) %collective-permute-start.2) | collective-permute-done | bytes 4128 | tf_op jit(solution)/shard_map/ppermute | solution.py:34
  72.3 1.6 all-to-all-done
  73.9 9.1 %all-to-all-start.1 = ((bf16[32,8,8,256]{3,2,1,0:T(8,128)(2,1)}), bf16[32,8,8,256]{3,2,1,0:T(8,128)(2,1)S(1)}, u32[]{:S(2)}, u32[]{:S(2)}) async-start(bf16[32,8,8,256]{3,2,1,0:T(8,128)(2,1)} %copy_bitcast_fusion), calls=%async_computation.1 | async-start | bytes 2097152 | tf_op jit(solution)/shard_map/all_to_all | solution.py:19
  83.0 0.0 copy-done.3
  83.0 0.0 copy-start.5
  83.0 0.7 copy-done.5
  83.7 0.1 copy.23.picks
  83.8 0.5 copy.22
  84.3 1.3 copy_bitcast_fusion.2.tensor
  85.6 0.0 copy-start.1
  85.6 0.6 copy-done.1
  86.3 6.1 %local_columns.1 = bf16[8,256,256]{2,1,0:T(8,128)(2,1)S(1)} custom-call(s32[4,2]{1,0:T(4,128)S(1)} %copy.23.picks, f32[4]{0:T(128)S(1)} %bitcast.75, bf16[8,256,256]{2,1,0:T(8,128)(2,1)S(1)} %copy_bitcast_fusion.2.tensor, bf16[8,256,256]{2,1,0:T(8,128)(2,1)S(1)} %copy-done, bf16[8,256,256]{2,1,0:T(8,128)(2,1)S(1)} %bitcast.74), custom_call_target="tpu_custom_call" | custom-call | flops 2147483648 | bytes 4194304 | tf_op jit(solution)/shard_map/local_columns/pallas_call | solution.py:58
  92.4 1.1 copy_bitcast_fusion.1
  93.5 19.3 %all-to-all-done.1 = bf16[32,8,8,256]{3,2,1,0:T(8,128)(2,1)S(1)} async-done(((bf16[32,8,8,256]{3,2,1,0:T(8,128)(2,1)}), bf16[32,8,8,256]{3,2,1,0:T(8,128)(2,1)S(1)}, u32[]{:S(2)}, u32[]{:S(2)}) %all-to-all-start.1) | async-done | bytes 1048608 | tf_op jit(solution)/shard_map/all_to_all | solution.py:19
  112.8 31.0 %all-to-all-start.2 = ((bf16[32,8,8,256]{3,2,1,0:T(8,128)(2,1)}), bf16[32,8,8,256]{3,2,1,0:T(8,128)(2,1)S(1)}, u32[]{:S(2)}, u32[]{:S(2)}) async-start(bf16[32,8,8,256]{3,2,1,0:T(8,128)(2,1)} %copy_bitcast_fusion.1), calls=%async_computation.2 | async-start | bytes 2097152 | tf_op jit(solution)/shard_map/all_to_all | solution.py:19
  143.9 2.1 collective-permute-start.3
  146.0 0.9 collective-permute-done.3
  146.9 3.3 %collective-permute-start.4 = (bf16[2,4,8,256]{3,2,0,1:T(8,128)(2,1)S(1)}, bf16[2,4,8,256]{3,2,0,1:T(8,128)(2,1)S(1)}, u32[]{:S(2)}, u32[]{:S(2)}) collective-permute-start(bf16[2,4,8,256]{3,2,0,1:T(8,128)(2,1)S(1)} %bitcast_dynamic-update-slice_fusion.5), channel_id=1, source_target_pairs={{0,8},{8,16},{16,24},{24,0},{1,9},{9,17},{17,25},{25,1},{2,10},{10... | collective-permute-start | bytes 98312 | tf_op jit(solution)/shard_map/ppermute | solution.py:34
  150.3 4.3 %collective-permute-start.5 = (bf16[2,4,8,256]{3,2,0,1:T(8,128)(2,1)S(1)}, bf16[2,4,8,256]{3,2,0,1:T(8,128)(2,1)S(1)}, u32[]{:S(2)}, u32[]{:S(2)}) collective-permute-start(bf16[2,4,8,256]{3,2,0,1:T(8,128)(2,1)S(1)} %bitcast_dynamic-update-slice_fusion.5), channel_id=1, source_target_pairs={{0,16},{8,24},{16,0},{24,8},{1,17},{9,25},{17,1},{25,9},{2,18},{10... | collective-permute-start | bytes 98312 | tf_op jit(solution)/shard_map/ppermute | solution.py:34
  154.6 3.1 %collective-permute-start.6 = (bf16[2,4,8,256]{3,2,0,1:T(8,128)(2,1)S(1)}, bf16[2,4,8,256]{3,2,0,1:T(8,128)(2,1)S(1)}, u32[]{:S(2)}, u32[]{:S(2)}) collective-permute-start(bf16[2,4,8,256]{3,2,0,1:T(8,128)(2,1)S(1)} %bitcast_dynamic-update-slice_fusion.5), channel_id=1, source_target_pairs={{0,24},{8,0},{16,8},{24,16},{1,25},{9,1},{17,9},{25,17},{2,26},{10... | collective-permute-start | bytes 98312 | tf_op jit(solution)/shard_map/ppermute | solution.py:34
  157.7 0.0 collective-permute-done.4
  157.7 0.0 collective-permute-done.5
  157.8 1.8 collective-permute-done.6
  159.6 14.7 %all-to-all-done.2 = bf16[32,8,8,256]{3,2,1,0:T(8,128)(2,1)S(1)} async-done(((bf16[32,8,8,256]{3,2,1,0:T(8,128)(2,1)}), bf16[32,8,8,256]{3,2,1,0:T(8,128)(2,1)S(1)}, u32[]{:S(2)}, u32[]{:S(2)}) %all-to-all-start.2) | async-done | bytes 1048608 | tf_op jit(solution)/shard_map/all_to_all | solution.py:19
  174.2 1.3 copy.27
  175.5 0.5 convolution_multiply_fusion.1
  176.0 0.3 fusion.5
  176.3 0.3 fusion.1
  176.6 14.5 %all_to_all.35 = bf16[32,8,256]{2,1,0:T(8,128)(2,1)S(1)} all-to-all(bf16[32,8,256]{2,1,0:T(8,128)(2,1)S(1)} %fusion.1), channel_id=1, replica_groups=mesh['x'=4,'zl'=4,'y'=4,'zh'=4,'c'=2] {'x','y','c'}, dimensions={0} | all-to-all | bytes 262144 | tf_op jit(solution)/shard_map/all_to_all | solution.py:19
  191.1 38.7 %all_to_all.36 = bf16[4,4,8,256]{3,2,1,0:T(8,128)(2,1)S(1)} all-to-all(bf16[4,4,8,256]{3,2,1,0:T(8,128)(2,1)S(1)} %broadcast_in_dim.67), channel_id=1, replica_groups=mesh['x'=4,'zl'=4,'y'=4,'zh'=4,'c'=2] {'zh'}, dimensions={0} | all-to-all | bytes 131072 | tf_op jit(solution)/shard_map/all_to_all | solution.py:19
  229.9 0.6 broadcast_in_dim.68
  230.5 4.8 %all-to-all-start.5 = ((f32[4,8,256]{2,1,0:T(8,128)}), f32[4,8,256]{2,1,0:T(8,128)S(1)}, u32[]{:S(2)}, u32[]{:S(2)}) async-start(f32[4,8,256]{2,1,0:T(8,128)} %broadcast_in_dim.68), calls=%async_computation.5 | async-start | bytes 65536 | tf_op jit(solution)/shard_map/all_to_all | solution.py:19
  235.4 4.5 %all-to-all-done.5 = f32[4,8,256]{2,1,0:T(8,128)S(1)} async-done(((f32[4,8,256]{2,1,0:T(8,128)}), f32[4,8,256]{2,1,0:T(8,128)S(1)}, u32[]{:S(2)}, u32[]{:S(2)}) %all-to-all-start.5) | async-done | bytes 32800 | tf_op jit(solution)/shard_map/all_to_all | solution.py:19
  239.9 0.7 dynamic-slice_add_fusion
  240.6 14.1 %all_to_all.37 = bf16[32,8,256]{2,1,0:T(8,128)(2,1)S(1)} all-to-all(bf16[32,8,256]{2,1,0:T(8,128)(2,1)S(1)} %bitcast.81), channel_id=1, replica_groups=mesh['x'=4,'zl'=4,'y'=4,'zh'=4,'c'=2] {'x','y','c'}, dimensions={0} | all-to-all | bytes 262144 | tf_op jit(solution)/shard_map/all_to_all | solution.py:19
  254.7 0.2 fusion.2
  254.9 0.3 fusion.hole
  255.2 2.5 result_rows.1
  (24 shorter events, 0.2 us)
Async XLA Ops:
  2.6 19.5 %copy-start.4 = (bf16[1,8,256]{2,1,0:T(8,128)(2,1)S(1)}, bf16[1,8,256]{2,1,0:T(8,128)(2,1)}, u32[]{:S(2)}) copy-start(bf16[1,8,256]{2,1,0:T(8,128)(2,1)} %param.10) | copy-start | bytes 12292
  2.6 40.7 %copy-start.2 = (bf16[1,8,256,256]{3,2,1,0:T(8,128)(2,1)S(1)}, bf16[1,8,256,256]{3,2,1,0:T(8,128)(2,1)}, u32[]{:S(2)}) copy-start(bf16[1,8,256,256]{3,2,1,0:T(8,128)(2,1)} %param.6) | copy-start | bytes 3145732
  2.6 71.3 %all-to-all-start = ((bf16[32,8,8,256]{3,2,1,0:T(8,128)(2,1)}), bf16[32,8,8,256]{3,2,1,0:T(8,128)(2,1)S(1)}, u32[]{:S(2)}, u32[]{:S(2)}) async-start(bf16[32,8,8,256]{3,2,1,0:T(8,128)(2,1)} %bitcast.4), calls=%async_computation | async-start | bytes 2097152 | tf_op jit(solution)/shard_map/all_to_all | solution.py:19
  22.1 28.7 %collective-permute-start = (bf16[8,256]{1,0:T(8,128)(2,1)S(1)}, bf16[8,256]{1,0:T(8,128)(2,1)S(1)}, u32[]{:S(2)}, u32[]{:S(2)}) collective-permute-start(bf16[8,256]{1,0:T(8,128)(2,1)S(1)} %bitcast.82), channel_id=1, source_target_pairs={{0,2},{2,4},{4,6},{6,0},{1,3},{3,5},{5,7},{7,1},{8,10},{10,12},{12... | collective-permute-start | bytes 12296 | tf_op jit(solution)/shard_map/ppermute | solution.py:34
  29.3 30.5 %collective-permute-start.1 = (bf16[8,256]{1,0:T(8,128)(2,1)S(1)}, bf16[8,256]{1,0:T(8,128)(2,1)S(1)}, u32[]{:S(2)}, u32[]{:S(2)}) collective-permute-start(bf16[8,256]{1,0:T(8,128)(2,1)S(1)} %bitcast.83), channel_id=1, source_target_pairs={{0,4},{2,6},{4,0},{6,2},{1,5},{3,7},{5,1},{7,3},{8,12},{10,14},{12... | collective-permute-start | bytes 12296 | tf_op jit(solution)/shard_map/ppermute | solution.py:34
  36.3 36.0 %collective-permute-start.2 = (bf16[8,256]{1,0:T(8,128)(2,1)S(1)}, bf16[8,256]{1,0:T(8,128)(2,1)S(1)}, u32[]{:S(2)}, u32[]{:S(2)}) collective-permute-start(bf16[8,256]{1,0:T(8,128)(2,1)S(1)} %bitcast.84), channel_id=1, source_target_pairs={{0,6},{2,0},{4,2},{6,4},{1,7},{3,1},{5,3},{7,5},{8,14},{10,8},{12,... | collective-permute-start | bytes 12296 | tf_op jit(solution)/shard_map/ppermute | solution.py:34
  72.3 11.5 %copy-start = (bf16[8,256,256]{2,1,0:T(8,128)(2,1)S(1)}, bf16[8,256,256]{2,1,0:T(8,128)(2,1)}, u32[]{:S(2)}) copy-start(bf16[8,256,256]{2,1,0:T(8,128)(2,1)} %bank.1) | copy-start | bytes 3145732
  73.9 9.1 %copy-start.3 = (bf16[32,8,8,256]{3,2,1,0:T(8,128)(2,1)}, bf16[32,8,8,256]{3,2,1,0:T(8,128)(2,1)S(1)}, u32[]{:S(2)}) copy-start(bf16[32,8,8,256]{3,2,1,0:T(8,128)(2,1)S(1)} %all-to-all-done) | copy-start | bytes 3145732
  73.9 38.9 %all-to-all-start.1 = ((bf16[32,8,8,256]{3,2,1,0:T(8,128)(2,1)}), bf16[32,8,8,256]{3,2,1,0:T(8,128)(2,1)S(1)}, u32[]{:S(2)}, u32[]{:S(2)}) async-start(bf16[32,8,8,256]{3,2,1,0:T(8,128)(2,1)} %copy_bitcast_fusion), calls=%async_computation.1 | async-start | bytes 2097152 | tf_op jit(solution)/shard_map/all_to_all | solution.py:19
  83.0 0.7 copy-start.5
  85.6 0.7 copy-start.1
  112.8 61.5 %all-to-all-start.2 = ((bf16[32,8,8,256]{3,2,1,0:T(8,128)(2,1)}), bf16[32,8,8,256]{3,2,1,0:T(8,128)(2,1)S(1)}, u32[]{:S(2)}, u32[]{:S(2)}) async-start(bf16[32,8,8,256]{3,2,1,0:T(8,128)(2,1)} %copy_bitcast_fusion.1), calls=%async_computation.2 | async-start | bytes 2097152 | tf_op jit(solution)/shard_map/all_to_all | solution.py:19
  143.9 3.1 %collective-permute-start.3 = (bf16[4,8,256]{2,1,0:T(8,128)(2,1)S(1)}, bf16[4,8,256]{2,1,0:T(8,128)(2,1)S(1)}, u32[]{:S(2)}, u32[]{:S(2)}) collective-permute-start(bf16[4,8,256]{2,1,0:T(8,128)(2,1)S(1)} %bitcast_dynamic-update-slice_fusion.6), channel_id=1, source_target_pairs={{0,1},{1,0},{2,3},{3,2},{4,5},{5,4},{6,7},{7,6},{8,9},{9,8},{10,11... | collective-permute-start | bytes 49160 | tf_op jit(solution)/shard_map/ppermute | solution.py:34
  146.9 10.8 %collective-permute-start.4 = (bf16[2,4,8,256]{3,2,0,1:T(8,128)(2,1)S(1)}, bf16[2,4,8,256]{3,2,0,1:T(8,128)(2,1)S(1)}, u32[]{:S(2)}, u32[]{:S(2)}) collective-permute-start(bf16[2,4,8,256]{3,2,0,1:T(8,128)(2,1)S(1)} %bitcast_dynamic-update-slice_fusion.5), channel_id=1, source_target_pairs={{0,8},{8,16},{16,24},{24,0},{1,9},{9,17},{17,25},{25,1},{2,10},{10... | collective-permute-start | bytes 98312 | tf_op jit(solution)/shard_map/ppermute | solution.py:34
  150.3 7.5 %collective-permute-start.5 = (bf16[2,4,8,256]{3,2,0,1:T(8,128)(2,1)S(1)}, bf16[2,4,8,256]{3,2,0,1:T(8,128)(2,1)S(1)}, u32[]{:S(2)}, u32[]{:S(2)}) collective-permute-start(bf16[2,4,8,256]{3,2,0,1:T(8,128)(2,1)S(1)} %bitcast_dynamic-update-slice_fusion.5), channel_id=1, source_target_pairs={{0,16},{8,24},{16,0},{24,8},{1,17},{9,25},{17,1},{25,9},{2,18},{10... | collective-permute-start | bytes 98312 | tf_op jit(solution)/shard_map/ppermute | solution.py:34
  154.6 5.0 %collective-permute-start.6 = (bf16[2,4,8,256]{3,2,0,1:T(8,128)(2,1)S(1)}, bf16[2,4,8,256]{3,2,0,1:T(8,128)(2,1)S(1)}, u32[]{:S(2)}, u32[]{:S(2)}) collective-permute-start(bf16[2,4,8,256]{3,2,0,1:T(8,128)(2,1)S(1)} %bitcast_dynamic-update-slice_fusion.5), channel_id=1, source_target_pairs={{0,24},{8,0},{16,8},{24,16},{1,25},{9,1},{17,9},{25,17},{2,26},{10... | collective-permute-start | bytes 98312 | tf_op jit(solution)/shard_map/ppermute | solution.py:34
  230.5 9.4 %all-to-all-start.5 = ((f32[4,8,256]{2,1,0:T(8,128)}), f32[4,8,256]{2,1,0:T(8,128)S(1)}, u32[]{:S(2)}, u32[]{:S(2)}) async-start(f32[4,8,256]{2,1,0:T(8,128)} %broadcast_in_dim.68), calls=%async_computation.5 | async-start | bytes 65536 | tf_op jit(solution)/shard_map/all_to_all | solution.py:19

commit v5 on v4

--- a/solution.py
+++ b/solution.py
@@ -10,6 +10,7 @@
 X, ZL, Y, ZH, C = 4, 4, 4, 4, 2
 SHARD = ("y", "zh", "c")
 PLANE = ("x", "y", "c")
+LINE = ("zl", "zh")
 HIGH = lax.Precision.HIGHEST
 F32 = jnp.float32
 BF16 = jnp.bfloat16
@@ -124,10 +125,10 @@
 
     lifted = exchange(lifted.astype(BF16).reshape(X * Y * C, blk, bond), PLANE)
     lifted = lifted.reshape(X, Y * C, blk, bond).astype(F32).sum(axis=1).astype(BF16)
-    lifted = exchange(jnp.broadcast_to(lifted[None], (ZH, X, blk, bond)), ("zh",))
-    mates = lifted.astype(F32).sum(axis=0)
-    total = exchange(jnp.broadcast_to(mates.sum(axis=0)[None], (ZL, blk, bond)), ("zl",))
-    total = total.sum(axis=0)
+    lifted = exchange(jnp.broadcast_to(lifted[None], (ZL * ZH, X, blk, bond)), LINE)
+    lifted = lifted.reshape(ZL, ZH, X, blk, bond).astype(F32).sum(axis=1)
+    total = lifted.sum(axis=(0, 1))
+    mates = lax.dynamic_index_in_dim(lifted, lax.axis_index("zl"), 0, keepdims=False)
     top_rows = lax.dynamic_slice_in_dim(top_env, plane * blk, blk, 0)
     coupling = ((total + top_rows)[None] - mates).astype(BF16)
     coupling = jnp.broadcast_to(coupling[:, None], (X, Y * C, blk, bond))

time: 259 us -> 255 us (0.985)
  blocking collectives: 67.3 us -> 27.8 us
  starting transfers between devices: 98.4 us -> 122 us
  waiting for transfers between devices: 70.6 us -> 81.9 us
    all_to_all x3 -> x2, blocking collectives: 67.3 us -> 27.8 us  [exchange(): return lax.all_to_all(parts, axes, 0, 0, tiled=True)]
    all_to_all x4, starting transfers between devices: 64.4 us -> 87.6 us  [exchange(): return lax.all_to_all(parts, axes, 0, 0, tiled=True)]
    all_to_all x4, waiting for transfers between devices: 40.1 us -> 51.4 us  [exchange(): return lax.all_to_all(parts, axes, 0, 0, tiled=True)]
where the time goes in v5:
time: 255 us; the launch traced here: 253 us
  starting transfers between devices  122 us (48%)
  waiting for transfers between devices  81.9 us (32%)
  blocking collectives  27.8 us (11%)
  local copies, waits for them, and re-layouts  10.2 us (4%)
  Pallas kernels  8.64 us (3%)
    all_to_all x4, starting transfers between devices, exchange(): return lax.all_to_all(parts, axes, 0, 0, tiled=True)  87.6 us
    all_to_all x4, waiting for transfers between devices, exchange(): return lax.all_to_all(parts, axes, 0, 0, tiled=True)  51.4 us
    ppermute x7, starting transfers between devices, permuted(): return lax.ppermute(piece, axis, pairs)  34 us
    ppermute x7, waiting for transfers between devices, permuted(): return lax.ppermute(piece, axis, pairs)  30.5 us
    all_to_all x2, blocking collectives, exchange(): return lax.all_to_all(parts, axes, 0, 0, tiled=True)  27.8 us
    pallas_call x1, Pallas kernels, local_columns(): pl.pallas_call(local_kernel, out_shape=jax.ShapeDtypeStruct((blk, bond, b...  6.14 us
  transfers between devices with their start and end apart: 11, of which 9 were waited for; matrix products, arithmetic and copies ran while one was open for 2% of the time, Pallas kernels for 2%

profile of v5, /device:TPU:1, one launch (start us, length us, event | category | flops | bytes accessed | tf_op | source)
XLA Modules:
  0.0 252.9 jit_solution(10388767304177550274)
XLA Ops:
  0.0 2.6 %copy.20 = bf16[1,8,256,256]{2,1,3,0:T(8,128)(2,1)} copy(bf16[1,8,256,256]{3,2,1,0:T(8,128)(2,1)} %param.6) | data formatting | bytes 2097152 | tf_op args[0]
  2.6 19.5 %all-to-all-start = ((bf16[32,8,8,256]{3,2,1,0:T(8,128)(2,1)}), bf16[32,8,8,256]{3,2,1,0:T(8,128)(2,1)S(1)}, u32[]{:S(2)}, u32[]{:S(2)}) async-start(bf16[32,8,8,256]{3,2,1,0:T(8,128)(2,1)} %bitcast.4), calls=%async_computation | async-start | bytes 2097152 | tf_op jit(solution)/shard_map/all_to_all | solution.py:20
  22.2 0.0 copy-done.4
  22.2 7.2 %collective-permute-start = (bf16[8,256]{1,0:T(8,128)(2,1)S(1)}, bf16[8,256]{1,0:T(8,128)(2,1)S(1)}, u32[]{:S(2)}, u32[]{:S(2)}) collective-permute-start(bf16[8,256]{1,0:T(8,128)(2,1)S(1)} %bitcast.88), channel_id=1, source_target_pairs={{0,2},{2,4},{4,6},{6,0},{1,3},{3,5},{5,7},{7,1},{8,10},{10,12},{12... | collective-permute-start | bytes 12296 | tf_op jit(solution)/shard_map/ppermute | solution.py:35
  29.3 7.0 %collective-permute-start.1 = (bf16[8,256]{1,0:T(8,128)(2,1)S(1)}, bf16[8,256]{1,0:T(8,128)(2,1)S(1)}, u32[]{:S(2)}, u32[]{:S(2)}) collective-permute-start(bf16[8,256]{1,0:T(8,128)(2,1)S(1)} %bitcast.89), channel_id=1, source_target_pairs={{0,4},{2,6},{4,0},{6,2},{1,5},{3,7},{5,1},{7,3},{8,12},{10,14},{12... | collective-permute-start | bytes 12296 | tf_op jit(solution)/shard_map/ppermute | solution.py:35
  36.3 7.0 %collective-permute-start.2 = (bf16[8,256]{1,0:T(8,128)(2,1)S(1)}, bf16[8,256]{1,0:T(8,128)(2,1)S(1)}, u32[]{:S(2)}, u32[]{:S(2)}) collective-permute-start(bf16[8,256]{1,0:T(8,128)(2,1)S(1)} %bitcast.90), channel_id=1, source_target_pairs={{0,6},{2,0},{4,2},{6,4},{1,7},{3,1},{5,3},{7,5},{8,14},{10,8},{12,... | collective-permute-start | bytes 12296 | tf_op jit(solution)/shard_map/ppermute | solution.py:35
  43.4 0.0 copy-done.2
  43.4 1.1 copy_bitcast_fusion
  44.5 6.4 %collective-permute-done = bf16[8,256]{1,0:T(8,128)(2,1)S(1)} collective-permute-done((bf16[8,256]{1,0:T(8,128)(2,1)S(1)}, bf16[8,256]{1,0:T(8,128)(2,1)S(1)}, u32[]{:S(2)}, u32[]{:S(2)}) %collective-permute-start) | collective-permute-done | bytes 4128 | tf_op jit(solution)/shard_map/ppermute | solution.py:35
  50.9 9.0 %collective-permute-done.1 = bf16[8,256]{1,0:T(8,128)(2,1)S(1)} collective-permute-done((bf16[8,256]{1,0:T(8,128)(2,1)S(1)}, bf16[8,256]{1,0:T(8,128)(2,1)S(1)}, u32[]{:S(2)}, u32[]{:S(2)}) %collective-permute-start.1) | collective-permute-done | bytes 4128 | tf_op jit(solution)/shard_map/ppermute | solution.py:35
  59.9 12.5 %collective-permute-done.2 = bf16[8,256]{1,0:T(8,128)(2,1)S(1)} collective-permute-done((bf16[8,256]{1,0:T(8,128)(2,1)S(1)}, bf16[8,256]{1,0:T(8,128)(2,1)S(1)}, u32[]{:S(2)}, u32[]{:S(2)}) %collective-permute-start.2) | collective-permute-done | bytes 4128 | tf_op jit(solution)/shard_map/ppermute | solution.py:35
  72.3 1.6 all-to-all-done
  73.9 9.1 %all-to-all-start.1 = ((bf16[32,8,8,256]{3,2,1,0:T(8,128)(2,1)}), bf16[32,8,8,256]{3,2,1,0:T(8,128)(2,1)S(1)}, u32[]{:S(2)}, u32[]{:S(2)}) async-start(bf16[32,8,8,256]{3,2,1,0:T(8,128)(2,1)} %copy_bitcast_fusion), calls=%async_computation.1 | async-start | bytes 2097152 | tf_op jit(solution)/shard_map/all_to_all | solution.py:20
  83.0 0.0 copy-done.3
  83.0 0.0 copy-start.5
  83.1 0.7 copy-done.5
  83.7 0.1 copy.23.picks
  83.8 0.5 copy.22
  84.3 1.3 copy_bitcast_fusion.2.tensor
  85.6 0.0 copy-start.1
  85.7 0.6 copy-done.1
  86.3 6.1 %local_columns.1 = bf16[8,256,256]{2,1,0:T(8,128)(2,1)S(1)} custom-call(s32[4,2]{1,0:T(4,128)S(1)} %copy.23.picks, f32[4]{0:T(128)S(1)} %bitcast.81, bf16[8,256,256]{2,1,0:T(8,128)(2,1)S(1)} %copy_bitcast_fusion.2.tensor, bf16[8,256,256]{2,1,0:T(8,128)(2,1)S(1)} %copy-done, bf16[8,256,256]{2,1,0:T(8,128)(2,1)S(1)} %bitcast.80), custom_call_target="tpu_custom_call" | custom-call | flops 2147483648 | bytes 4194304 | tf_op jit(solution)/shard_map/local_columns/pallas_call | solution.py:59
  92.4 1.1 copy_bitcast_fusion.1
  93.5 19.3 %all-to-all-done.1 = bf16[32,8,8,256]{3,2,1,0:T(8,128)(2,1)S(1)} async-done(((bf16[32,8,8,256]{3,2,1,0:T(8,128)(2,1)}), bf16[32,8,8,256]{3,2,1,0:T(8,128)(2,1)S(1)}, u32[]{:S(2)}, u32[]{:S(2)}) %all-to-all-start.1) | async-done | bytes 1048608 | tf_op jit(solution)/shard_map/all_to_all | solution.py:20
  112.8 31.0 %all-to-all-start.2 = ((bf16[32,8,8,256]{3,2,1,0:T(8,128)(2,1)}), bf16[32,8,8,256]{3,2,1,0:T(8,128)(2,1)S(1)}, u32[]{:S(2)}, u32[]{:S(2)}) async-start(bf16[32,8,8,256]{3,2,1,0:T(8,128)(2,1)} %copy_bitcast_fusion.1), calls=%async_computation.2 | async-start | bytes 2097152 | tf_op jit(solution)/shard_map/all_to_all | solution.py:20
  143.9 2.1 collective-permute-start.3
  146.1 0.9 collective-permute-done.3
  147.0 3.3 %collective-permute-start.4 = (bf16[2,4,8,256]{3,2,0,1:T(8,128)(2,1)S(1)}, bf16[2,4,8,256]{3,2,0,1:T(8,128)(2,1)S(1)}, u32[]{:S(2)}, u32[]{:S(2)}) collective-permute-start(bf16[2,4,8,256]{3,2,0,1:T(8,128)(2,1)S(1)} %bitcast_dynamic-update-slice_fusion.5), channel_id=1, source_target_pairs={{0,8},{8,16},{16,24},{24,0},{1,9},{9,17},{17,25},{25,1},{2,10},{10... | collective-permute-start | bytes 98312 | tf_op jit(solution)/shard_map/ppermute | solution.py:35
  150.3 4.3 %collective-permute-start.5 = (bf16[2,4,8,256]{3,2,0,1:T(8,128)(2,1)S(1)}, bf16[2,4,8,256]{3,2,0,1:T(8,128)(2,1)S(1)}, u32[]{:S(2)}, u32[]{:S(2)}) collective-permute-start(bf16[2,4,8,256]{3,2,0,1:T(8,128)(2,1)S(1)} %bitcast_dynamic-update-slice_fusion.5), channel_id=1, source_target_pairs={{0,16},{8,24},{16,0},{24,8},{1,17},{9,25},{17,1},{25,9},{2,18},{10... | collective-permute-start | bytes 98312 | tf_op jit(solution)/shard_map/ppermute | solution.py:35
  154.6 3.1 %collective-permute-start.6 = (bf16[2,4,8,256]{3,2,0,1:T(8,128)(2,1)S(1)}, bf16[2,4,8,256]{3,2,0,1:T(8,128)(2,1)S(1)}, u32[]{:S(2)}, u32[]{:S(2)}) collective-permute-start(bf16[2,4,8,256]{3,2,0,1:T(8,128)(2,1)S(1)} %bitcast_dynamic-update-slice_fusion.5), channel_id=1, source_target_pairs={{0,24},{8,0},{16,8},{24,16},{1,25},{9,1},{17,9},{25,17},{2,26},{10... | collective-permute-start | bytes 98312 | tf_op jit(solution)/shard_map/ppermute | solution.py:35
  157.7 0.0 collective-permute-done.4
  157.7 0.0 collective-permute-done.5
  157.8 1.8 collective-permute-done.6
  159.6 14.7 %all-to-all-done.2 = bf16[32,8,8,256]{3,2,1,0:T(8,128)(2,1)S(1)} async-done(((bf16[32,8,8,256]{3,2,1,0:T(8,128)(2,1)}), bf16[32,8,8,256]{3,2,1,0:T(8,128)(2,1)S(1)}, u32[]{:S(2)}, u32[]{:S(2)}) %all-to-all-start.2) | async-done | bytes 1048608 | tf_op jit(solution)/shard_map/all_to_all | solution.py:20
  174.3 1.3 copy.27
  175.5 0.5 convolution_multiply_fusion.1
  176.0 0.3 fusion.6
  176.3 0.3 fusion.1
  176.6 14.5 %all_to_all.30 = bf16[32,8,256]{2,1,0:T(8,128)(2,1)S(1)} all-to-all(bf16[32,8,256]{2,1,0:T(8,128)(2,1)S(1)} %fusion.1), channel_id=1, replica_groups=mesh['x'=4,'zl'=4,'y'=4,'zh'=4,'c'=2] {'x','y','c'}, dimensions={0} | all-to-all | bytes 262144 | tf_op jit(solution)/shard_map/all_to_all | solution.py:20
  191.1 0.7 broadcast_in_dim.61
  191.9 28.0 %all-to-all-start.4 = ((bf16[16,4,8,256]{3,2,1,0:T(8,128)(2,1)}), bf16[16,4,8,256]{3,2,1,0:T(8,128)(2,1)S(1)}, u32[]{:S(2)}, u32[]{:S(2)}) async-start(bf16[16,4,8,256]{3,2,1,0:T(8,128)(2,1)} %broadcast_in_dim.61), calls=%async_computation.4 | async-start | bytes 524288 | tf_op jit(solution)/shard_map/all_to_all | solution.py:20
  219.9 15.8 %all-to-all-done.4 = bf16[16,4,8,256]{3,2,1,0:T(8,128)(2,1)S(1)} async-done(((bf16[16,4,8,256]{3,2,1,0:T(8,128)(2,1)}), bf16[16,4,8,256]{3,2,1,0:T(8,128)(2,1)S(1)}, u32[]{:S(2)}, u32[]{:S(2)}) %all-to-all-start.4) | async-done | bytes 262176 | tf_op jit(solution)/shard_map/all_to_all | solution.py:20
  235.7 0.1 convert_reduce_fusion
  235.8 0.7 dynamic-slice_add_fusion
  236.6 13.2 %all_to_all.31 = bf16[32,8,256]{2,1,0:T(8,128)(2,1)S(1)} all-to-all(bf16[32,8,256]{2,1,0:T(8,128)(2,1)S(1)} %bitcast.87), channel_id=1, replica_groups=mesh['x'=4,'zl'=4,'y'=4,'zh'=4,'c'=2] {'x','y','c'}, dimensions={0} | all-to-all | bytes 262144 | tf_op jit(solution)/shard_map/all_to_all | solution.py:20
  249.8 0.2 fusion.2
  250.0 0.3 fusion.hole
  250.4 2.5 result_rows.1
  (22 shorter events, 0.2 us)
Async XLA Ops:
  2.6 19.5 %copy-start.4 = (bf16[1,8,256]{2,1,0:T(8,128)(2,1)S(1)}, bf16[1,8,256]{2,1,0:T(8,128)(2,1)}, u32[]{:S(2)}) copy-start(bf16[1,8,256]{2,1,0:T(8,128)(2,1)} %param.10) | copy-start | bytes 12292
  2.6 40.7 %copy-start.2 = (bf16[1,8,256,256]{3,2,1,0:T(8,128)(2,1)S(1)}, bf16[1,8,256,256]{3,2,1,0:T(8,128)(2,1)}, u32[]{:S(2)}) copy-start(bf16[1,8,256,256]{3,2,1,0:T(8,128)(2,1)} %param.6) | copy-start | bytes 3145732
  2.6 71.3 %all-to-all-start = ((bf16[32,8,8,256]{3,2,1,0:T(8,128)(2,1)}), bf16[32,8,8,256]{3,2,1,0:T(8,128)(2,1)S(1)}, u32[]{:S(2)}, u32[]{:S(2)}) async-start(bf16[32,8,8,256]{3,2,1,0:T(8,128)(2,1)} %bitcast.4), calls=%async_computation | async-start | bytes 2097152 | tf_op jit(solution)/shard_map/all_to_all | solution.py:20
  22.2 28.7 %collective-permute-start = (bf16[8,256]{1,0:T(8,128)(2,1)S(1)}, bf16[8,256]{1,0:T(8,128)(2,1)S(1)}, u32[]{:S(2)}, u32[]{:S(2)}) collective-permute-start(bf16[8,256]{1,0:T(8,128)(2,1)S(1)} %bitcast.88), channel_id=1, source_target_pairs={{0,2},{2,4},{4,6},{6,0},{1,3},{3,5},{5,7},{7,1},{8,10},{10,12},{12... | collective-permute-start | bytes 12296 | tf_op jit(solution)/shard_map/ppermute | solution.py:35
  29.3 30.5 %collective-permute-start.1 = (bf16[8,256]{1,0:T(8,128)(2,1)S(1)}, bf16[8,256]{1,0:T(8,128)(2,1)S(1)}, u32[]{:S(2)}, u32[]{:S(2)}) collective-permute-start(bf16[8,256]{1,0:T(8,128)(2,1)S(1)} %bitcast.89), channel_id=1, source_target_pairs={{0,4},{2,6},{4,0},{6,2},{1,5},{3,7},{5,1},{7,3},{8,12},{10,14},{12... | collective-permute-start | bytes 12296 | tf_op jit(solution)/shard_map/ppermute | solution.py:35
  36.3 36.0 %collective-permute-start.2 = (bf16[8,256]{1,0:T(8,128)(2,1)S(1)}, bf16[8,256]{1,0:T(8,128)(2,1)S(1)}, u32[]{:S(2)}, u32[]{:S(2)}) collective-permute-start(bf16[8,256]{1,0:T(8,128)(2,1)S(1)} %bitcast.90), channel_id=1, source_target_pairs={{0,6},{2,0},{4,2},{6,4},{1,7},{3,1},{5,3},{7,5},{8,14},{10,8},{12,... | collective-permute-start | bytes 12296 | tf_op jit(solution)/shard_map/ppermute | solution.py:35
  72.3 11.5 %copy-start = (bf16[8,256,256]{2,1,0:T(8,128)(2,1)S(1)}, bf16[8,256,256]{2,1,0:T(8,128)(2,1)}, u32[]{:S(2)}) copy-start(bf16[8,256,256]{2,1,0:T(8,128)(2,1)} %bank.1) | copy-start | bytes 3145732
  73.9 9.1 %copy-start.3 = (bf16[32,8,8,256]{3,2,1,0:T(8,128)(2,1)}, bf16[32,8,8,256]{3,2,1,0:T(8,128)(2,1)S(1)}, u32[]{:S(2)}) copy-start(bf16[32,8,8,256]{3,2,1,0:T(8,128)(2,1)S(1)} %all-to-all-done) | copy-start | bytes 3145732
  73.9 38.9 %all-to-all-start.1 = ((bf16[32,8,8,256]{3,2,1,0:T(8,128)(2,1)}), bf16[32,8,8,256]{3,2,1,0:T(8,128)(2,1)S(1)}, u32[]{:S(2)}, u32[]{:S(2)}) async-start(bf16[32,8,8,256]{3,2,1,0:T(8,128)(2,1)} %copy_bitcast_fusion), calls=%async_computation.1 | async-start | bytes 2097152 | tf_op jit(solution)/shard_map/all_to_all | solution.py:20
  83.0 0.7 copy-start.5
  85.6 0.7 copy-start.1
  112.8 61.5 %all-to-all-start.2 = ((bf16[32,8,8,256]{3,2,1,0:T(8,128)(2,1)}), bf16[32,8,8,256]{3,2,1,0:T(8,128)(2,1)S(1)}, u32[]{:S(2)}, u32[]{:S(2)}) async-start(bf16[32,8,8,256]{3,2,1,0:T(8,128)(2,1)} %copy_bitcast_fusion.1), calls=%async_computation.2 | async-start | bytes 2097152 | tf_op jit(solution)/shard_map/all_to_all | solution.py:20
  143.9 3.1 %collective-permute-start.3 = (bf16[4,8,256]{2,1,0:T(8,128)(2,1)S(1)}, bf16[4,8,256]{2,1,0:T(8,128)(2,1)S(1)}, u32[]{:S(2)}, u32[]{:S(2)}) collective-permute-start(bf16[4,8,256]{2,1,0:T(8,128)(2,1)S(1)} %bitcast_dynamic-update-slice_fusion.6), channel_id=1, source_target_pairs={{0,1},{1,0},{2,3},{3,2},{4,5},{5,4},{6,7},{7,6},{8,9},{9,8},{10,11... | collective-permute-start | bytes 49160 | tf_op jit(solution)/shard_map/ppermute | solution.py:35
  147.0 10.8 %collective-permute-start.4 = (bf16[2,4,8,256]{3,2,0,1:T(8,128)(2,1)S(1)}, bf16[2,4,8,256]{3,2,0,1:T(8,128)(2,1)S(1)}, u32[]{:S(2)}, u32[]{:S(2)}) collective-permute-start(bf16[2,4,8,256]{3,2,0,1:T(8,128)(2,1)S(1)} %bitcast_dynamic-update-slice_fusion.5), channel_id=1, source_target_pairs={{0,8},{8,16},{16,24},{24,0},{1,9},{9,17},{17,25},{25,1},{2,10},{10... | collective-permute-start | bytes 98312 | tf_op jit(solution)/shard_map/ppermute | solution.py:35
  150.3 7.5 %collective-permute-start.5 = (bf16[2,4,8,256]{3,2,0,1:T(8,128)(2,1)S(1)}, bf16[2,4,8,256]{3,2,0,1:T(8,128)(2,1)S(1)}, u32[]{:S(2)}, u32[]{:S(2)}) collective-permute-start(bf16[2,4,8,256]{3,2,0,1:T(8,128)(2,1)S(1)} %bitcast_dynamic-update-slice_fusion.5), channel_id=1, source_target_pairs={{0,16},{8,24},{16,0},{24,8},{1,17},{9,25},{17,1},{25,9},{2,18},{10... | collective-permute-start | bytes 98312 | tf_op jit(solution)/shard_map/ppermute | solution.py:35
  154.6 5.0 %collective-permute-start.6 = (bf16[2,4,8,256]{3,2,0,1:T(8,128)(2,1)S(1)}, bf16[2,4,8,256]{3,2,0,1:T(8,128)(2,1)S(1)}, u32[]{:S(2)}, u32[]{:S(2)}) collective-permute-start(bf16[2,4,8,256]{3,2,0,1:T(8,128)(2,1)S(1)} %bitcast_dynamic-update-slice_fusion.5), channel_id=1, source_target_pairs={{0,24},{8,0},{16,8},{24,16},{1,25},{9,1},{17,9},{25,17},{2,26},{10... | collective-permute-start | bytes 98312 | tf_op jit(solution)/shard_map/ppermute | solution.py:35
  191.9 43.9 %all-to-all-start.4 = ((bf16[16,4,8,256]{3,2,1,0:T(8,128)(2,1)}), bf16[16,4,8,256]{3,2,1,0:T(8,128)(2,1)S(1)}, u32[]{:S(2)}, u32[]{:S(2)}) async-start(bf16[16,4,8,256]{3,2,1,0:T(8,128)(2,1)} %broadcast_in_dim.61), calls=%async_computation.4 | async-start | bytes 524288 | tf_op jit(solution)/shard_map/all_to_all | solution.py:20

commit v6 on v5

--- a/solution.py
+++ b/solution.py
@@ -109,15 +109,15 @@
     lift = gathered(parent[0], "zh", ZH)
 
     blocks = tensor.reshape(blk, devices, blk, bond).transpose(1, 0, 2, 3)
-    blocks, lift = lax.optimization_barrier((blocks, lift))
-    right = exchange(blocks, SHARD).reshape(bond * blk, bond)
 
     local = local_columns(columns, leg_ops, leg_ops.transpose(0, 2, 1), term_ops[0], term_coef[0])
     local = local.reshape(blk, devices, blk, bond).transpose(1, 0, 2, 3)
-    local, right, lift = lax.optimization_barrier((local, right, lift))
+    both, lift = lax.optimization_barrier((jnp.concatenate([blocks, local], axis=1), lift))
     lift = gathered(gathered(lift, "c", C), "y", Y)
     lift = lift.transpose(0, 2, 1, 3, 4).reshape(bond, bond).astype(F32)
-    local = exchange(local, SHARD).reshape(bond, blk, bond)
+    both = exchange(both, SHARD)
+    right = both[:, :blk].reshape(bond * blk, bond)
+    local = both[:, blk:].reshape(bond, blk, bond)
     local = local.transpose(2, 1, 0).reshape(bond * blk, bond)
 
     env = jnp.einsum("pu,pv->uv", right, local, preferred_element_type=F32) / bond

time: 255 us -> 249 us (0.976)
  starting transfers between devices: 122 us -> 115 us
  waiting for transfers between devices: 81.9 us -> 84.5 us
    all_to_all x4 -> x3, starting transfers between devices: 87.6 us -> 80.9 us  [exchange(): return lax.all_to_all(parts, axes, 0, 0, tiled=True)]
    all_to_all x4 -> x3, waiting for transfers between devices: 51.4 us -> 53.3 us  [exchange(): return lax.all_to_all(parts, axes, 0, 0, tiled=True)]
  transfers between devices with their start and end apart: 11 -> 10, of which waited for: 9 -> 8; matrix products, arithmetic and copies ran while one was open for 2% -> 0% of each run, Pallas kernels for 2% -> 0%
where the time goes in v6:
time: 249 us; the launch traced here: 247 us
  starting transfers between devices  115 us (46%)
  waiting for transfers between devices  84.5 us (34%)
  blocking collectives  26.9 us (11%)
  local copies, waits for them, and re-layouts  8.79 us (4%)
  Pallas kernels  8.64 us (3%)
    all_to_all x3, starting transfers between devices, exchange(): return lax.all_to_all(parts, axes, 0, 0, tiled=True)  80.9 us
    all_to_all x3, waiting for transfers between devices, exchange(): return lax.all_to_all(parts, axes, 0, 0, tiled=True)  53.3 us
    ppermute x7, starting transfers between devices, permuted(): return lax.ppermute(piece, axis, pairs)  34.1 us
    ppermute x7, waiting for transfers between devices, permuted(): return lax.ppermute(piece, axis, pairs)  31.2 us
    all_to_all x2, blocking collectives, exchange(): return lax.all_to_all(parts, axes, 0, 0, tiled=True)  26.9 us
    pallas_call x1, Pallas kernels, local_columns(): pl.pallas_call(local_kernel, out_shape=jax.ShapeDtypeStruct((blk, bond, b...  6.14 us
  transfers between devices with their start and end apart: 10, of which 8 were waited for; matrix products, arithmetic and copies ran while one was open for 0% of the time, Pallas kernels for 0%

profile of v6, /device:TPU:1, one launch (start us, length us, event | category | flops | bytes accessed | tf_op | source)
XLA Modules:
  0.0 246.9 jit_solution(396105601989223289)
XLA Ops:
  0.0 0.0 copy-start.3
  0.0 2.7 %copy.35 = bf16[1,8,256,256]{2,1,3,0:T(8,128)(2,1)} copy(bf16[1,8,256,256]{3,2,1,0:T(8,128)(2,1)} %param.6) | data formatting | bytes 2097152 | tf_op args[0]
  2.7 19.5 %all-to-all-start = ((bf16[32,8,8,256]{3,2,1,0:T(8,128)(2,1)}), bf16[32,8,8,256]{3,2,1,0:T(8,128)(2,1)S(1)}, u32[]{:S(2)}, u32[]{:S(2)}) async-start(bf16[32,8,8,256]{3,2,1,0:T(8,128)(2,1)} %bitcast.6), calls=%async_computation | async-start | bytes 2097152 | tf_op jit(solution)/shard_map/all_to_all | solution.py:20
  22.2 0.0 copy-done.3
  22.3 7.2 %collective-permute-start = (bf16[8,256]{1,0:T(8,128)(2,1)S(1)}, bf16[8,256]{1,0:T(8,128)(2,1)S(1)}, u32[]{:S(2)}, u32[]{:S(2)}) collective-permute-start(bf16[8,256]{1,0:T(8,128)(2,1)S(1)} %bitcast.86), channel_id=1, source_target_pairs={{0,2},{2,4},{4,6},{6,0},{1,3},{3,5},{5,7},{7,1},{8,10},{10,12},{12... | collective-permute-start | bytes 12296 | tf_op jit(solution)/shard_map/ppermute | solution.py:35
  29.4 7.0 %collective-permute-start.1 = (bf16[8,256]{1,0:T(8,128)(2,1)S(1)}, bf16[8,256]{1,0:T(8,128)(2,1)S(1)}, u32[]{:S(2)}, u32[]{:S(2)}) collective-permute-start(bf16[8,256]{1,0:T(8,128)(2,1)S(1)} %bitcast.87), channel_id=1, source_target_pairs={{0,4},{2,6},{4,0},{6,2},{1,5},{3,7},{5,1},{7,3},{8,12},{10,14},{12... | collective-permute-start | bytes 12296 | tf_op jit(solution)/shard_map/ppermute | solution.py:35
  36.4 7.0 %collective-permute-start.2 = (bf16[8,256]{1,0:T(8,128)(2,1)S(1)}, bf16[8,256]{1,0:T(8,128)(2,1)S(1)}, u32[]{:S(2)}, u32[]{:S(2)}) collective-permute-start(bf16[8,256]{1,0:T(8,128)(2,1)S(1)} %bitcast.88), channel_id=1, source_target_pairs={{0,6},{2,0},{4,2},{6,4},{1,7},{3,1},{5,3},{7,5},{8,14},{10,8},{12,... | collective-permute-start | bytes 12296 | tf_op jit(solution)/shard_map/ppermute | solution.py:35
  43.5 0.0 copy-done
  43.6 0.0 copy-start.1
  43.6 0.5 copy.37
  44.1 0.0 copy-done.4
  44.1 0.1 copy.38.picks
  44.2 6.7 %collective-permute-done = bf16[8,256]{1,0:T(8,128)(2,1)S(1)} collective-permute-done((bf16[8,256]{1,0:T(8,128)(2,1)S(1)}, bf16[8,256]{1,0:T(8,128)(2,1)S(1)}, u32[]{:S(2)}, u32[]{:S(2)}) %collective-permute-start) | collective-permute-done | bytes 4128 | tf_op jit(solution)/shard_map/ppermute | solution.py:35
  50.9 9.0 %collective-permute-done.1 = bf16[8,256]{1,0:T(8,128)(2,1)S(1)} collective-permute-done((bf16[8,256]{1,0:T(8,128)(2,1)S(1)}, bf16[8,256]{1,0:T(8,128)(2,1)S(1)}, u32[]{:S(2)}, u32[]{:S(2)}) %collective-permute-start.1) | collective-permute-done | bytes 4128 | tf_op jit(solution)/shard_map/ppermute | solution.py:35
  59.9 12.5 %collective-permute-done.2 = bf16[8,256]{1,0:T(8,128)(2,1)S(1)} collective-permute-done((bf16[8,256]{1,0:T(8,128)(2,1)S(1)}, bf16[8,256]{1,0:T(8,128)(2,1)S(1)}, u32[]{:S(2)}, u32[]{:S(2)}) %collective-permute-start.2) | collective-permute-done | bytes 4128 | tf_op jit(solution)/shard_map/ppermute | solution.py:35
  72.4 1.6 all-to-all-done
  74.0 0.1 copy_bitcast_fusion.tensor
  74.1 0.0 copy-done.1
  74.1 0.0 copy-start.2
  74.1 6.1 %local_columns.1 = bf16[8,256,256]{2,1,0:T(8,128)(2,1)S(1)} custom-call(s32[4,2]{1,0:T(4,128)S(1)} %copy.38.picks, f32[4]{0:T(128)S(1)} %bitcast.78, bf16[8,256,256]{2,1,0:T(8,128)(2,1)S(1)} %copy_bitcast_fusion.tensor, bf16[8,256,256]{2,1,0:T(8,128)(2,1)S(1)} %copy-done, bf16[8,256,256]{2,1,0:T(8,128)(2,1)S(1)} %bitcast.76), custom_call_target="tpu_custom_call" | custom-call | flops 2147483648 | bytes 4194304 | tf_op jit(solution)/shard_map/local_columns/pallas_call | solution.py:59
  80.3 0.0 copy-done.2
  80.3 0.2 pad_maximum_fusion
  80.5 1.6 copy.39
  82.0 9.0 %all-to-all-start.1 = ((bf16[32,16,8,256]{3,2,1,0:T(8,128)(2,1)}), bf16[32,16,8,256]{3,2,1,0:T(8,128)(2,1)}, u32[]{:S(2)}, u32[]{:S(2)}) async-start(bf16[32,16,8,256]{3,2,1,0:T(8,128)(2,1)} %copy.39), calls=%async_computation.1 | async-start | bytes 4194304 | tf_op jit(solution)/shard_map/all_to_all | solution.py:20
  91.2 2.2 collective-permute-start.3
  93.4 0.8 collective-permute-done.3
  94.2 3.3 %collective-permute-start.4 = (bf16[2,4,8,256]{3,2,0,1:T(8,128)(2,1)S(1)}, bf16[2,4,8,256]{3,2,0,1:T(8,128)(2,1)S(1)}, u32[]{:S(2)}, u32[]{:S(2)}) collective-permute-start(bf16[2,4,8,256]{3,2,0,1:T(8,128)(2,1)S(1)} %bitcast_dynamic-update-slice_fusion.5), channel_id=1, source_target_pairs={{0,8},{8,16},{16,24},{24,0},{1,9},{9,17},{17,25},{25,1},{2,10},{10... | collective-permute-start | bytes 98312 | tf_op jit(solution)/shard_map/ppermute | solution.py:35
  97.5 4.3 %collective-permute-start.5 = (bf16[2,4,8,256]{3,2,0,1:T(8,128)(2,1)S(1)}, bf16[2,4,8,256]{3,2,0,1:T(8,128)(2,1)S(1)}, u32[]{:S(2)}, u32[]{:S(2)}) collective-permute-start(bf16[2,4,8,256]{3,2,0,1:T(8,128)(2,1)S(1)} %bitcast_dynamic-update-slice_fusion.5), channel_id=1, source_target_pairs={{0,16},{8,24},{16,0},{24,8},{1,17},{9,25},{17,1},{25,9},{2,18},{10... | collective-permute-start | bytes 98312 | tf_op jit(solution)/shard_map/ppermute | solution.py:35
  101.9 3.1 %collective-permute-start.6 = (bf16[2,4,8,256]{3,2,0,1:T(8,128)(2,1)S(1)}, bf16[2,4,8,256]{3,2,0,1:T(8,128)(2,1)S(1)}, u32[]{:S(2)}, u32[]{:S(2)}) collective-permute-start(bf16[2,4,8,256]{3,2,0,1:T(8,128)(2,1)S(1)} %bitcast_dynamic-update-slice_fusion.5), channel_id=1, source_target_pairs={{0,24},{8,0},{16,8},{24,16},{1,25},{9,1},{17,9},{25,17},{2,26},{10... | collective-permute-start | bytes 98312 | tf_op jit(solution)/shard_map/ppermute | solution.py:35
  105.0 0.0 collective-permute-done.4
  105.0 0.0 collective-permute-done.5
  105.0 2.2 collective-permute-done.6
  107.3 35.8 %all-to-all-done.1 = bf16[32,16,8,256]{3,2,1,0:T(8,128)(2,1)} async-done(((bf16[32,16,8,256]{3,2,1,0:T(8,128)(2,1)}), bf16[32,16,8,256]{3,2,1,0:T(8,128)(2,1)}, u32[]{:S(2)}, u32[]{:S(2)}) %all-to-all-start.1) | async-done | bytes 2097184 | tf_op jit(solution)/shard_map/all_to_all | solution.py:20
  143.1 1.7 fusion.6
  144.8 1.3 copy.41
  146.1 0.5 convolution_multiply_fusion.1
  146.5 0.3 fusion.7
  146.8 0.3 fusion.1
  147.1 13.6 %all_to_all.25 = bf16[32,8,256]{2,1,0:T(8,128)(2,1)S(1)} all-to-all(bf16[32,8,256]{2,1,0:T(8,128)(2,1)S(1)} %fusion.1), channel_id=1, replica_groups=mesh['x'=4,'zl'=4,'y'=4,'zh'=4,'c'=2] {'x','y','c'}, dimensions={0} | all-to-all | bytes 262144 | tf_op jit(solution)/shard_map/all_to_all | solution.py:20
  160.8 0.7 broadcast_in_dim.61
  161.5 52.4 %all-to-all-start.3 = ((bf16[16,4,8,256]{3,2,1,0:T(8,128)(2,1)}), bf16[16,4,8,256]{3,2,1,0:T(8,128)(2,1)S(1)}, u32[]{:S(2)}, u32[]{:S(2)}) async-start(bf16[16,4,8,256]{3,2,1,0:T(8,128)(2,1)} %broadcast_in_dim.61), calls=%async_computation.3 | async-start | bytes 524288 | tf_op jit(solution)/shard_map/all_to_all | solution.py:20
  214.0 15.8 %all-to-all-done.3 = bf16[16,4,8,256]{3,2,1,0:T(8,128)(2,1)S(1)} async-done(((bf16[16,4,8,256]{3,2,1,0:T(8,128)(2,1)}), bf16[16,4,8,256]{3,2,1,0:T(8,128)(2,1)S(1)}, u32[]{:S(2)}, u32[]{:S(2)}) %all-to-all-start.3) | async-done | bytes 262176 | tf_op jit(solution)/shard_map/all_to_all | solution.py:20
  229.8 0.1 convert_reduce_fusion
  229.9 0.7 dynamic-slice_add_fusion
  230.6 13.2 %all_to_all.26 = bf16[32,8,256]{2,1,0:T(8,128)(2,1)S(1)} all-to-all(bf16[32,8,256]{2,1,0:T(8,128)(2,1)S(1)} %bitcast.85), channel_id=1, replica_groups=mesh['x'=4,'zl'=4,'y'=4,'zh'=4,'c'=2] {'x','y','c'}, dimensions={0} | all-to-all | bytes 262144 | tf_op jit(solution)/shard_map/all_to_all | solution.py:20
  243.9 0.2 fusion.2
  244.1 0.3 fusion.hole
  244.4 2.5 %result_rows.1 = bf16[2048,256]{1,0:T(8,128)(2,1)} custom-call(bf16[2048,256]{1,0:T(8,128)(2,1)S(1)} %bitcast.75, bf16[256,256]{1,0:T(8,128)(2,1)S(1)} %fusion.hole, bf16[2048,256]{1,0:T(8,128)(2,1)S(1)} %bitcast.73), custom_call_target="tpu_custom_call" | custom-call | flops 268435456 | bytes 3145728 | tf_op jit(solution)/shard_map/result_rows/pallas_call | solution.py:87
  (19 shorter events, 0.2 us)
Async XLA Ops:
  0.0 22.2 %copy-start.3 = (bf16[1,8,256]{2,1,0:T(8,128)(2,1)S(1)}, bf16[1,8,256]{2,1,0:T(8,128)(2,1)}, u32[]{:S(2)}) copy-start(bf16[1,8,256]{2,1,0:T(8,128)(2,1)} %param.10) | copy-start | bytes 12292
  0.0 43.5 %copy-start = (bf16[8,256,256]{2,1,0:T(8,128)(2,1)S(1)}, bf16[8,256,256]{2,1,0:T(8,128)(2,1)}, u32[]{:S(2)}) copy-start(bf16[8,256,256]{2,1,0:T(8,128)(2,1)} %bank.1) | copy-start | bytes 3145732
  2.7 41.4 %copy-start.4 = (s32[1,4,2]{1,2,0:T(2,128)S(1)}, s32[1,4,2]{1,2,0:T(2,128)}, u32[]{:S(2)}) copy-start(s32[1,4,2]{1,2,0:T(2,128)} %param.8) | copy-start | bytes 100
  2.7 71.3 %all-to-all-start = ((bf16[32,8,8,256]{3,2,1,0:T(8,128)(2,1)}), bf16[32,8,8,256]{3,2,1,0:T(8,128)(2,1)S(1)}, u32[]{:S(2)}, u32[]{:S(2)}) async-start(bf16[32,8,8,256]{3,2,1,0:T(8,128)(2,1)} %bitcast.6), calls=%async_computation | async-start | bytes 2097152 | tf_op jit(solution)/shard_map/all_to_all | solution.py:20
  22.3 28.7 %collective-permute-start = (bf16[8,256]{1,0:T(8,128)(2,1)S(1)}, bf16[8,256]{1,0:T(8,128)(2,1)S(1)}, u32[]{:S(2)}, u32[]{:S(2)}) collective-permute-start(bf16[8,256]{1,0:T(8,128)(2,1)S(1)} %bitcast.86), channel_id=1, source_target_pairs={{0,2},{2,4},{4,6},{6,0},{1,3},{3,5},{5,7},{7,1},{8,10},{10,12},{12... | collective-permute-start | bytes 12296 | tf_op jit(solution)/shard_map/ppermute | solution.py:35
  29.4 30.5 %collective-permute-start.1 = (bf16[8,256]{1,0:T(8,128)(2,1)S(1)}, bf16[8,256]{1,0:T(8,128)(2,1)S(1)}, u32[]{:S(2)}, u32[]{:S(2)}) collective-permute-start(bf16[8,256]{1,0:T(8,128)(2,1)S(1)} %bitcast.87), channel_id=1, source_target_pairs={{0,4},{2,6},{4,0},{6,2},{1,5},{3,7},{5,1},{7,3},{8,12},{10,14},{12... | collective-permute-start | bytes 12296 | tf_op jit(solution)/shard_map/ppermute | solution.py:35
  36.4 36.0 %collective-permute-start.2 = (bf16[8,256]{1,0:T(8,128)(2,1)S(1)}, bf16[8,256]{1,0:T(8,128)(2,1)S(1)}, u32[]{:S(2)}, u32[]{:S(2)}) collective-permute-start(bf16[8,256]{1,0:T(8,128)(2,1)S(1)} %bitcast.88), channel_id=1, source_target_pairs={{0,6},{2,0},{4,2},{6,4},{1,7},{3,1},{5,3},{7,5},{8,14},{10,8},{12,... | collective-permute-start | bytes 12296 | tf_op jit(solution)/shard_map/ppermute | solution.py:35
  43.6 30.5 %copy-start.1 = (f32[1,4]{1,0:T(1,128)S(1)}, f32[1,4]{1,0:T(1,128)}, u32[]{:S(2)}) copy-start(f32[1,4]{1,0:T(1,128)} %param.9) | copy-start | bytes 52
  74.1 6.2 %copy-start.2 = (bf16[1,8,256,256]{3,2,1,0:T(8,128)(2,1)S(1)}, bf16[1,8,256,256]{3,2,1,0:T(8,128)(2,1)}, u32[]{:S(2)}) copy-start(bf16[1,8,256,256]{3,2,1,0:T(8,128)(2,1)} %param.6) | copy-start | bytes 3145732
  82.0 61.1 %all-to-all-start.1 = ((bf16[32,16,8,256]{3,2,1,0:T(8,128)(2,1)}), bf16[32,16,8,256]{3,2,1,0:T(8,128)(2,1)}, u32[]{:S(2)}, u32[]{:S(2)}) async-start(bf16[32,16,8,256]{3,2,1,0:T(8,128)(2,1)} %copy.39), calls=%async_computation.1 | async-start | bytes 4194304 | tf_op jit(solution)/shard_map/all_to_all | solution.py:20
  91.2 3.1 %collective-permute-start.3 = (bf16[4,8,256]{2,1,0:T(8,128)(2,1)S(1)}, bf16[4,8,256]{2,1,0:T(8,128)(2,1)S(1)}, u32[]{:S(2)}, u32[]{:S(2)}) collective-permute-start(bf16[4,8,256]{2,1,0:T(8,128)(2,1)S(1)} %bitcast_dynamic-update-slice_fusion.6), channel_id=1, source_target_pairs={{0,1},{1,0},{2,3},{3,2},{4,5},{5,4},{6,7},{7,6},{8,9},{9,8},{10,11... | collective-permute-start | bytes 49160 | tf_op jit(solution)/shard_map/ppermute | solution.py:35
  94.2 10.8 %collective-permute-start.4 = (bf16[2,4,8,256]{3,2,0,1:T(8,128)(2,1)S(1)}, bf16[2,4,8,256]{3,2,0,1:T(8,128)(2,1)S(1)}, u32[]{:S(2)}, u32[]{:S(2)}) collective-permute-start(bf16[2,4,8,256]{3,2,0,1:T(8,128)(2,1)S(1)} %bitcast_dynamic-update-slice_fusion.5), channel_id=1, source_target_pairs={{0,8},{8,16},{16,24},{24,0},{1,9},{9,17},{17,25},{25,1},{2,10},{10... | collective-permute-start | bytes 98312 | tf_op jit(solution)/shard_map/ppermute | solution.py:35
  97.5 7.5 %collective-permute-start.5 = (bf16[2,4,8,256]{3,2,0,1:T(8,128)(2,1)S(1)}, bf16[2,4,8,256]{3,2,0,1:T(8,128)(2,1)S(1)}, u32[]{:S(2)}, u32[]{:S(2)}) collective-permute-start(bf16[2,4,8,256]{3,2,0,1:T(8,128)(2,1)S(1)} %bitcast_dynamic-update-slice_fusion.5), channel_id=1, source_target_pairs={{0,16},{8,24},{16,0},{24,8},{1,17},{9,25},{17,1},{25,9},{2,18},{10... | collective-permute-start | bytes 98312 | tf_op jit(solution)/shard_map/ppermute | solution.py:35
  101.9 5.4 %collective-permute-start.6 = (bf16[2,4,8,256]{3,2,0,1:T(8,128)(2,1)S(1)}, bf16[2,4,8,256]{3,2,0,1:T(8,128)(2,1)S(1)}, u32[]{:S(2)}, u32[]{:S(2)}) collective-permute-start(bf16[2,4,8,256]{3,2,0,1:T(8,128)(2,1)S(1)} %bitcast_dynamic-update-slice_fusion.5), channel_id=1, source_target_pairs={{0,24},{8,0},{16,8},{24,16},{1,25},{9,1},{17,9},{25,17},{2,26},{10... | collective-permute-start | bytes 98312 | tf_op jit(solution)/shard_map/ppermute | solution.py:35
  161.5 68.3 %all-to-all-start.3 = ((bf16[16,4,8,256]{3,2,1,0:T(8,128)(2,1)}), bf16[16,4,8,256]{3,2,1,0:T(8,128)(2,1)S(1)}, u32[]{:S(2)}, u32[]{:S(2)}) async-start(bf16[16,4,8,256]{3,2,1,0:T(8,128)(2,1)} %broadcast_in_dim.61), calls=%async_computation.3 | async-start | bytes 524288 | tf_op jit(solution)/shard_map/all_to_all | solution.py:20

commit v7 on v6

--- a/solution.py
+++ b/solution.py
@@ -35,9 +35,11 @@
     return lax.ppermute(piece, axis, pairs)
 
 
-def local_kernel(picks, coefs, tensor, bank, bank_t, out):
+def local_kernel(picks, coefs, tensor, blocks, bank, bank_t, out):
+    count, blk, _, bond = tensor.shape
+
     def column(u, carry):
-        block = tensor[u]
+        block = tensor[:, u].reshape(bond, bond)
         total = None
         for term in range(picks.shape[0]):
             left = bank[picks[term, 0]]
@@ -47,27 +49,28 @@
             ).astype(BF16)
             part = coefs[term] * jnp.dot(image, left, preferred_element_type=F32)
             total = part if total is None else total + part
-        out[u] = total.astype(out.dtype)
+        out[:, blk + u] = total.astype(out.dtype).reshape(count, blk, bond)
+        out[:, u] = blocks[:, u]
         return carry
 
-    lax.fori_loop(0, tensor.shape[0], column, 0)
+    lax.fori_loop(0, blk, column, 0, unroll=2)
 
 
-def local_columns(tensor, bank, bank_t, picks, coefs):
-    blk, bond, _ = tensor.shape
+def local_columns(tensor, blocks, bank, bank_t, picks, coefs):
+    count, blk, _, bond = tensor.shape
     flops = 4 * blk * bond**3 * picks.shape[0]
     return pl.pallas_call(
         local_kernel,
-        out_shape=jax.ShapeDtypeStruct((blk, bond, bond), BF16),
+        out_shape=jax.ShapeDtypeStruct((count, 2 * blk, blk, bond), BF16),
         in_specs=[pl.BlockSpec(memory_space=pltpu.SMEM)] * 2
-        + [pl.BlockSpec(memory_space=pltpu.VMEM)] * 3,
+        + [pl.BlockSpec(memory_space=pltpu.VMEM)] * 4,
         out_specs=pl.BlockSpec(memory_space=pltpu.VMEM),
         cost_estimate=pl.CostEstimate(
-            flops=flops, bytes_accessed=8 * blk * bond * bond, transcendentals=0
+            flops=flops, bytes_accessed=12 * blk * bond * bond, transcendentals=0
         ),
         compiler_params=pltpu.CompilerParams(vmem_limit_bytes=16 * 2**20),
         name="local_columns",
-    )(picks, coefs, tensor, bank, bank_t)
+    )(picks, coefs, tensor, blocks, bank, bank_t)
 
 
 def result_kernel(right, hole, arrived, out):
@@ -104,15 +107,16 @@
     devices = Y * ZH * C
 
     turned = tensor.transpose(2, 0, 1).reshape(devices, blk, blk, bond)
-    columns = exchange(turned, SHARD).transpose(1, 0, 2, 3).reshape(blk, bond, bond)
+    columns = exchange(turned, SHARD)
 
     lift = gathered(parent[0], "zh", ZH)
 
     blocks = tensor.reshape(blk, devices, blk, bond).transpose(1, 0, 2, 3)
 
-    local = local_columns(columns, leg_ops, leg_ops.transpose(0, 2, 1), term_ops[0], term_coef[0])
-    local = local.reshape(blk, devices, blk, bond).transpose(1, 0, 2, 3)
-    both, lift = lax.optimization_barrier((jnp.concatenate([blocks, local], axis=1), lift))
+    both = local_columns(
+        columns, blocks, leg_ops, leg_ops.transpose(0, 2, 1), term_ops[0], term_coef[0]
+    )
+    both, lift = lax.optimization_barrier((both, lift))
     lift = gathered(gathered(lift, "c", C), "y", Y)
     lift = lift.transpose(0, 2, 1, 3, 4).reshape(bond, bond).astype(F32)
     both = exchange(both, SHARD)

time: 249 us -> 248 us (level)
    transpose x1 -> x2, local copies, waits for them, and re-layouts: 1.26 us -> 4 us  [the longest x1 2.65 us: shards(): turned = tensor.transpose(2, 0, 1).reshape(devices, blk, blk, bond)]
  transfers between devices with their start and end apart: 10 -> 10, of which waited for: 8 -> 8; matrix products, arithmetic and copies ran while one was open for 0% -> 1% of each run, Pallas kernels for 0% -> 0%
where the time goes in v7:
time: 248 us; the launch traced here: 246 us
  starting transfers between devices  115 us (46%)
  waiting for transfers between devices  82.4 us (33%)
  blocking collectives  26.9 us (11%)
  local copies, waits for them, and re-layouts  10.4 us (4%)
  Pallas kernels  8.31 us (3%)
    all_to_all x3, starting transfers between devices, exchange(): return lax.all_to_all(parts, axes, 0, 0, tiled=True)  80.9 us
    all_to_all x3, waiting for transfers between devices, exchange(): return lax.all_to_all(parts, axes, 0, 0, tiled=True)  53.3 us
    ppermute x7, starting transfers between devices, permuted(): return lax.ppermute(piece, axis, pairs)  34.1 us
    ppermute x7, waiting for transfers between devices, permuted(): return lax.ppermute(piece, axis, pairs)  29.1 us
    all_to_all x2, blocking collectives, exchange(): return lax.all_to_all(parts, axes, 0, 0, tiled=True)  26.9 us
    pallas_call x1, Pallas kernels, local_columns(): pl.pallas_call(local_kernel, out_shape=jax.ShapeDtypeStruct((count, 2 * b...  5.81 us
  transfers between devices with their start and end apart: 10, of which 8 were waited for; matrix products, arithmetic and copies ran while one was open for 1% of the time, Pallas kernels for 0%

profile of v7, /device:TPU:1, one launch (start us, length us, event | category | flops | bytes accessed | tf_op | source)
XLA Modules:
  0.0 245.9 jit_solution(17091897333881173139)
XLA Ops:
  0.0 0.0 copy-start.3
  0.0 2.6 %copy.17 = bf16[256,8,256]{2,1,0:T(8,128)(2,1)} copy(bf16[256,8,256]{0,2,1:T(8,128)(2,1)} %bitcast.71) | data formatting | bytes 2097152 | tf_op jit(solution)/shard_map/transpose | solution.py:109
  2.7 0.0 copy-start.4
  2.7 0.0 copy-start
  2.7 19.5 %all-to-all-start = ((bf16[32,8,8,256]{3,2,1,0:T(8,128)(2,1)}), bf16[32,8,8,256]{3,2,1,0:T(8,128)(2,1)S(1)}, u32[]{:S(2)}, u32[]{:S(2)}) async-start(bf16[32,8,8,256]{3,2,1,0:T(8,128)(2,1)} %bitcast.4), calls=%async_computation | async-start | bytes 2097152 | tf_op jit(solution)/shard_map/all_to_all | solution.py:20
  22.2 0.0 copy-done.3
  22.2 7.2 %collective-permute-start = (bf16[8,256]{1,0:T(8,128)(2,1)S(1)}, bf16[8,256]{1,0:T(8,128)(2,1)S(1)}, u32[]{:S(2)}, u32[]{:S(2)}) collective-permute-start(bf16[8,256]{1,0:T(8,128)(2,1)S(1)} %bitcast.78), channel_id=1, source_target_pairs={{0,2},{2,4},{4,6},{6,0},{1,3},{3,5},{5,7},{7,1},{8,10},{10,12},{12... | collective-permute-start | bytes 12296 | tf_op jit(solution)/shard_map/ppermute | solution.py:35
  29.4 7.0 %collective-permute-start.1 = (bf16[8,256]{1,0:T(8,128)(2,1)S(1)}, bf16[8,256]{1,0:T(8,128)(2,1)S(1)}, u32[]{:S(2)}, u32[]{:S(2)}) collective-permute-start(bf16[8,256]{1,0:T(8,128)(2,1)S(1)} %bitcast.79), channel_id=1, source_target_pairs={{0,4},{2,6},{4,0},{6,2},{1,5},{3,7},{5,1},{7,3},{8,12},{10,14},{12... | collective-permute-start | bytes 12296 | tf_op jit(solution)/shard_map/ppermute | solution.py:35
  36.4 7.0 %collective-permute-start.2 = (bf16[8,256]{1,0:T(8,128)(2,1)S(1)}, bf16[8,256]{1,0:T(8,128)(2,1)S(1)}, u32[]{:S(2)}, u32[]{:S(2)}) collective-permute-start(bf16[8,256]{1,0:T(8,128)(2,1)S(1)} %bitcast.80), channel_id=1, source_target_pairs={{0,6},{2,0},{4,2},{6,4},{1,7},{3,1},{5,3},{7,5},{8,14},{10,8},{12,... | collective-permute-start | bytes 12296 | tf_op jit(solution)/shard_map/ppermute | solution.py:35
  43.4 0.0 copy-start.2
  43.4 1.3 copy_bitcast_fusion.blocks
  44.8 0.0 copy-done.4
  44.8 0.1 copy.20.picks
  44.9 0.0 copy-done
  44.9 1.3 copy.19
  46.2 4.6 %collective-permute-done = bf16[8,256]{1,0:T(8,128)(2,1)S(1)} collective-permute-done((bf16[8,256]{1,0:T(8,128)(2,1)S(1)}, bf16[8,256]{1,0:T(8,128)(2,1)S(1)}, u32[]{:S(2)}, u32[]{:S(2)}) %collective-permute-start) | collective-permute-done | bytes 4128 | tf_op jit(solution)/shard_map/ppermute | solution.py:35
  50.9 9.0 %collective-permute-done.1 = bf16[8,256]{1,0:T(8,128)(2,1)S(1)} collective-permute-done((bf16[8,256]{1,0:T(8,128)(2,1)S(1)}, bf16[8,256]{1,0:T(8,128)(2,1)S(1)}, u32[]{:S(2)}, u32[]{:S(2)}) %collective-permute-start.1) | collective-permute-done | bytes 4128 | tf_op jit(solution)/shard_map/ppermute | solution.py:35
  59.9 12.5 %collective-permute-done.2 = bf16[8,256]{1,0:T(8,128)(2,1)S(1)} collective-permute-done((bf16[8,256]{1,0:T(8,128)(2,1)S(1)}, bf16[8,256]{1,0:T(8,128)(2,1)S(1)}, u32[]{:S(2)}, u32[]{:S(2)}) %collective-permute-start.2) | collective-permute-done | bytes 4128 | tf_op jit(solution)/shard_map/ppermute | solution.py:35
  72.3 1.6 all-to-all-done.tensor
  73.9 0.0 copy-done.2
  73.9 0.0 copy-start.1
  74.0 1.2 copy-done.1
  75.2 5.8 %local_columns.1 = bf16[32,16,8,256]{3,2,1,0:T(8,128)(2,1)} custom-call(s32[4,2]{1,0:T(4,128)S(1)} %copy.20.picks, f32[4]{0:T(128)S(1)} %bitcast.70, bf16[32,8,8,256]{3,2,1,0:T(8,128)(2,1)S(1)} %all-to-all-done.tensor, bf16[32,8,8,256]{3,2,1,0:T(8,128)(2,1)S(1)} %copy_bitcast_fusion.blocks, bf16[8,256,256]{2,1,0:T(8,128)(2,1)S(1)} %copy-done, ...), custom_call_target="tpu_custom_call" | custom-call | flops 2147483648 | bytes 6291456 | tf_op jit(solution)/shard_map/local_columns/pallas_call | solution.py:62
  81.0 9.0 %all-to-all-start.1 = ((bf16[32,16,8,256]{3,2,1,0:T(8,128)(2,1)}), bf16[32,16,8,256]{3,2,1,0:T(8,128)(2,1)}, u32[]{:S(2)}, u32[]{:S(2)}) async-start(bf16[32,16,8,256]{3,2,1,0:T(8,128)(2,1)} %local_columns.1), calls=%async_computation.1 | async-start | bytes 4194304 | tf_op jit(solution)/shard_map/all_to_all | solution.py:20
  90.1 2.2 collective-permute-start.3
  92.3 0.8 collective-permute-done.3
  93.2 3.3 %collective-permute-start.4 = (bf16[2,4,8,256]{3,2,0,1:T(8,128)(2,1)S(1)}, bf16[2,4,8,256]{3,2,0,1:T(8,128)(2,1)S(1)}, u32[]{:S(2)}, u32[]{:S(2)}) collective-permute-start(bf16[2,4,8,256]{3,2,0,1:T(8,128)(2,1)S(1)} %bitcast_dynamic-update-slice_fusion.5), channel_id=1, source_target_pairs={{0,8},{8,16},{16,24},{24,0},{1,9},{9,17},{17,25},{25,1},{2,10},{10... | collective-permute-start | bytes 98312 | tf_op jit(solution)/shard_map/ppermute | solution.py:35
  96.5 4.3 %collective-permute-start.5 = (bf16[2,4,8,256]{3,2,0,1:T(8,128)(2,1)S(1)}, bf16[2,4,8,256]{3,2,0,1:T(8,128)(2,1)S(1)}, u32[]{:S(2)}, u32[]{:S(2)}) collective-permute-start(bf16[2,4,8,256]{3,2,0,1:T(8,128)(2,1)S(1)} %bitcast_dynamic-update-slice_fusion.5), channel_id=1, source_target_pairs={{0,16},{8,24},{16,0},{24,8},{1,17},{9,25},{17,1},{25,9},{2,18},{10... | collective-permute-start | bytes 98312 | tf_op jit(solution)/shard_map/ppermute | solution.py:35
  100.8 3.1 %collective-permute-start.6 = (bf16[2,4,8,256]{3,2,0,1:T(8,128)(2,1)S(1)}, bf16[2,4,8,256]{3,2,0,1:T(8,128)(2,1)S(1)}, u32[]{:S(2)}, u32[]{:S(2)}) collective-permute-start(bf16[2,4,8,256]{3,2,0,1:T(8,128)(2,1)S(1)} %bitcast_dynamic-update-slice_fusion.5), channel_id=1, source_target_pairs={{0,24},{8,0},{16,8},{24,16},{1,25},{9,1},{17,9},{25,17},{2,26},{10... | collective-permute-start | bytes 98312 | tf_op jit(solution)/shard_map/ppermute | solution.py:35
  103.9 0.0 collective-permute-done.4
  104.0 0.0 collective-permute-done.5
  104.0 2.2 collective-permute-done.6
  106.2 35.8 %all-to-all-done.1 = bf16[32,16,8,256]{3,2,1,0:T(8,128)(2,1)} async-done(((bf16[32,16,8,256]{3,2,1,0:T(8,128)(2,1)}), bf16[32,16,8,256]{3,2,1,0:T(8,128)(2,1)}, u32[]{:S(2)}, u32[]{:S(2)}) %all-to-all-start.1) | async-done | bytes 2097184 | tf_op jit(solution)/shard_map/all_to_all | solution.py:20
  142.0 1.7 fusion.6
  143.7 1.3 copy.22
  145.0 0.5 convolution_multiply_fusion.1
  145.5 0.3 fusion.7
  145.8 0.3 fusion.1
  146.1 13.6 %all_to_all.25 = bf16[32,8,256]{2,1,0:T(8,128)(2,1)S(1)} all-to-all(bf16[32,8,256]{2,1,0:T(8,128)(2,1)S(1)} %fusion.1), channel_id=1, replica_groups=mesh['x'=4,'zl'=4,'y'=4,'zh'=4,'c'=2] {'x','y','c'}, dimensions={0} | all-to-all | bytes 262144 | tf_op jit(solution)/shard_map/all_to_all | solution.py:20
  159.7 0.7 broadcast_in_dim.61
  160.5 52.4 %all-to-all-start.3 = ((bf16[16,4,8,256]{3,2,1,0:T(8,128)(2,1)}), bf16[16,4,8,256]{3,2,1,0:T(8,128)(2,1)S(1)}, u32[]{:S(2)}, u32[]{:S(2)}) async-start(bf16[16,4,8,256]{3,2,1,0:T(8,128)(2,1)} %broadcast_in_dim.61), calls=%async_computation.3 | async-start | bytes 524288 | tf_op jit(solution)/shard_map/all_to_all | solution.py:20
  212.9 15.8 %all-to-all-done.3 = bf16[16,4,8,256]{3,2,1,0:T(8,128)(2,1)S(1)} async-done(((bf16[16,4,8,256]{3,2,1,0:T(8,128)(2,1)}), bf16[16,4,8,256]{3,2,1,0:T(8,128)(2,1)S(1)}, u32[]{:S(2)}, u32[]{:S(2)}) %all-to-all-start.3) | async-done | bytes 262176 | tf_op jit(solution)/shard_map/all_to_all | solution.py:20
  228.7 0.1 convert_reduce_fusion
  228.8 0.7 dynamic-slice_add_fusion
  229.6 13.2 %all_to_all.26 = bf16[32,8,256]{2,1,0:T(8,128)(2,1)S(1)} all-to-all(bf16[32,8,256]{2,1,0:T(8,128)(2,1)S(1)} %bitcast.77), channel_id=1, replica_groups=mesh['x'=4,'zl'=4,'y'=4,'zh'=4,'c'=2] {'x','y','c'}, dimensions={0} | all-to-all | bytes 262144 | tf_op jit(solution)/shard_map/all_to_all | solution.py:20
  242.8 0.2 fusion.2
  243.0 0.3 fusion.hole
  243.4 2.5 %result_rows.1 = bf16[2048,256]{1,0:T(8,128)(2,1)} custom-call(bf16[2048,256]{1,0:T(8,128)(2,1)S(1)} %bitcast.68, bf16[256,256]{1,0:T(8,128)(2,1)S(1)} %fusion.hole, bf16[2048,256]{1,0:T(8,128)(2,1)S(1)} %bitcast.66), custom_call_target="tpu_custom_call" | custom-call | flops 268435456 | bytes 3145728 | tf_op jit(solution)/shard_map/result_rows/pallas_call | solution.py:90
  (17 shorter events, 0.2 us)
Async XLA Ops:
  0.0 22.2 %copy-start.3 = (bf16[1,8,256]{2,1,0:T(8,128)(2,1)S(1)}, bf16[1,8,256]{2,1,0:T(8,128)(2,1)}, u32[]{:S(2)}) copy-start(bf16[1,8,256]{2,1,0:T(8,128)(2,1)} %param.10) | copy-start | bytes 12292
  2.7 42.2 %copy-start.4 = (s32[1,4,2]{1,2,0:T(2,128)S(1)}, s32[1,4,2]{1,2,0:T(2,128)}, u32[]{:S(2)}) copy-start(s32[1,4,2]{1,2,0:T(2,128)} %param.8) | copy-start | bytes 100
  2.7 42.3 %copy-start = (bf16[8,256,256]{2,1,0:T(8,128)(2,1)S(1)}, bf16[8,256,256]{2,1,0:T(8,128)(2,1)}, u32[]{:S(2)}) copy-start(bf16[8,256,256]{2,1,0:T(8,128)(2,1)} %bank.1) | copy-start | bytes 3145732
  2.7 71.3 %all-to-all-start = ((bf16[32,8,8,256]{3,2,1,0:T(8,128)(2,1)}), bf16[32,8,8,256]{3,2,1,0:T(8,128)(2,1)S(1)}, u32[]{:S(2)}, u32[]{:S(2)}) async-start(bf16[32,8,8,256]{3,2,1,0:T(8,128)(2,1)} %bitcast.4), calls=%async_computation | async-start | bytes 2097152 | tf_op jit(solution)/shard_map/all_to_all | solution.py:20
  22.2 28.7 %collective-permute-start = (bf16[8,256]{1,0:T(8,128)(2,1)S(1)}, bf16[8,256]{1,0:T(8,128)(2,1)S(1)}, u32[]{:S(2)}, u32[]{:S(2)}) collective-permute-start(bf16[8,256]{1,0:T(8,128)(2,1)S(1)} %bitcast.78), channel_id=1, source_target_pairs={{0,2},{2,4},{4,6},{6,0},{1,3},{3,5},{5,7},{7,1},{8,10},{10,12},{12... | collective-permute-start | bytes 12296 | tf_op jit(solution)/shard_map/ppermute | solution.py:35
  29.4 30.5 %collective-permute-start.1 = (bf16[8,256]{1,0:T(8,128)(2,1)S(1)}, bf16[8,256]{1,0:T(8,128)(2,1)S(1)}, u32[]{:S(2)}, u32[]{:S(2)}) collective-permute-start(bf16[8,256]{1,0:T(8,128)(2,1)S(1)} %bitcast.79), channel_id=1, source_target_pairs={{0,4},{2,6},{4,0},{6,2},{1,5},{3,7},{5,1},{7,3},{8,12},{10,14},{12... | collective-permute-start | bytes 12296 | tf_op jit(solution)/shard_map/ppermute | solution.py:35
  36.4 36.0 %collective-permute-start.2 = (bf16[8,256]{1,0:T(8,128)(2,1)S(1)}, bf16[8,256]{1,0:T(8,128)(2,1)S(1)}, u32[]{:S(2)}, u32[]{:S(2)}) collective-permute-start(bf16[8,256]{1,0:T(8,128)(2,1)S(1)} %bitcast.80), channel_id=1, source_target_pairs={{0,6},{2,0},{4,2},{6,4},{1,7},{3,1},{5,3},{7,5},{8,14},{10,8},{12,... | collective-permute-start | bytes 12296 | tf_op jit(solution)/shard_map/ppermute | solution.py:35
  43.4 30.6 %copy-start.2 = (f32[1,4]{1,0:T(1,128)S(1)}, f32[1,4]{1,0:T(1,128)}, u32[]{:S(2)}) copy-start(f32[1,4]{1,0:T(1,128)} %param.9) | copy-start | bytes 52
  73.9 1.2 copy-start.1
  81.0 61.1 %all-to-all-start.1 = ((bf16[32,16,8,256]{3,2,1,0:T(8,128)(2,1)}), bf16[32,16,8,256]{3,2,1,0:T(8,128)(2,1)}, u32[]{:S(2)}, u32[]{:S(2)}) async-start(bf16[32,16,8,256]{3,2,1,0:T(8,128)(2,1)} %local_columns.1), calls=%async_computation.1 | async-start | bytes 4194304 | tf_op jit(solution)/shard_map/all_to_all | solution.py:20
  90.1 3.1 %collective-permute-start.3 = (bf16[4,8,256]{2,1,0:T(8,128)(2,1)S(1)}, bf16[4,8,256]{2,1,0:T(8,128)(2,1)S(1)}, u32[]{:S(2)}, u32[]{:S(2)}) collective-permute-start(bf16[4,8,256]{2,1,0:T(8,128)(2,1)S(1)} %bitcast_dynamic-update-slice_fusion.6), channel_id=1, source_target_pairs={{0,1},{1,0},{2,3},{3,2},{4,5},{5,4},{6,7},{7,6},{8,9},{9,8},{10,11... | collective-permute-start | bytes 49160 | tf_op jit(solution)/shard_map/ppermute | solution.py:35
  93.2 10.8 %collective-permute-start.4 = (bf16[2,4,8,256]{3,2,0,1:T(8,128)(2,1)S(1)}, bf16[2,4,8,256]{3,2,0,1:T(8,128)(2,1)S(1)}, u32[]{:S(2)}, u32[]{:S(2)}) collective-permute-start(bf16[2,4,8,256]{3,2,0,1:T(8,128)(2,1)S(1)} %bitcast_dynamic-update-slice_fusion.5), channel_id=1, source_target_pairs={{0,8},{8,16},{16,24},{24,0},{1,9},{9,17},{17,25},{25,1},{2,10},{10... | collective-permute-start | bytes 98312 | tf_op jit(solution)/shard_map/ppermute | solution.py:35
  96.5 7.5 %collective-permute-start.5 = (bf16[2,4,8,256]{3,2,0,1:T(8,128)(2,1)S(1)}, bf16[2,4,8,256]{3,2,0,1:T(8,128)(2,1)S(1)}, u32[]{:S(2)}, u32[]{:S(2)}) collective-permute-start(bf16[2,4,8,256]{3,2,0,1:T(8,128)(2,1)S(1)} %bitcast_dynamic-update-slice_fusion.5), channel_id=1, source_target_pairs={{0,16},{8,24},{16,0},{24,8},{1,17},{9,25},{17,1},{25,9},{2,18},{10... | collective-permute-start | bytes 98312 | tf_op jit(solution)/shard_map/ppermute | solution.py:35
  100.8 5.4 %collective-permute-start.6 = (bf16[2,4,8,256]{3,2,0,1:T(8,128)(2,1)S(1)}, bf16[2,4,8,256]{3,2,0,1:T(8,128)(2,1)S(1)}, u32[]{:S(2)}, u32[]{:S(2)}) collective-permute-start(bf16[2,4,8,256]{3,2,0,1:T(8,128)(2,1)S(1)} %bitcast_dynamic-update-slice_fusion.5), channel_id=1, source_target_pairs={{0,24},{8,0},{16,8},{24,16},{1,25},{9,1},{17,9},{25,17},{2,26},{10... | collective-permute-start | bytes 98312 | tf_op jit(solution)/shard_map/ppermute | solution.py:35
  160.5 68.3 %all-to-all-start.3 = ((bf16[16,4,8,256]{3,2,1,0:T(8,128)(2,1)}), bf16[16,4,8,256]{3,2,1,0:T(8,128)(2,1)S(1)}, u32[]{:S(2)}, u32[]{:S(2)}) async-start(bf16[16,4,8,256]{3,2,1,0:T(8,128)(2,1)} %broadcast_in_dim.61), calls=%async_computation.3 | async-start | bytes 524288 | tf_op jit(solution)/shard_map/all_to_all | solution.py:20
